TPU v7x, 256 devices: a whole 4x4x8 slice. The times are simulated.
256 devices in a mesh: gx: 4 (over x), gy: 8 (over z_lo, y), gz: 8 (over z_hi, core).
Axes of the slice: x: 4, y: 4, z: 8 (z_hi: 4, z_lo: 2; z = z_hi * 2 + z_lo), core: 2. Of those that a mesh axis runs over, the one named last changes fastest.
Arguments:
- charges: float32 [128, 512, 1024], P('gx', 'gy', 'gz'), may hold values from -8 to 8
- kernel_taps: float32 [5, 3, 17], replicated, may hold values from 0.08 to 0.4
Outputs:
- potential: float32 [128, 512, 1024], P('gx', 'gy', 'gz')
All inputs are finite; a program needn't handle non-finite values.
Results may differ from a plain program's by a relative error of at most 0.00029.
Values sent between devices are 32-bit elements; how exact they have to be, the bound alone decides.
No kernel may reach another device: no remote copies, remote signals or barrier semaphores. Data moves between devices by JAX's collectives and lax.ppermute only.
A program may use at most 128 MiB of HBM per device.

v0:
```python
import jax
import jax.numpy as jnp
from jax import lax
from jax.sharding import PartitionSpec as P

LEVELS = 5


CUBIC = (-0.0625, 0.0, 0.5625, 1.0, 0.5625, 0.0, -0.0625)
PATTERNS = ("ij,jbc->ibc", "ij,ajc->aic", "ij,abj->abi")


def extended(block, sides, width):
    for axis, dim in sides:
        count = lax.axis_size(axis)
        forward = [(i, i + 1) for i in range(count - 1)]
        backward = [(target, source) for source, target in forward]
        low = lax.ppermute(
            lax.slice_in_dim(block, block.shape[dim] - width, None, axis=dim), axis, forward
        )
        high = lax.ppermute(lax.slice_in_dim(block, 0, width, axis=dim), axis, backward)
        block = jnp.concatenate([low, block, high], axis=dim)
    return block


def picks_matrix(weights, offsets):
    count = weights.shape[0]
    picks = (offsets[None, :, :] == jnp.arange(count, dtype=jnp.int32)[:, None, None]).astype(
        jnp.float32
    )
    return jnp.sum(weights[:, None, None] * picks, axis=0)


def apply_axis(matrix, values, axis):
    return jnp.einsum(PATTERNS[axis], matrix, values, precision=lax.Precision.HIGHEST)


def stencil_axis(padded, taps_row, axis):
    length = padded.shape[axis] - 16
    offsets = (
        jnp.arange(length + 16, dtype=jnp.int32)[None, :]
        - jnp.arange(length, dtype=jnp.int32)[:, None]
    )
    return apply_axis(picks_matrix(taps_row, offsets), padded, axis)


def stencil_padded(padded, taps_level):
    for axis in range(3):
        padded = stencil_axis(padded, taps_level[axis], axis)
    return padded


def restrict_padded(padded):
    cubic = jnp.array(CUBIC, jnp.float32)
    for axis in range(3):
        length = padded.shape[axis] - 6
        offsets = (
            jnp.arange(length + 6, dtype=jnp.int32)[None, :]
            - 2 * jnp.arange(length // 2, dtype=jnp.int32)[:, None]
        )
        padded = apply_axis(picks_matrix(cubic, offsets), padded, axis)
    return padded


def prolong_padded(padded):
    cubic = jnp.array(CUBIC, jnp.float32)
    for axis in range(3):
        length = padded.shape[axis] - 4
        offsets = (
            7
            + jnp.arange(2 * length, dtype=jnp.int32)[:, None]
            - 2 * jnp.arange(length + 4, dtype=jnp.int32)[None, :]
        )
        padded = apply_axis(picks_matrix(cubic, offsets), padded, axis)
    return padded


def per_device(charges, kernel_taps):
    top_level = 3
    direct_terms = []
    grid_now = charges
    for level in range(top_level):
        padded = extended(grid_now, (("gx", 0), ("gy", 1), ("gz", 2)), 8)
        direct_terms.append(stencil_padded(padded, kernel_taps[level]))
        grid_now = restrict_padded(padded[5:-5, 5:-5, 5:-5])
    block_x, block_y, block_z = grid_now.shape
    gathered = lax.all_gather(grid_now[None], ("gx", "gy", "gz"), axis=0, tiled=True)
    count_x, count_y, count_z = (lax.axis_size("gx"), lax.axis_size("gy"), lax.axis_size("gz"))
    whole_grid = gathered.reshape(count_x, count_y, count_z, block_x, block_y, block_z)
    whole_grid = whole_grid.transpose(0, 3, 1, 4, 2, 5).reshape(
        count_x * block_x, count_y * block_y, count_z * block_z
    )
    coarse_list = [whole_grid]
    coarse_list.append(restrict_padded(jnp.pad(coarse_list[-1], 3)))
    coarse_pot = stencil_padded(jnp.pad(coarse_list[-1], 8), kernel_taps[LEVELS - 1])
    level = 3
    coarse_pot = stencil_padded(
        jnp.pad(coarse_list[level - top_level], 8), kernel_taps[level]
    ) + prolong_padded(jnp.pad(coarse_pot, 2))
    padded_pot = jnp.pad(coarse_pot, 2)
    starts = (
        lax.axis_index("gx") * block_x,
        lax.axis_index("gy") * block_y,
        lax.axis_index("gz") * block_z,
    )
    rim_pot = lax.dynamic_slice(padded_pot, starts, (block_x + 4, block_y + 4, block_z + 4))
    current = rim_pot
    for level in range(top_level - 1, -1, -1):
        current = direct_terms[level] + prolong_padded(rim_pot)
        if level > 0:
            rim_pot = extended(current, (("gx", 0), ("gy", 1), ("gz", 2)), 2)
    return current


def solution(mesh):
    in_specs = (P("gx", "gy", "gz"), P())
    out_specs = P("gx", "gy", "gz")
    return jax.shard_map(
        per_device, mesh=mesh, in_specs=in_specs, out_specs=out_specs, check_vma=False
    )
```

profile of v0, /device:TPU:9, one launch (start us, length us, event | category | flops | bytes accessed | tf_op | source)
XLA Modules:
  0.0 594.8 jit_solution(3449505044220305900)
XLA Ops:
  21.1 3.6 fusion.123
  47.1 5.0 collective-permute-start.5
  52.1 5.0 collective-permute-start.4
  60.5 3.4 fusion.14
  72.2 3.7 collective-permute-done.7
  81.9 3.7 collective-permute-done.9
  92.3 7.7 %collective-permute-start.10 = (f32[32,48,8]{1,2,0:T(8,128)}, f32[32,48,8]{1,2,0:T(8,128)}, u32[]{:S(2)}, u32[]{:S(2)}) collective-permute-start(f32[32,48,8]{1,2,0:T(8,128)} %copy.101), channel_id=1, source_target_pairs={{0,1},{1,2},{2,3},{3,4},{4,5},{5,6},{6,7},{8,9},{9,10},{10,11},{11... | collective-permute-start | bytes 147464 | tf_op jit(solution)/shard_map/ppermute | solution.py:18
  110.5 4.0 collective-permute-start.12
  115.9 7.3 %collective-permute-start.14 = (f32[24,8,32]{2,1,0:T(8,128)S(1)}, f32[24,8,32]{2,1,0:T(8,128)S(1)}, u32[]{:S(2)}, u32[]{:S(2)}) collective-permute-start(f32[24,8,32]{2,1,0:T(8,128)S(1)} %get-tuple-element.40), channel_id=1, source_target_pairs={{0,8},{8,16},{16,24},{24,32},{32,40},{40,48},{48,56},{1,9},{9,17},... | collective-permute-start | bytes 73736 | tf_op jit(solution)/shard_map/ppermute | solution.py:18
  125.9 4.9 collective-permute-done.15
  131.8 7.7 %collective-permute-start.16 = (f32[24,32,8]{2,1,0:T(8,128)}, f32[24,32,8]{2,1,0:T(8,128)S(1)}, u32[]{:S(2)}, u32[]{:S(2)}) collective-permute-start(f32[24,32,8]{2,1,0:T(8,128)} %get-tuple-element.32), channel_id=1, source_target_pairs={{0,1},{1,2},{2,3},{3,4},{4,5},{5,6},{6,7},{8,9},{9,10},{10,11},{11... | collective-permute-start | bytes 73736 | tf_op jit(solution)/shard_map/ppermute | solution.py:18
  144.5 6.2 %collective-permute-done.17 = f32[24,32,8]{2,1,0:T(8,128)} collective-permute-done((f32[24,32,8]{2,1,0:T(8,128)}, f32[24,32,8]{2,1,0:T(8,128)}, u32[]{:S(2)}, u32[]{:S(2)}) %collective-permute-start.17) | collective-permute-done | bytes 24608 | tf_op jit(solution)/shard_map/ppermute | solution.py:21
  153.8 343.1 %all-gather = f32[1024,8,16]{2,1,0:T(8,128)S(1)} all-gather(f32[4,8,16]{2,1,0:T(8,128)S(1)} %fusion.105), channel_id=2, replica_groups=mesh['gx'=4,'gy'=8,'gz'=8] {'gx','gy','gz'}, dimensions={0}, use_global_device_ids=true | all-gather | bytes 526336 | tf_op jit(solution)/shard_map/all_gather | solution.py:87
  496.9 4.4 copy.180
  501.3 3.9 reshape.425
  528.2 9.5 %collective-permute-start.21 = (f32[12,2,32]{2,1,0:T(2,128)S(1)}, f32[12,2,32]{2,1,0:T(2,128)S(1)}, u32[]{:S(2)}, u32[]{:S(2)}) collective-permute-start(f32[12,2,32]{2,1,0:T(2,128)S(1)} %get-tuple-element.45), channel_id=1, source_target_pairs={{8,0},{16,8},{24,16},{32,24},{40,32},{48,40},{56,48},{9,1},{17,9},... | collective-permute-start | bytes 9224 | tf_op jit(solution)/shard_map/ppermute | solution.py:21
  538.6 4.7 collective-permute-start.22
  545.5 5.5 collective-permute-done.23
  556.3 3.3 collective-permute-done.25
  559.7 3.5 collective-permute-start.26
  565.2 3.7 fusion
  570.4 4.4 collective-permute-start.28
  576.7 6.0 %fusion.28 = f32[32,144,64]{1,2,0:T(8,128)S(1)} fusion(f32[32,80,144]{1,0,2:T(8,128)S(1)} %fusion, f32[64,80]{1,0:T(8,128)S(1)} %copy-done.21), kind=kOutput, calls=%fused_computation.30 | convolution fusion | flops 283115520 | bytes 2674688 | tf_op jit(solution)/shard_map/ij,ajc->aic/dot_general | solution.py:35
  582.7 5.8 collective-permute-done.29
  (269 shorter events, 133.0 us)
Async XLA Ops:
  3.2 14.4 %collective-permute-start = (f32[8,64,128]{1,0,2:T(8,128)S(1)}, f32[8,64,128]{1,0,2:T(8,128)S(1)}, u32[]{:S(2)}, u32[]{:S(2)}) collective-permute-start(f32[8,64,128]{1,0,2:T(8,128)S(1)} %get-tuple-element.24), channel_id=1, source_target_pairs={{0,64},{64,128},{128,192},{1,65},{65,129},{129,193},{2,66},{66,130... | collective-permute-start | bytes 786440 | tf_op jit(solution)/shard_map/ppermute | solution.py:18
  6.3 14.4 %collective-permute-start.1 = (f32[8,64,128]{1,0,2:T(8,128)S(1)}, f32[8,64,128]{1,0,2:T(8,128)S(1)}, u32[]{:S(2)}, u32[]{:S(2)}) collective-permute-start(f32[8,64,128]{1,0,2:T(8,128)S(1)} %get-tuple-element.25), channel_id=1, source_target_pairs={{64,0},{128,64},{192,128},{65,1},{129,65},{193,129},{66,2},{130,66... | collective-permute-start | bytes 786440 | tf_op jit(solution)/shard_map/ppermute | solution.py:21
  30.0 12.1 %collective-permute-start.3 = (f32[48,8,128]{2,1,0:T(8,128)S(1)}, f32[48,8,128]{2,1,0:T(8,128)}, u32[]{:S(2)}, u32[]{:S(2)}) collective-permute-start(f32[48,8,128]{2,1,0:T(8,128)S(1)} %copy.92), channel_id=1, source_target_pairs={{8,0},{16,8},{24,16},{32,24},{40,32},{48,40},{56,48},{9,1},{17,9},... | collective-permute-start | bytes 589832 | tf_op jit(solution)/shard_map/ppermute | solution.py:21
  32.1 7.0 %collective-permute-start.2 = (f32[48,8,128]{2,1,0:T(8,128)}, f32[48,8,128]{2,1,0:T(8,128)}, u32[]{:S(2)}, u32[]{:S(2)}) collective-permute-start(f32[48,8,128]{2,1,0:T(8,128)} %copy.91), channel_id=1, source_target_pairs={{0,8},{8,16},{16,24},{24,32},{32,40},{40,48},{48,56},{1,9},{9,17},... | collective-permute-start | bytes 589832 | tf_op jit(solution)/shard_map/ppermute | solution.py:18
  47.1 13.3 %collective-permute-start.5 = (f32[48,80,8]{1,2,0:T(8,128)S(1)}, f32[48,80,8]{1,2,0:T(8,128)S(1)}, u32[]{:S(2)}, u32[]{:S(2)}) collective-permute-start(f32[48,80,8]{1,2,0:T(8,128)S(1)} %copy.96), channel_id=1, source_target_pairs={{1,0},{2,1},{3,2},{4,3},{5,4},{6,5},{7,6},{9,8},{10,9},{11,10},{12... | collective-permute-start | bytes 368648 | tf_op jit(solution)/shard_map/ppermute | solution.py:21
  52.1 8.3 %collective-permute-start.4 = (f32[48,80,8]{1,2,0:T(8,128)S(1)}, f32[48,80,8]{1,2,0:T(8,128)S(1)}, u32[]{:S(2)}, u32[]{:S(2)}) collective-permute-start(f32[48,80,8]{1,2,0:T(8,128)S(1)} %copy.95), channel_id=1, source_target_pairs={{0,1},{1,2},{2,3},{3,4},{4,5},{5,6},{6,7},{8,9},{9,10},{10,11},{11... | collective-permute-start | bytes 368648 | tf_op jit(solution)/shard_map/ppermute | solution.py:18
  70.1 5.7 collective-permute-start.7
  75.9 6.0 %collective-permute-start.8 = (f32[32,8,64]{2,1,0:T(8,128)S(1)}, f32[32,8,64]{2,1,0:T(8,128)S(1)}, u32[]{:S(2)}, u32[]{:S(2)}) collective-permute-start(f32[32,8,64]{2,1,0:T(8,128)S(1)} %get-tuple-element.28), channel_id=1, source_target_pairs={{0,8},{8,16},{16,24},{24,32},{32,40},{40,48},{48,56},{1,9},{9,17},... | collective-permute-start | bytes 196616 | tf_op jit(solution)/shard_map/ppermute | solution.py:18
  79.1 6.5 %collective-permute-start.9 = (f32[32,8,64]{2,1,0:T(8,128)S(1)}, f32[32,8,64]{2,1,0:T(8,128)S(1)}, u32[]{:S(2)}, u32[]{:S(2)}) collective-permute-start(f32[32,8,64]{2,1,0:T(8,128)S(1)} %get-tuple-element.29), channel_id=1, source_target_pairs={{8,0},{16,8},{24,16},{32,24},{40,32},{48,40},{56,48},{9,1},{17,9},... | collective-permute-start | bytes 196616 | tf_op jit(solution)/shard_map/ppermute | solution.py:21
  90.4 13.0 %collective-permute-start.11 = (f32[32,48,8]{1,2,0:T(8,128)}, f32[32,48,8]{1,2,0:T(8,128)}, u32[]{:S(2)}, u32[]{:S(2)}) collective-permute-start(f32[32,48,8]{1,2,0:T(8,128)} %copy.102), channel_id=1, source_target_pairs={{1,0},{2,1},{3,2},{4,3},{5,4},{6,5},{7,6},{9,8},{10,9},{11,10},{12... | collective-permute-start | bytes 147464 | tf_op jit(solution)/shard_map/ppermute | solution.py:21
  92.3 9.9 %collective-permute-start.10 = (f32[32,48,8]{1,2,0:T(8,128)}, f32[32,48,8]{1,2,0:T(8,128)}, u32[]{:S(2)}, u32[]{:S(2)}) collective-permute-start(f32[32,48,8]{1,2,0:T(8,128)} %copy.101), channel_id=1, source_target_pairs={{0,1},{1,2},{2,3},{3,4},{4,5},{5,6},{6,7},{8,9},{9,10},{10,11},{11... | collective-permute-start | bytes 147464 | tf_op jit(solution)/shard_map/ppermute | solution.py:18
  109.2 6.0 %collective-permute-start.13 = (f32[8,16,32]{2,1,0:T(8,128)S(1)}, f32[8,16,32]{2,1,0:T(8,128)S(1)}, u32[]{:S(2)}, u32[]{:S(2)}) collective-permute-start(f32[8,16,32]{2,1,0:T(8,128)S(1)} %fusion.93), channel_id=1, source_target_pairs={{64,0},{128,64},{192,128},{65,1},{129,65},{193,129},{66,2},{130,66... | collective-permute-start | bytes 49160 | tf_op jit(solution)/shard_map/ppermute | solution.py:21
  115.9 9.9 %collective-permute-start.14 = (f32[24,8,32]{2,1,0:T(8,128)S(1)}, f32[24,8,32]{2,1,0:T(8,128)S(1)}, u32[]{:S(2)}, u32[]{:S(2)}) collective-permute-start(f32[24,8,32]{2,1,0:T(8,128)S(1)} %get-tuple-element.40), channel_id=1, source_target_pairs={{0,8},{8,16},{16,24},{24,32},{32,40},{40,48},{48,56},{1,9},{9,17},... | collective-permute-start | bytes 73736 | tf_op jit(solution)/shard_map/ppermute | solution.py:18
  123.3 7.5 %collective-permute-start.15 = (f32[24,8,32]{2,1,0:T(8,128)S(1)}, f32[24,8,32]{2,1,0:T(8,128)S(1)}, u32[]{:S(2)}, u32[]{:S(2)}) collective-permute-start(f32[24,8,32]{2,1,0:T(8,128)S(1)} %get-tuple-element.41), channel_id=1, source_target_pairs={{8,0},{16,8},{24,16},{32,24},{40,32},{48,40},{56,48},{9,1},{17,9},... | collective-permute-start | bytes 73736 | tf_op jit(solution)/shard_map/ppermute | solution.py:21
  131.8 12.7 %collective-permute-start.16 = (f32[24,32,8]{2,1,0:T(8,128)}, f32[24,32,8]{2,1,0:T(8,128)S(1)}, u32[]{:S(2)}, u32[]{:S(2)}) collective-permute-start(f32[24,32,8]{2,1,0:T(8,128)} %get-tuple-element.32), channel_id=1, source_target_pairs={{0,1},{1,2},{2,3},{3,4},{4,5},{5,6},{6,7},{8,9},{9,10},{10,11},{11... | collective-permute-start | bytes 73736 | tf_op jit(solution)/shard_map/ppermute | solution.py:18
  139.5 11.2 %collective-permute-start.17 = (f32[24,32,8]{2,1,0:T(8,128)}, f32[24,32,8]{2,1,0:T(8,128)}, u32[]{:S(2)}, u32[]{:S(2)}) collective-permute-start(f32[24,32,8]{2,1,0:T(8,128)} %get-tuple-element.33), channel_id=1, source_target_pairs={{1,0},{2,1},{3,2},{4,3},{5,4},{6,5},{7,6},{9,8},{10,9},{11,10},{12... | collective-permute-start | bytes 73736 | tf_op jit(solution)/shard_map/ppermute | solution.py:21
  526.3 12.0 %collective-permute-start.20 = (f32[12,2,32]{2,1,0:T(2,128)S(1)}, f32[12,2,32]{2,1,0:T(2,128)S(1)}, u32[]{:S(2)}, u32[]{:S(2)}) collective-permute-start(f32[12,2,32]{2,1,0:T(2,128)S(1)} %get-tuple-element.44), channel_id=1, source_target_pairs={{0,8},{8,16},{16,24},{24,32},{32,40},{40,48},{48,56},{1,9},{9,17},... | collective-permute-start | bytes 9224 | tf_op jit(solution)/shard_map/ppermute | solution.py:18
  528.2 10.2 %collective-permute-start.21 = (f32[12,2,32]{2,1,0:T(2,128)S(1)}, f32[12,2,32]{2,1,0:T(2,128)S(1)}, u32[]{:S(2)}, u32[]{:S(2)}) collective-permute-start(f32[12,2,32]{2,1,0:T(2,128)S(1)} %get-tuple-element.45), channel_id=1, source_target_pairs={{8,0},{16,8},{24,16},{32,24},{40,32},{48,40},{56,48},{9,1},{17,9},... | collective-permute-start | bytes 9224 | tf_op jit(solution)/shard_map/ppermute | solution.py:21
  538.6 7.0 %collective-permute-start.22 = (f32[12,20,2]{2,1,0:T(8,128)S(1)}, f32[12,20,2]{2,1,0:T(8,128)S(1)}, u32[]{:S(2)}, u32[]{:S(2)}) collective-permute-start(f32[12,20,2]{2,1,0:T(8,128)S(1)} %get-tuple-element.42), channel_id=1, source_target_pairs={{0,1},{1,2},{2,3},{3,4},{4,5},{5,6},{6,7},{8,9},{9,10},{10,11},{11... | collective-permute-start | bytes 5768 | tf_op jit(solution)/shard_map/ppermute | solution.py:18
  543.2 7.8 %collective-permute-start.23 = (f32[12,20,2]{2,1,0:T(8,128)S(1)}, f32[12,20,2]{2,1,0:T(8,128)S(1)}, u32[]{:S(2)}, u32[]{:S(2)}) collective-permute-start(f32[12,20,2]{2,1,0:T(8,128)S(1)} %get-tuple-element.43), channel_id=1, source_target_pairs={{1,0},{2,1},{3,2},{4,3},{5,4},{6,5},{7,6},{9,8},{10,9},{11,10},{12... | collective-permute-start | bytes 5768 | tf_op jit(solution)/shard_map/ppermute | solution.py:21
  559.7 9.3 %collective-permute-start.26 = (f32[20,2,64]{2,1,0:T(2,128)S(1)}, f32[20,2,64]{2,1,0:T(2,128)S(1)}, u32[]{:S(2)}, u32[]{:S(2)}) collective-permute-start(f32[20,2,64]{2,1,0:T(2,128)S(1)} %get-tuple-element.34), channel_id=1, source_target_pairs={{0,8},{8,16},{16,24},{24,32},{32,40},{40,48},{48,56},{1,9},{9,17},... | collective-permute-start | bytes 30728 | tf_op jit(solution)/shard_map/ppermute | solution.py:18
  563.2 6.9 %collective-permute-start.27 = (f32[20,2,64]{2,1,0:T(2,128)S(1)}, f32[20,2,64]{2,1,0:T(2,128)S(1)}, u32[]{:S(2)}, u32[]{:S(2)}) collective-permute-start(f32[20,2,64]{2,1,0:T(2,128)S(1)} %get-tuple-element.35), channel_id=1, source_target_pairs={{8,0},{16,8},{24,16},{32,24},{40,32},{48,40},{56,48},{9,1},{17,9},... | collective-permute-start | bytes 30728 | tf_op jit(solution)/shard_map/ppermute | solution.py:21
  570.4 12.3 %collective-permute-start.28 = (f32[20,36,2]{2,1,0:T(8,128)S(1)}, f32[20,36,2]{2,1,0:T(8,128)S(1)}, u32[]{:S(2)}, u32[]{:S(2)}) collective-permute-start(f32[20,36,2]{2,1,0:T(8,128)S(1)} %get-tuple-element.30), channel_id=1, source_target_pairs={{0,1},{1,2},{2,3},{3,4},{4,5},{5,6},{6,7},{8,9},{9,10},{10,11},{11... | collective-permute-start | bytes 17288 | tf_op jit(solution)/shard_map/ppermute | solution.py:18
  574.7 13.8 %collective-permute-start.29 = (f32[20,36,2]{2,1,0:T(8,128)S(1)}, f32[20,36,2]{2,1,0:T(8,128)S(1)}, u32[]{:S(2)}, u32[]{:S(2)}) collective-permute-start(f32[20,36,2]{2,1,0:T(8,128)S(1)} %get-tuple-element.31), channel_id=1, source_target_pairs={{1,0},{2,1},{3,2},{4,3},{5,4},{6,5},{7,6},{9,8},{10,9},{11,10},{12... | collective-permute-start | bytes 17288 | tf_op jit(solution)/shard_map/ppermute | solution.py:21
  (58 other events, 814.2 us)
where the time goes:
time: 601 us; the launch traced here: 595 us
  blocking collectives  343 us (57%)
  starting transfers between devices  99.5 us (17%)
  waiting for transfers between devices  50.6 us (8%)
  local copies, waits for them, and re-layouts  40 us (7%)
  matrix products  40 us (7%)
  other arithmetic  19.9 us (3%)
    all_gather x1, blocking collectives, per_device(): lax.all_gather(grid_now[None], ('gx', 'gy', 'gz'), axis=0, tiled=True)  343 us
    ppermute x15, starting transfers between devices, extended(): lax.ppermute(lax.slice_in_dim(block, block.shape[dim] - width, None, axis...  62.9 us
    ppermute x15, waiting for transfers between devices, extended(): lax.ppermute(lax.slice_in_dim(block, 0, width, axis=dim), axis, backward)  43 us
    dot_general x39, matrix products, apply_axis(): jnp.einsum(PATTERNS[axis], matrix, values, precision=lax.Precision.HIGHEST)  40 us
    ppermute x15, starting transfers between devices, extended(): lax.ppermute(lax.slice_in_dim(block, 0, width, axis=dim), axis, backward)  36.7 us
  transfers between devices with their start and end apart: 30, of which 16 were waited for; matrix products, arithmetic and copies ran while one was open for 5% of the time, Pallas kernels for 0%

commit v1 on v0

v1 whole, which is shorter than its diff:
```python
import functools
import jax
import jax.numpy as jnp
import numpy as np
from jax import lax
from jax.experimental import pallas as pl
from jax.experimental.pallas import tpu as pltpu
from jax.sharding import PartitionSpec as P

F32, BF16, I32 = jnp.float32, jnp.bfloat16, jnp.int32
CUBIC = (-0.0625, 0.0, 0.5625, 1.0, 0.5625, 0.0, -0.0625)
TAPS_AT = tuple((k - 3, w) for k, w in enumerate(CUBIC) if w != 0.0)

DEVICES = (4, 8, 8)
BX, BY, BZ = (32, 16, 8, 4, 2), (64, 32, 16, 8, 4), (128, 64, 32, 16, 8)
LOW = (0, -1, -2, -2, -2)
EX = (32, 19, 13, 9, 7)
EY = (64, 35, 21, 13, 9)
EZ = (128, 67, 37, 21, 13)
PY = (64, 40, 24, 16, 16)
OZ = (0, 0, 67, 104, 44)
X_SLABS = 9
SECOND = EX[2] - X_SLABS


def inside(level, axis, blocks, cls):
    count = (EX, EY, EZ)[axis][level]
    cells = LOW[level] + np.arange(count)
    ok = np.ones(count, bool)
    if cls == 0:
        ok &= cells >= 0
    if cls == 2:
        ok &= cells < blocks[level]
    return ok


def cubic_matrix(level, axis, blocks, cls):
    ext = (EX, EY, EZ)[axis]
    fine = LOW[level] + np.arange(ext[level])
    coarse = LOW[level + 1] + np.arange(ext[level + 1])
    offset = fine[None, :] - 2 * coarse[:, None]
    matrix = np.zeros(offset.shape)
    for k, w in TAPS_AT:
        matrix[offset == k] = w
    return matrix * inside(level, axis, blocks, cls)[None, :] * inside(level + 1, axis, blocks, cls)[:, None]


def padded(matrix, rows, columns, at_row=0, at_column=0):
    out = np.zeros((rows, columns))
    out[at_row : at_row + matrix.shape[0], at_column : at_column + matrix.shape[1]] = matrix
    return out


def constants():
    out = {}
    for l in range(4):
        out[f"ry{l + 1}"] = np.stack([padded(cubic_matrix(l, 1, BY, c), PY[l + 1], PY[l]) for c in range(3)])
        out[f"py{l}"] = np.stack([padded(cubic_matrix(l, 1, BY, c).T, PY[l], PY[l + 1]) for c in range(3)])
        out[f"rz{l + 1}"] = np.stack(
            [padded(cubic_matrix(l, 2, BZ, c).T, 128, 128, OZ[l], OZ[l + 1]) for c in range(3)]
        )
    for l in range(1, 5):
        mats = []
        for c in range(3):
            m = cubic_matrix(0, 2, BZ, c)
            for k in range(1, l):
                m = cubic_matrix(k, 2, BZ, c) @ m
            mats.append(padded(m, 128, 128))
        out[f"pz{l}"] = np.stack(mats)
    return out


CONSTS = constants()


def split(v):
    hi = v.astype(BF16)
    return hi, (v - hi.astype(F32)).astype(BF16)


def dot(a, b, dims=(((1,), (0,)), ((), ()))):
    return lax.dot_general(a, b, dims, preferred_element_type=F32)


def dot_left_exact(m, b):
    hi, lo = split(b)
    return dot(m, hi) + dot(m, lo)


def dot_right_exact(a, m):
    hi, lo = split(a)
    return dot(hi, m) + dot(lo, m)


def dot3(a, b, dims=(((1,), (0,)), ((), ()))):
    return dot(a[0], b[0], dims) + (dot(a[0], b[1], dims) + dot(a[1], b[0], dims))


def class_of(axis, count):
    i = lax.axis_index(axis)
    return jnp.where(i == 0, 0, jnp.where(i == count - 1, 2, 1))


def x_mask(level, cell):
    i = lax.axis_index("gx")
    if cell < 0:
        return jnp.where(i * BX[level] + cell >= 0, 1.0, 0.0).astype(F32)
    if cell >= BX[level]:
        return jnp.where(i * BX[level] + cell < BX[level] * DEVICES[0], 1.0, 0.0).astype(F32)
    return None


def masked(value, mask):
    return value if mask is None else value * mask


def lanes_mask(first, count):
    lane = lax.broadcasted_iota(I32, (1, 128), 1)
    return (lane >= first) & (lane < first + count)


def restrict_x(level, slab):
    first, last = LOW[level], LOW[level] + EX[level]
    out = []
    for i in range(LOW[level + 1], LOW[level + 1] + EX[level + 1]):
        total = None
        for k, w in TAPS_AT:
            if first <= 2 * i + k < last:
                term = slab(2 * i + k)
                term = term if w == 1.0 else term * w
                total = term if total is None else total + term
        out.append(masked(total, x_mask(level + 1, i)))
    return out


def restrict_kernel(q_ref, *refs):
    names = [f"r{a}{l}" for l in range(1, 5) for a in "yz"]
    mats = dict(zip(names, refs[:8]))
    c1_ref, s1f_ref, s1b_ref, pack_ref = refs[8:12]
    cy, cz = class_of("gy", 8), class_of("gz", 8)
    slab = lambda i: q_ref[i]
    packed = [jnp.zeros((24, 128), F32) for _ in range(X_SLABS)]
    for l in range(1, 5):
        planes = restrict_x(l - 1, slab)
        n, rows = EX[l], PY[l]
        wide = jnp.concatenate(planes, axis=1)
        wide = dot_left_exact(mats[f"ry{l}"][cy], wide)
        tall = jnp.concatenate([wide[:, s * 128 : (s + 1) * 128] for s in range(n)], axis=0)
        tall = dot_right_exact(tall, mats[f"rz{l}"][cz])
        planes = [tall[s * rows : (s + 1) * rows] for s in range(n)]
        if l == 1:
            for s in range(n):
                c1_ref[s] = planes[s]
                if s < 11:
                    s1b_ref[s] = planes[s]
                if s >= n - 11:
                    s1f_ref[s - (n - 11)] = planes[s]
        else:
            for s in range(n):
                value = planes[s]
                if rows < 24:
                    value = jnp.concatenate([value, jnp.zeros((24 - rows, 128), F32)], axis=0)
                if s >= X_SLABS:
                    packed[s - X_SLABS] += pltpu.roll(value, 64, 1)
                else:
                    packed[s] += value
        current = planes
        slab = lambda i, current=current, low=LOW[l]: current[i - low]
    for d in range(4):
        for s in range(X_SLABS):
            pack_ref[d, s] = packed[s]


def conv_x(out_count, taps_ref, level, load, store):
    taps = [taps_ref[level * 51 + t] for t in range(17)]
    for i in range(out_count):
        total = load(i) * taps[0]
        for t in range(1, 17):
            total = total + load(i + t) * taps[t]
        store(i, total)


def x_kernel(taps_ref, q_ref, xl_ref, xr_ref, c1_ref, l1_ref, r1_ref, pack_ref,
             y0_ref, o1_ref, o2_ref, fw_ref, bw_ref, v_ref, q1, g2, g3, g4, o3, o4):
    ix = lax.axis_index("gx")
    taps0 = [taps_ref[t] for t in range(17)]

    def level0(j, _):
        rows = pl.ds(pl.multiple_of(j * 8, 8), 8)
        acc = [None] * 32
        for p in range(48):
            v = xl_ref[p, rows, :] if p < 8 else q_ref[p - 8, rows, :] if p < 40 else xr_ref[p - 40, rows, :]
            for t in range(17):
                i = p - t
                if 0 <= i < 32:
                    term = v * taps0[t]
                    acc[i] = term if acc[i] is None else acc[i] + term
        for i in range(32):
            y0_ref[i, rows, :] = acc[i]
        return 0

    lax.fori_loop(0, 8, level0, 0)
    for i in range(32):
        bw_ref[pl.ds(i * 8, 8), :] = y0_ref[i, pl.ds(0, 8), :]
        fw_ref[pl.ds(i * 8, 8), :] = y0_ref[i, pl.ds(56, 8), :]
    for r in range(35):
        cell = r - 9
        total = None
        for ref, at in ((c1_ref, cell + 1), (l1_ref, cell + 9), (r1_ref, cell - 15)):
            if 0 <= at < ref.shape[0]:
                total = ref[at] if total is None else total + ref[at]
        q1[r] = total

    def keep1(i, total):
        o1_ref[i] = masked(total, x_mask(1, LOW[1] + i))

    conv_x(EX[1], taps_ref, 1, lambda r: q1[r], keep1)
    for level, g in ((2, g2), (3, g3), (4, g4)):
        rows, total_cells = g.shape[1], BX[level] * 4
        g[...] = jnp.zeros_like(g)
        for d in range(4):
            for s in range(EX[level]):
                cell = d * BX[level] + LOW[level] + s
                if not 0 <= cell < total_cells:
                    continue
                if s >= X_SLABS:
                    value = pltpu.roll(pack_ref[d, s - X_SLABS], 64, 1)
                else:
                    value = pack_ref[d, s, pl.ds(0, rows), :]
                g[cell + 10] += value
        out = {2: o2_ref, 3: o3, 4: o4}[level]

        def keep(i, total, out=out, level=level):
            out[i] = masked(total, x_mask(level, LOW[level] + i))

        start = ix * BX[level] + 10 + LOW[level] - 8
        conv_x(EX[level], taps_ref, level, lambda r, g=g, start=start: g[start + r], keep)
    low = lanes_mask(0, EZ[1])
    for s in range(EX[1]):
        f, b = o1_ref[s, pl.ds(24, 16), :], o1_ref[s, pl.ds(0, 16), :]
        if s < EX[2]:
            f = jnp.where(low, f, o2_ref[s, pl.ds(8, 16), :])
            b = jnp.where(low, b, o2_ref[s, pl.ds(0, 16), :])
        fw_ref[pl.ds(256 + s * 16, 16), :] = f
        bw_ref[pl.ds(256 + s * 16, 16), :] = b
    columns = []
    for level, o, members in ((3, o3, range(0, 5)), (3, o3, range(5, 9)), (4, o4, range(0, 7))):
        mask = lanes_mask(OZ[level], EZ[level])
        total = jnp.zeros((16, 128), F32)
        for n, s in enumerate(members):
            value = jnp.where(mask, o[s], 0.0)
            total = total + pltpu.roll(value, (n * EZ[level] - OZ[level]) % 128, 1)
        columns.append(total)
    for d in range(8):
        for c in range(3):
            v_ref[d, :, pl.ds(c * 128, 128)] = columns[c]


def toeplitz(taps_ref, level, axis, diff):
    total = jnp.zeros(diff.shape, F32)
    for t in range(17):
        total = jnp.where(diff == t, taps_ref[level * 51 + axis * 17 + t], total)
    return total


def store_split(refs, value, rows=None):
    hi, lo = split(value)
    if rows is None:
        refs[0][...] = hi
        refs[1][...] = lo
    else:
        refs[0][rows, :] = hi
        refs[1][rows, :] = lo


def prep_kernel(taps_ref, pz1, pz2, pz3, pz4, *out):
    iy = lax.axis_index("gy")
    cz = class_of("gz", 8)
    iz = lax.axis_index("gz")
    bad = 1000
    iota = lambda shape, d: lax.broadcasted_iota(I32, shape, d)
    outs = [out[2 * k : 2 * k + 2] for k in range(10)]

    def out_cells(level, blocks, ext, index, position, count):
        cell = index + LOW[level]
        g = cell + position * blocks[level]
        ok = (index < ext[level]) & (g >= 0) & (g < blocks[level] * count)
        return jnp.where(ok, cell, -bad)

    for level, width, ref in ((0, 80, outs[0]), (1, 72, outs[1]), (2, 56, outs[2])):
        shape = (PY[level], width)
        i, j = iota(shape, 0), iota(shape, 1)
        to = out_cells(level, BY, EY, i, iy, 8)
        if level == 0:
            at = j - 8
        else:
            halo, reach = 16, 11 if level == 1 else 13
            own = j - halo
            upper = own - PY[level]
            lowest = LOW[level] - 8
            at = jnp.where(
                own < 0,
                jnp.where(j < reach, j + lowest, bad),
                jnp.where(
                    upper < 0,
                    jnp.where(own < EY[level], own + LOW[level], bad),
                    jnp.where(upper < reach, upper + LOW[level] + BY[level], bad),
                ),
            )
        store_split(ref, toeplitz(taps_ref, level, 1, at - to + 8))
    for level, ref in ((3, outs[3]), (4, outs[4])):
        i, j = iota((16, 128), 0), iota((16, 128), 1)
        to = out_cells(level, BY, EY, i, iy, 8)
        d, r = j // 16, j % 16
        at = jnp.where(r < EY[level], (d - iy) * BY[level] + r + LOW[level], bad)
        store_split(ref, toeplitz(taps_ref, level, 1, at - to + 8))
    j = iota((128, 128), 0)
    c = iota((128, 128), 1)
    store_split(outs[5], toeplitz(taps_ref, 0, 2, j - c + 8), pl.ds(0, 128))
    j, c = iota((16, 128), 0), iota((16, 128), 1)
    store_split(outs[5], toeplitz(taps_ref, 0, 2, jnp.where(j < 8, j - 8, j - 8 + 128) - c + 8), pl.ds(128, 16))
    for level, pz, ref in ((1, pz1, outs[6]), (2, pz2, outs[7]), (3, pz3, outs[8]), (4, pz4, outs[9])):
        prolong = split(pz[cz])
        c = iota((128, 128), 1)
        to = out_cells(level, BZ, EZ, c, iz, 8)
        j = iota((128, 128), 0) - OZ[level]
        at = jnp.where((j >= 0) & (j < EZ[level]), j + LOW[level], bad)
        store_split(ref, dot3(split(toeplitz(taps_ref, level, 2, at - to + 8)), prolong), pl.ds(0, 128))
        rows = 64 if level == 4 else 32
        c = iota((rows, 128), 1)
        to = out_cells(level, BZ, EZ, c, iz, 8)
        j = iota((rows, 128), 0)
        r = j % 16
        if level == 4:
            d = j // 16
            shift = jnp.where(d == 0, -2, jnp.where(d == 1, -1, jnp.where(d == 2, 1, 2))) * BZ[4]
            at = jnp.where(r < EZ[4], shift + r + LOW[4], bad)
        else:
            reach = 11 if level == 1 else 13
            at = jnp.where(j < 16, r + LOW[level] - 8, r + LOW[level] + BZ[level])
            at = jnp.where(r < reach, at, bad)
        store_split(ref, dot3(split(toeplitz(taps_ref, level, 2, at - to + 8)), prolong), pl.ds(128, rows))


def y_kernel(y0_ref, o1_ref, o2_ref, lo_ref, hi_ref, v_ref, *refs):
    my = [(refs[2 * k], refs[2 * k + 1]) for k in range(5)]
    z0_ref, z1_ref, z2_ref, z3_ref, z4_ref, fw_ref, bw_ref, t4_ref = refs[10:]
    m0 = (my[0][0][...], my[0][1][...])
    for base in range(0, 32, 4):
        parts = []
        for i in range(base, base + 4):
            parts.append(jnp.concatenate(
                [lo_ref[pl.ds(i * 8, 8), :], y0_ref[i], hi_ref[pl.ds(i * 8, 8), :]], axis=0))
        out = dot3(m0, split(jnp.concatenate(parts, axis=1)))
        for n in range(4):
            z0_ref[pl.ds((base + n) * 64, 64), :] = out[:, n * 128 : (n + 1) * 128]
    for level, o_ref, z_ref in ((1, o1_ref, z1_ref), (2, o2_ref, z2_ref)):
        m = (my[level][0][...], my[level][1][...])
        n, rows = EX[level], PY[level]
        parts = [jnp.concatenate([lo_ref[pl.ds(256 + s * 16, 16), :], o_ref[s], hi_ref[pl.ds(256 + s * 16, 16), :]], axis=0)
                 for s in range(n)]
        out = dot3(m, split(jnp.concatenate(parts, axis=1)))
        for s in range(n):
            z_ref[pl.ds(s * rows, rows), :] = out[:, s * 128 : (s + 1) * 128]
    everything = jnp.concatenate([v_ref[d] for d in range(8)], axis=0)
    pair = split(everything)
    o3 = dot3((my[3][0][...], my[3][1][...]), (pair[0][:, :256], pair[1][:, :256]))
    o4 = dot3((my[4][0][...], my[4][1][...]), (pair[0][:, 256:], pair[1][:, 256:]))
    for level, source, members, z_ref in (
        (3, o3[:, :128], range(0, 5), z3_ref), (3, o3[:, 128:], range(5, 9), z3_ref), (4, o4, range(0, 7), z4_ref)
    ):
        for n, s in enumerate(members):
            z_ref[pl.ds(s * 16, 16), :] = pltpu.roll(source, (OZ[level] - n * EZ[level]) % 128, 1)
    for k in range(16):
        t = z0_ref[pl.ds(k * 128, 128), :].T
        bw_ref[pl.ds(0, 8), pl.ds(k * 128, 128)] = t[:8]
        fw_ref[pl.ds(0, 8), pl.ds(k * 128, 128)] = t[120:]
    for k in range(6):
        size = 128 if k < 5 else 120
        block = z1_ref[pl.ds(k * 128, size), :]
        if size < 128:
            block = jnp.concatenate([block, jnp.zeros((128 - size, 128), F32)], axis=0)
        t = block.T
        bw_ref[pl.ds(8, 16), pl.ds(k * 128, 128)] = t[0:16]
        fw_ref[pl.ds(8, 16), pl.ds(k * 128, 128)] = t[56:72]
    for level, z_ref, at, f, count in ((2, z2_ref, 768, 24, 312), (3, z3_ref, 1152, 8, 144)):
        for k in range((count + 127) // 128):
            size = min(128, count - k * 128)
            block = pltpu.roll(z_ref[pl.ds(k * 128, size), :], (-OZ[level]) % 128, 1)
            if size < 128:
                block = jnp.concatenate([block, jnp.zeros((128 - size, 128), F32)], axis=0)
            t = block.T
            bw_ref[pl.ds(8, 16), pl.ds(at + k * 128, 128)] = t[0:16]
            fw_ref[pl.ds(8, 16), pl.ds(at + k * 128, 128)] = t[f : f + 16]
    block = pltpu.roll(z4_ref[...], (-OZ[4]) % 128, 1)
    t = jnp.concatenate([block, jnp.zeros((16, 128), F32)], axis=0).T[:16]
    for ref in (bw_ref, fw_ref):
        ref[pl.ds(8, 16), pl.ds(1408, 128)] = t
    t4_ref[...] = t


def z_kernel(z0_ref, z1_ref, z2_ref, z3_ref, z4_ref, lo_ref, hi_ref, l4_ref, h4_ref, *refs):
    mz = [(refs[2 * k], refs[2 * k + 1]) for k in range(5)]
    py = refs[10:14]
    out_ref = refs[14]
    acc = refs[15]
    cy = class_of("gy", 8)
    first = (((0,), (0,)), ((), ()))

    def level_out(level, own, halo, rows_own=128):
        a, b = mz[level]
        k = halo.shape[0]
        return dot3(split(own), (a[pl.ds(0, 128), :], b[pl.ds(0, 128), :])) + dot3(
            split(halo), (a[pl.ds(128, k), :], b[pl.ds(128, k), :]), first)

    at = {1: 0, 2: 768, 3: 1152, 4: 1408}
    rows = {1: 760, 2: 312, 3: 144, 4: 112}
    z_refs = {1: z1_ref, 2: z2_ref, 3: z3_ref, 4: z4_ref}
    total = None
    for level in (4, 3, 2, 1):
        n = rows[level]
        columns = pl.ds(at[level], (n + 127) // 128 * 128)
        if level == 4:
            halo = jnp.concatenate([l4_ref[...], lo_ref[pl.ds(8, 16), columns], hi_ref[pl.ds(8, 16), columns], h4_ref[...]], axis=0)
        else:
            halo = jnp.concatenate([lo_ref[pl.ds(8, 16), columns], hi_ref[pl.ds(8, 16), columns]], axis=0)
        full = (n + 127) // 128 * 128
        own = z_refs[level][...]
        if full > n:
            own = jnp.concatenate([own, jnp.zeros((full - n, 128), F32)], axis=0)
        term = level_out(level, own, halo)
        planes = [term[s * PY[level] : (s + 1) * PY[level]] for s in range(EX[level])]
        if total is not None:
            planes = [a + b for a, b in zip(planes, total)]
        fine = level - 1
        wide = dot_left_exact(py[fine][cy], jnp.concatenate(planes, axis=1))
        coarse = [wide[:, s * 128 : (s + 1) * 128] for s in range(EX[level])]
        total = []
        for cell in range(LOW[fine], LOW[fine] + EX[fine]):
            value = None
            for k, w in TAPS_AT:
                if (cell - k) % 2 == 0:
                    s = (cell - k) // 2 - LOW[level]
                    if 0 <= s < EX[level]:
                        term = coarse[s] if w == 1.0 else coarse[s] * w
                        value = term if value is None else value + term
            value = masked(value, x_mask(fine, cell)) if fine else value
            total.append(value)
            if fine == 0:
                acc[cell] = value
    halo = jnp.concatenate([lo_ref[pl.ds(0, 8), :], hi_ref[pl.ds(0, 8), :]], axis=0)
    for k in range(4):
        term = level_out(0, z0_ref[pl.ds(k * 512, 512), :], halo[:, k * 512 : (k + 1) * 512])
        for i in range(8):
            out_ref[k * 8 + i] = acc[k * 8 + i] + term[i * 64 : (i + 1) * 64]


VM = pl.BlockSpec(memory_space=pltpu.VMEM)
SM = pl.BlockSpec(memory_space=pltpu.SMEM)


def call(body, name, shapes, in_specs, scratch=(), flops=10**8):
    return pl.pallas_call(
        body,
        name=name,
        out_shape=[jax.ShapeDtypeStruct(s, d) for s, d in shapes],
        in_specs=in_specs,
        out_specs=[VM] * len(shapes),
        scratch_shapes=list(scratch),
        cost_estimate=pl.CostEstimate(flops=flops, bytes_accessed=2**21, transcendentals=0),
    )


def steps(axis, by):
    count = lax.axis_size(axis)
    return [(i, i + by) for i in range(count) if 0 <= i + by < count]


def per_device(charges, kernel_taps):
    taps = kernel_taps.reshape(-1)
    shift = lambda v, axis, by: lax.ppermute(v, axis, steps(axis, by))
    const = {k: jnp.asarray(v, F32 if k.startswith("pz") else BF16) for k, v in CONSTS.items()}
    xl = shift(charges[24:], "gx", 1)
    xr = shift(charges[:8], "gx", -1)
    c1, s1f, s1b, pack = call(
        restrict_kernel, "restrict",
        [((19, 40, 128), F32), ((11, 40, 128), F32), ((11, 40, 128), F32), ((4, X_SLABS, 24, 128), F32)],
        [VM] * 9,
    )(charges, *[const[f"r{a}{l}"] for l in range(1, 5) for a in "yz"])
    l1 = shift(s1f, "gx", 1)
    r1 = shift(s1b, "gx", -1)
    packs = lax.all_to_all(pack, "gx", 0, 0)
    widths = [(64, 80), (40, 72), (24, 56), (16, 128), (16, 128), (144, 128), (160, 128), (160, 128), (160, 128), (192, 128)]
    mats = call(
        prep_kernel, "prep", [(w, BF16) for w in widths for _ in range(2)], [SM] + [VM] * 4
    )(taps, *[const[f"pz{l}"] for l in range(1, 5)])
    y0, o1, o2, fw, bw, v = call(
        x_kernel, "alongx",
        [((32, 64, 128), F32), ((19, 40, 128), F32), ((13, 24, 128), F32), ((560, 128), F32), ((560, 128), F32),
         ((8, 16, 384), F32)],
        [SM] + [VM] * 7,
        [pltpu.VMEM((35, 40, 128), F32), pltpu.VMEM((53, 24, 128), F32), pltpu.VMEM((37, 16, 128), F32),
         pltpu.VMEM((29, 16, 128), F32), pltpu.VMEM((9, 16, 128), F32), pltpu.VMEM((7, 16, 128), F32)],
    )(taps, charges, xl, xr, c1, l1, r1, packs)
    lo = shift(fw, "gy", 1)
    hi = shift(bw, "gy", -1)
    vs = lax.all_to_all(v, "gy", 0, 0)
    z0, z1, z2, z3, z4, fw, bw, t4 = call(
        y_kernel, "alongy",
        [((2048, 128), F32), ((760, 128), F32), ((312, 128), F32), ((144, 128), F32), ((112, 128), F32),
         ((24, 2048), F32), ((24, 2048), F32), ((16, 128), F32)],
        [VM] * 16,
    )(y0, o1, o2, lo, hi, vs, *mats[:10])
    lo = shift(fw, "gz", 1)
    hi = shift(bw, "gz", -1)
    l4 = shift(t4, "gz", 2)
    h4 = shift(t4, "gz", -2)
    (out,) = call(
        z_kernel, "alongz", [((32, 64, 128), F32)], [VM] * 23, [pltpu.VMEM((32, 64, 128), F32)]
    )(z0, z1, z2, z3, z4, lo, hi, l4, h4, *mats[10:], *[const[f"py{l}"] for l in range(4)])
    return out


def solution(mesh):
    return jax.shard_map(
        per_device,
        mesh=mesh,
        in_specs=(P("gx", "gy", "gz"), P()),
        out_specs=P("gx", "gy", "gz"),
        check_vma=False,
    )
```

time: 601 us -> 80.7 us (0.13)
  the two profiles are of different devices: /device:TPU:9 before, /device:TPU:216 now
where the time goes in v1:
time: 80.7 us; the launch traced here: 80 us
  starting transfers between devices  38.9 us (48%)
  Pallas kernels  20.8 us (26%)
  waiting for transfers between devices  16.8 us (21%)
  local copies, waits for them, and re-layouts  3.26 us (4%)
    ppermute x10, starting transfers between devices, per_device(): shift = lambda v, axis, by: lax.ppermute(v, axis, steps(axis, by))  29.3 us
    ppermute x10, waiting for transfers between devices, per_device(): shift = lambda v, axis, by: lax.ppermute(v, axis, steps(axis, by))  16.8 us
    pallas_call x1, Pallas kernels, per_device(): call(z_kernel, 'alongz', [((32, 64, 128), F32)], [VM] * 23, [pltpu.VMEM((...  5.77 us
    all_to_all x1, starting transfers between devices, per_device(): vs = lax.all_to_all(v, 'gy', 0, 0)  5.28 us
    pallas_call x1, Pallas kernels, per_device(): call(x_kernel, 'alongx', [((32, 64, 128), F32), ((19, 40, 128), F32), ((1...  4.96 us
    all_to_all x1, starting transfers between devices, per_device(): packs = lax.all_to_all(pack, 'gx', 0, 0)  4.29 us
    pallas_call x1, Pallas kernels, per_device(): call(restrict_kernel, 'restrict', [((19, 40, 128), F32), ((11, 40, 128),...  3.87 us
    pallas_call x1, Pallas kernels, per_device(): call(y_kernel, 'alongy', [((2048, 128), F32), ((760, 128), F32), ((312, 1...  3.62 us
  transfers between devices with their start and end apart: 12, of which 6 were waited for; matrix products, arithmetic and copies ran while one was open for 1% of the time, Pallas kernels for 3%

profile of v1, /device:TPU:216, one launch (start us, length us, event | category | flops | bytes accessed | tf_op | source)
XLA Modules:
  0.0 80.0 jit_solution(17968714767373433743)
XLA Ops:
  0.0 3.9 %restrict.1 = (f32[19,40,128]{2,1,0:T(8,128)}, f32[11,40,128]{2,1,0:T(8,128)}, f32[11,40,128]{2,1,0:T(8,128)}, f32[4,9,24,128]{3,2,1,0:T(8,128)}) custom-call(f32[32,64,128]{2,1,0:T(8,128)} %q_ref.3, bf16[3,40,64]{2,1,0:T(8,128)(2,1)} %constant.32.clone.refs_0_, bf16[3,128,128]{2,1,0:T(8,128)(2,1)} %constant.34.clone.refs_1_, ...), custom_call_target="tpu_custom_call" | custom-call | flops 100000000 | bytes 2097152 | tf_op jit(solution)/shard_map/restrict/pallas_call | solution.py:485
  3.9 4.3 %all-to-all-start = ((f32[4,9,24,128]{3,2,1,0:T(8,128)}), f32[4,9,24,128]{3,2,1,0:T(8,128)S(1)}, u32[]{:S(2)}, u32[]{:S(2)}) async-start(f32[4,9,24,128]{3,2,1,0:T(8,128)} %get-tuple-element.46), calls=%async_computation | async-start | bytes 884736 | tf_op jit(solution)/shard_map/all_to_all | solution.py:492
  8.2 1.4 %collective-permute-start.1 = (f32[8,64,128]{2,1,0:T(8,128)S(1)}, f32[8,64,128]{2,1,0:T(8,128)S(1)}, u32[]{:S(2)}, u32[]{:S(2)}) collective-permute-start(f32[8,64,128]{2,1,0:T(8,128)S(1)} %get-tuple-element.81), channel_id=1, source_target_pairs={{64,0},{128,64},{192,128},{65,1},{129,65},{193,129},{66,2},{130,66... | collective-permute-start | bytes 786440 | tf_op jit(solution)/shard_map/ppermute | solution.py:481
  9.7 4.6 %collective-permute-start = (f32[8,64,128]{2,1,0:T(8,128)S(1)}, f32[8,64,128]{2,1,0:T(8,128)S(1)}, u32[]{:S(2)}, u32[]{:S(2)}) collective-permute-start(f32[8,64,128]{2,1,0:T(8,128)S(1)} %get-tuple-element.82), channel_id=1, source_target_pairs={{0,64},{64,128},{128,192},{1,65},{65,129},{129,193},{2,66},{66,130... | collective-permute-start | bytes 786440 | tf_op jit(solution)/shard_map/ppermute | solution.py:481
  14.2 3.9 %collective-permute-start.2 = (f32[11,40,128]{2,1,0:T(8,128)S(1)}, f32[11,40,128]{2,1,0:T(8,128)S(1)}, u32[]{:S(2)}, u32[]{:S(2)}) collective-permute-start(f32[11,40,128]{2,1,0:T(8,128)S(1)} %copy-done.16), channel_id=1, source_target_pairs={{0,64},{64,128},{128,192},{1,65},{65,129},{129,193},{2,66},{66,130... | collective-permute-start | bytes 675848 | tf_op jit(solution)/shard_map/ppermute | solution.py:481
  18.2 1.3 %collective-permute-start.3 = (f32[11,40,128]{2,1,0:T(8,128)S(1)}, f32[11,40,128]{2,1,0:T(8,128)S(1)}, u32[]{:S(2)}, u32[]{:S(2)}) collective-permute-start(f32[11,40,128]{2,1,0:T(8,128)S(1)} %copy-done.15), channel_id=1, source_target_pairs={{64,0},{128,64},{192,128},{65,1},{129,65},{193,129},{66,2},{130,66... | collective-permute-start | bytes 675848 | tf_op jit(solution)/shard_map/ppermute | solution.py:481
  19.5 0.7 reshape.3.taps_ref
  20.2 3.9 %collective-permute-done.2.l1_ref = f32[11,40,128]{2,1,0:T(8,128)S(1)} collective-permute-done((f32[11,40,128]{2,1,0:T(8,128)S(1)}, f32[11,40,128]{2,1,0:T(8,128)S(1)}, u32[]{:S(2)}, u32[]{:S(2)}) %collective-permute-start.2) | collective-permute-done | bytes 225312 | tf_op jit(solution)/shard_map/ppermute | solution.py:481
  24.0 2.0 %collective-permute-done.3.r1_ref = f32[11,40,128]{2,1,0:T(8,128)S(1)} collective-permute-done((f32[11,40,128]{2,1,0:T(8,128)S(1)}, f32[11,40,128]{2,1,0:T(8,128)S(1)}, u32[]{:S(2)}, u32[]{:S(2)}) %collective-permute-start.3) | collective-permute-done | bytes 225312 | tf_op jit(solution)/shard_map/ppermute | solution.py:481
  26.1 0.6 copy-done.8
  27.1 5.0 %alongx.1 = (f32[32,64,128]{2,1,0:T(8,128)}, f32[19,40,128]{2,1,0:T(8,128)}, f32[13,24,128]{2,1,0:T(8,128)}, f32[560,128]{1,0:T(8,128)}, f32[560,128]{1,0:T(8,128)}, /*index=5*/f32[8,16,384]{2,1,0:T(8,128)}) custom-call(f32[255]{0:T(256)} %reshape.3.taps_ref, f32[32,64,128]{2,1,0:T(8,128)} %q_ref.3, f32[8,64,128]{2,1,0:T(8,128)} %copy-done.6, ...), custom_call_target="tpu_custom_call" | custom-call | flops 100000000 | bytes 2097152 | tf_op jit(solution)/shard_map/alongx/pallas_call | solution.py:497
  32.1 5.3 %all-to-all-start.1 = ((f32[8,16,384]{2,1,0:T(8,128)}), f32[8,16,384]{2,1,0:T(8,128)S(1)}, u32[]{:S(2)}, u32[]{:S(2)}) async-start(f32[8,16,384]{2,1,0:T(8,128)} %get-tuple-element.52), calls=%async_computation.1 | async-start | bytes 393216 | tf_op jit(solution)/shard_map/all_to_all | solution.py:507
  37.4 3.4 %collective-permute-start.4 = (f32[560,128]{1,0:T(8,128)}, f32[560,128]{1,0:T(8,128)S(1)}, u32[]{:S(2)}, u32[]{:S(2)}) collective-permute-start(f32[560,128]{1,0:T(8,128)} %get-tuple-element.50), channel_id=1, source_target_pairs={{0,8},{8,16},{16,24},{24,32},{32,40},{40,48},{48,56},{1,9},{9,17},... | collective-permute-start | bytes 860168 | tf_op jit(solution)/shard_map/ppermute | solution.py:481
  40.7 2.5 %collective-permute-start.5 = (f32[560,128]{1,0:T(8,128)S(1)}, f32[560,128]{1,0:T(8,128)S(1)}, u32[]{:S(2)}, u32[]{:S(2)}) collective-permute-start(f32[560,128]{1,0:T(8,128)S(1)} %copy-done.14), channel_id=1, source_target_pairs={{8,0},{16,8},{24,16},{32,24},{40,32},{48,40},{56,48},{9,1},{17,9},... | collective-permute-start | bytes 860168 | tf_op jit(solution)/shard_map/ppermute | solution.py:481
  43.2 2.6 %prep.1 = (bf16[64,80]{1,0:T(8,128)(2,1)}, bf16[64,80]{1,0:T(8,128)(2,1)}, bf16[40,72]{1,0:T(8,128)(2,1)}, bf16[40,72]{1,0:T(8,128)(2,1)}, bf16[24,56]{1,0:T(8,1...) custom-call(f32[255]{0:T(256)} %reshape.3.taps_ref, ...), custom_call_target="tpu_custom_call" | custom-call | flops 100000000 | bytes 2097152 | tf_op jit(solution)/shard_map/prep/pallas_call | solution.py:494
  46.1 5.3 %collective-permute-done.5.hi_ref = f32[560,128]{1,0:T(8,128)S(1)} collective-permute-done((f32[560,128]{1,0:T(8,128)S(1)}, f32[560,128]{1,0:T(8,128)S(1)}, u32[]{:S(2)}, u32[]{:S(2)}) %collective-permute-start.5) | collective-permute-done | bytes 286752 | tf_op jit(solution)/shard_map/ppermute | solution.py:481
  51.4 0.7 copy-done.4
  52.2 3.6 %alongy.1 = (f32[2048,128]{1,0:T(8,128)}, f32[760,128]{1,0:T(8,128)}, f32[312,128]{1,0:T(8,128)}, f32[144,128]{1,0:T(8,128)}, f32[112,128]{1,0:T(8,128)}, /*inde...) custom-call(f32[32,64,128]{2,1,0:T(8,128)} %get-tuple-element.47.y0_ref, ...), custom_call_target="tpu_custom_call" | custom-call | flops 100000000 | bytes 2097152 | tf_op jit(solution)/shard_map/alongy/pallas_call | solution.py:508
  55.8 1.9 %collective-permute-start.6 = (f32[24,2048]{1,0:T(8,128)}, f32[24,2048]{1,0:T(8,128)S(1)}, u32[]{:S(2)}, u32[]{:S(2)}) collective-permute-start(f32[24,2048]{1,0:T(8,128)} %get-tuple-element.68), channel_id=1, source_target_pairs={{0,1},{1,2},{2,3},{3,4},{4,5},{5,6},{6,7},{8,9},{9,10},{10,11},{11... | collective-permute-start | bytes 589832 | tf_op jit(solution)/shard_map/ppermute | solution.py:481
  57.7 4.5 %collective-permute-start.7 = (f32[24,2048]{1,0:T(8,128)}, f32[24,2048]{1,0:T(8,128)S(1)}, u32[]{:S(2)}, u32[]{:S(2)}) collective-permute-start(f32[24,2048]{1,0:T(8,128)} %get-tuple-element.69), channel_id=1, source_target_pairs={{1,0},{2,1},{3,2},{4,3},{5,4},{6,5},{7,6},{9,8},{10,9},{11,10},{12... | collective-permute-start | bytes 589832 | tf_op jit(solution)/shard_map/ppermute | solution.py:481
  62.3 4.6 %collective-permute-start.9 = (f32[16,128]{1,0:T(8,128)}, f32[16,128]{1,0:T(8,128)S(1)}, u32[]{:S(2)}, u32[]{:S(2)}) collective-permute-start(f32[16,128]{1,0:T(8,128)} %get-tuple-element.70), channel_id=1, source_target_pairs={{2,0},{3,1},{4,2},{5,3},{6,4},{7,5},{10,8},{11,9},{12,10},{13,11},... | collective-permute-start | bytes 24584 | tf_op jit(solution)/shard_map/ppermute | solution.py:481
  66.8 1.3 %collective-permute-start.8 = (f32[16,128]{1,0:T(8,128)}, f32[16,128]{1,0:T(8,128)S(1)}, u32[]{:S(2)}, u32[]{:S(2)}) collective-permute-start(f32[16,128]{1,0:T(8,128)} %get-tuple-element.70), channel_id=1, source_target_pairs={{0,2},{1,3},{2,4},{3,5},{4,6},{5,7},{8,10},{9,11},{10,12},{11,13},... | collective-permute-start | bytes 24584 | tf_op jit(solution)/shard_map/ppermute | solution.py:481
  68.4 5.1 %collective-permute-done.8.l4_ref = f32[16,128]{1,0:T(8,128)S(1)} collective-permute-done((f32[16,128]{1,0:T(8,128)}, f32[16,128]{1,0:T(8,128)S(1)}, u32[]{:S(2)}, u32[]{:S(2)}) %collective-permute-start.8) | collective-permute-done | bytes 8224 | tf_op jit(solution)/shard_map/ppermute | solution.py:481
  74.2 5.8 %alongz.1 = f32[32,64,128]{2,1,0:T(8,128)} custom-call(f32[2048,128]{1,0:T(8,128)} %get-tuple-element.63.z0_ref, f32[760,128]{1,0:T(8,128)} %get-tuple-element.64.z1_ref, f32[312,128]{1,0:T(8,128)} %get-tuple-element.65.z2_ref, f32[144,128]{1,0:T(8,128)} %get-tuple-element.66.z3_ref, f32[112,128]{1,0:T(8,128)} %get-tuple-element.67.z4_ref, ...), custom_call_target="tpu_custom_call" | custom-call | flops 100000000 | bytes 2097152 | tf_op jit(solution)/shard_map/alongz/pallas_call | solution.py:518
  (41 shorter events, 1.8 us)
Async XLA Ops:
  0.0 8.2 %copy-start = (f32[32,64,128]{2,1,0:T(8,128)S(1)}, f32[32,64,128]{2,1,0:T(8,128)}, u32[]{:S(2)}) copy-start(f32[32,64,128]{2,1,0:T(8,128)} %q_ref.3) | copy-start | bytes 3145732
  3.9 22.2 %all-to-all-start = ((f32[4,9,24,128]{3,2,1,0:T(8,128)}), f32[4,9,24,128]{3,2,1,0:T(8,128)S(1)}, u32[]{:S(2)}, u32[]{:S(2)}) async-start(f32[4,9,24,128]{3,2,1,0:T(8,128)} %get-tuple-element.46), calls=%async_computation | async-start | bytes 884736 | tf_op jit(solution)/shard_map/all_to_all | solution.py:492
  8.2 6.1 %copy-start.16 = (f32[11,40,128]{2,1,0:T(8,128)S(1)}, f32[11,40,128]{2,1,0:T(8,128)}, u32[]{:S(2)}) copy-start(f32[11,40,128]{2,1,0:T(8,128)} %get-tuple-element.44) | copy-start | bytes 675844
  8.2 10.0 %copy-start.15 = (f32[11,40,128]{2,1,0:T(8,128)S(1)}, f32[11,40,128]{2,1,0:T(8,128)}, u32[]{:S(2)}) copy-start(f32[11,40,128]{2,1,0:T(8,128)} %get-tuple-element.45) | copy-start | bytes 675844
  8.2 11.3 %copy-start.11 = (f32[5,3,17]{2,1,0:T(4,128)S(1)}, f32[5,3,17]{2,1,0:T(4,128)}, u32[]{:S(2)}) copy-start(f32[5,3,17]{2,1,0:T(4,128)} %param.19) | copy-start | bytes 3064
  8.2 17.8 %collective-permute-start.1 = (f32[8,64,128]{2,1,0:T(8,128)S(1)}, f32[8,64,128]{2,1,0:T(8,128)S(1)}, u32[]{:S(2)}, u32[]{:S(2)}) collective-permute-start(f32[8,64,128]{2,1,0:T(8,128)S(1)} %get-tuple-element.81), channel_id=1, source_target_pairs={{64,0},{128,64},{192,128},{65,1},{129,65},{193,129},{66,2},{130,66... | collective-permute-start | bytes 786440 | tf_op jit(solution)/shard_map/ppermute | solution.py:481
  9.7 16.4 %collective-permute-start = (f32[8,64,128]{2,1,0:T(8,128)S(1)}, f32[8,64,128]{2,1,0:T(8,128)S(1)}, u32[]{:S(2)}, u32[]{:S(2)}) collective-permute-start(f32[8,64,128]{2,1,0:T(8,128)S(1)} %get-tuple-element.82), channel_id=1, source_target_pairs={{0,64},{64,128},{128,192},{1,65},{65,129},{129,193},{2,66},{66,130... | collective-permute-start | bytes 786440 | tf_op jit(solution)/shard_map/ppermute | solution.py:481
  14.2 9.8 %collective-permute-start.2 = (f32[11,40,128]{2,1,0:T(8,128)S(1)}, f32[11,40,128]{2,1,0:T(8,128)S(1)}, u32[]{:S(2)}, u32[]{:S(2)}) collective-permute-start(f32[11,40,128]{2,1,0:T(8,128)S(1)} %copy-done.16), channel_id=1, source_target_pairs={{0,64},{64,128},{128,192},{1,65},{65,129},{129,193},{2,66},{66,130... | collective-permute-start | bytes 675848 | tf_op jit(solution)/shard_map/ppermute | solution.py:481
  18.2 7.9 %collective-permute-start.3 = (f32[11,40,128]{2,1,0:T(8,128)S(1)}, f32[11,40,128]{2,1,0:T(8,128)S(1)}, u32[]{:S(2)}, u32[]{:S(2)}) collective-permute-start(f32[11,40,128]{2,1,0:T(8,128)S(1)} %copy-done.15), channel_id=1, source_target_pairs={{64,0},{128,64},{192,128},{65,1},{129,65},{193,129},{66,2},{130,66... | collective-permute-start | bytes 675848 | tf_op jit(solution)/shard_map/ppermute | solution.py:481
  24.0 2.1 %copy-start.7 = (f32[11,40,128]{2,1,0:T(8,128)}, f32[11,40,128]{2,1,0:T(8,128)S(1)}, u32[]{:S(2)}) copy-start(f32[11,40,128]{2,1,0:T(8,128)S(1)} %collective-permute-done.2.l1_ref) | copy-start | bytes 675844
  26.1 0.8 copy-start.5
  26.1 0.9 %copy-start.6 = (f32[8,64,128]{2,1,0:T(8,128)}, f32[8,64,128]{2,1,0:T(8,128)S(1)}, u32[]{:S(2)}) copy-start(f32[8,64,128]{2,1,0:T(8,128)S(1)} %collective-permute-done.xl_ref) | copy-start | bytes 786436
  26.1 1.0 %copy-start.1 = (f32[4,9,24,128]{3,2,1,0:T(8,128)}, f32[4,9,24,128]{3,2,1,0:T(8,128)S(1)}, u32[]{:S(2)}) copy-start(f32[4,9,24,128]{3,2,1,0:T(8,128)S(1)} %all-to-all-done.pack_ref) | copy-start | bytes 1327108
  32.1 8.7 %copy-start.14 = (f32[560,128]{1,0:T(8,128)S(1)}, f32[560,128]{1,0:T(8,128)}, u32[]{:S(2)}) copy-start(f32[560,128]{1,0:T(8,128)} %get-tuple-element.51) | copy-start | bytes 860164
  32.1 19.3 %all-to-all-start.1 = ((f32[8,16,384]{2,1,0:T(8,128)}), f32[8,16,384]{2,1,0:T(8,128)S(1)}, u32[]{:S(2)}, u32[]{:S(2)}) async-start(f32[8,16,384]{2,1,0:T(8,128)} %get-tuple-element.52), calls=%async_computation.1 | async-start | bytes 393216 | tf_op jit(solution)/shard_map/all_to_all | solution.py:507
  37.4 8.7 %collective-permute-start.4 = (f32[560,128]{1,0:T(8,128)}, f32[560,128]{1,0:T(8,128)S(1)}, u32[]{:S(2)}, u32[]{:S(2)}) collective-permute-start(f32[560,128]{1,0:T(8,128)} %get-tuple-element.50), channel_id=1, source_target_pairs={{0,8},{8,16},{16,24},{24,32},{32,40},{40,48},{48,56},{1,9},{9,17},... | collective-permute-start | bytes 860168 | tf_op jit(solution)/shard_map/ppermute | solution.py:481
  40.7 10.6 %collective-permute-start.5 = (f32[560,128]{1,0:T(8,128)S(1)}, f32[560,128]{1,0:T(8,128)S(1)}, u32[]{:S(2)}, u32[]{:S(2)}) collective-permute-start(f32[560,128]{1,0:T(8,128)S(1)} %copy-done.14), channel_id=1, source_target_pairs={{8,0},{16,8},{24,16},{32,24},{40,32},{48,40},{56,48},{9,1},{17,9},... | collective-permute-start | bytes 860168 | tf_op jit(solution)/shard_map/ppermute | solution.py:481
  46.1 5.3 %copy-start.3 = (f32[560,128]{1,0:T(8,128)}, f32[560,128]{1,0:T(8,128)S(1)}, u32[]{:S(2)}) copy-start(f32[560,128]{1,0:T(8,128)S(1)} %collective-permute-done.4.lo_ref) | copy-start | bytes 860164
  51.4 0.8 copy-start.2
  55.8 17.7 %collective-permute-start.6 = (f32[24,2048]{1,0:T(8,128)}, f32[24,2048]{1,0:T(8,128)S(1)}, u32[]{:S(2)}, u32[]{:S(2)}) collective-permute-start(f32[24,2048]{1,0:T(8,128)} %get-tuple-element.68), channel_id=1, source_target_pairs={{0,1},{1,2},{2,3},{3,4},{4,5},{5,6},{6,7},{8,9},{9,10},{10,11},{11... | collective-permute-start | bytes 589832 | tf_op jit(solution)/shard_map/ppermute | solution.py:481
  57.7 15.8 %collective-permute-start.7 = (f32[24,2048]{1,0:T(8,128)}, f32[24,2048]{1,0:T(8,128)S(1)}, u32[]{:S(2)}, u32[]{:S(2)}) collective-permute-start(f32[24,2048]{1,0:T(8,128)} %get-tuple-element.69), channel_id=1, source_target_pairs={{1,0},{2,1},{3,2},{4,3},{5,4},{6,5},{7,6},{9,8},{10,9},{11,10},{12... | collective-permute-start | bytes 589832 | tf_op jit(solution)/shard_map/ppermute | solution.py:481
  62.3 6.1 %collective-permute-start.9 = (f32[16,128]{1,0:T(8,128)}, f32[16,128]{1,0:T(8,128)S(1)}, u32[]{:S(2)}, u32[]{:S(2)}) collective-permute-start(f32[16,128]{1,0:T(8,128)} %get-tuple-element.70), channel_id=1, source_target_pairs={{2,0},{3,1},{4,2},{5,3},{6,4},{7,5},{10,8},{11,9},{12,10},{13,11},... | collective-permute-start | bytes 24584 | tf_op jit(solution)/shard_map/ppermute | solution.py:481
  66.8 6.7 %collective-permute-start.8 = (f32[16,128]{1,0:T(8,128)}, f32[16,128]{1,0:T(8,128)S(1)}, u32[]{:S(2)}, u32[]{:S(2)}) collective-permute-start(f32[16,128]{1,0:T(8,128)} %get-tuple-element.70), channel_id=1, source_target_pairs={{0,2},{1,3},{2,4},{3,5},{4,6},{5,7},{8,10},{9,11},{10,12},{11,13},... | collective-permute-start | bytes 24584 | tf_op jit(solution)/shard_map/ppermute | solution.py:481
  68.4 5.1 %copy-start.12 = (f32[16,128]{1,0:T(8,128)}, f32[16,128]{1,0:T(8,128)S(1)}, u32[]{:S(2)}) copy-start(f32[16,128]{1,0:T(8,128)S(1)} %collective-permute-done.9.h4_ref) | copy-start | bytes 24580
  (5 other events, 3.4 us)

commit v2 on v1

v2 whole, which is shorter than its diff:
```python
import jax
import jax.numpy as jnp
from jax import lax
from jax.experimental import pallas as pl
from jax.experimental.pallas import tpu as pltpu
from jax.sharding import PartitionSpec as P


F32, BF16, I32 = jnp.float32, jnp.bfloat16, jnp.int32
CUBIC = (-0.0625, 0.0, 0.5625, 1.0, 0.5625, 0.0, -0.0625)
TAPS_AT = tuple((k - 3, w) for k, w in enumerate(CUBIC) if w != 0.0)

DEVICES = (4, 8, 8)
BX, BY, BZ = (32, 16, 8, 4, 2), (64, 32, 16, 8, 4), (128, 64, 32, 16, 8)
LOW = (0, -1, -2, -2, -2)
EX = (32, 19, 13, 9, 7)
EY = (64, 35, 21, 13, 9)
EZ = (128, 67, 37, 21, 13)
PY = (64, 40, 24, 16, 16)
OZ = (0, 0, 67, 104, 44)
FAR = (range(0, 3), range(3, 5))
V_COLUMNS = ((3, range(0, 5)), (3, range(5, 9)), (4, range(0, 7)))


def up16(n):
    return (n + 15) // 16 * 16


def iota(shape, dim):
    return lax.broadcasted_iota(I32, shape, dim)


def in_grid(level, ext, blocks, count, index, position):
    cell = index + LOW[level]
    g = cell + position * blocks[level]
    return (index >= 0) & (index < ext[level]) & (g >= 0) & (g < blocks[level] * count)


def cubic_matrix(level, ext, blocks, count, position, fine, coarse):
    offset = fine + LOW[level] - 2 * (coarse + LOW[level + 1])
    value = jnp.zeros(offset.shape, F32)
    for k, w in TAPS_AT:
        value = jnp.where(offset == k, w, value)
    ok = in_grid(level, ext, blocks, count, fine, position) & in_grid(level + 1, ext, blocks, count, coarse, position)
    return jnp.where(ok, value, 0.0)


def repeated(index, period):
    for _ in range(2):
        index = jnp.where(index >= period, index - period, index)
    return index


def restrict_y(level, position):
    half = up16(PY[level])
    shape = (PY[level + 1], 2 * half)
    return cubic_matrix(level, EY, BY, 8, position, repeated(iota(shape, 1), half), iota(shape, 0)).astype(BF16)


def prolong_y(level, position):
    half = up16(PY[level + 1])
    shape = (PY[level], 2 * half)
    return cubic_matrix(level, EY, BY, 8, position, iota(shape, 0), repeated(iota(shape, 1), half)).astype(BF16)


def restrict_z(level, position):
    shape = (128, 128)
    m = cubic_matrix(level, EZ, BZ, 8, position, iota(shape, 0) - OZ[level], iota(shape, 1) - OZ[level + 1]).astype(BF16)
    return jnp.concatenate([m, m], axis=0)


def split(v):
    hi = v.astype(BF16)
    return hi, (v - hi.astype(F32)).astype(BF16)


def dot(a, b, dims=(((1,), (0,)), ((), ()))):
    return lax.dot_general(a, b, dims, preferred_element_type=F32)


def stacked(value, *order):
    rows = up16(value.shape[0])
    if rows > value.shape[0]:
        value = jnp.concatenate([value, jnp.zeros((rows - value.shape[0], value.shape[1]), F32)], axis=0)
    parts = split(value)
    return jnp.concatenate([parts[k] for k in order], axis=0)


def dot_left_exact(m, b):
    return dot(m, stacked(b, 0, 1))


def dot_right_exact(a, m):
    return dot(jnp.concatenate(split(a), axis=1), m)


def dot3(a, b, dims=(((1,), (0,)), ((), ()))):
    return dot(a[0], b[0], dims) + (dot(a[0], b[1], dims) + dot(a[1], b[0], dims))


def x_mask(level, cell):
    i = lax.axis_index("gx")
    if cell < 0:
        return jnp.where(i * BX[level] + cell >= 0, 1.0, 0.0).astype(F32)
    if cell >= BX[level]:
        return jnp.where(i * BX[level] + cell < BX[level] * DEVICES[0], 1.0, 0.0).astype(F32)
    return None


def masked(value, mask):
    return value if mask is None else value * mask


def lanes_mask(first, count):
    lane = lax.broadcasted_iota(I32, (1, 128), 1)
    return (lane >= first) & (lane < first + count)


def restrict_x(level, slab):
    first, last = LOW[level], LOW[level] + EX[level]
    out = []
    for i in range(LOW[level + 1], LOW[level + 1] + EX[level + 1]):
        total = None
        for k, w in TAPS_AT:
            if first <= 2 * i + k < last:
                term = slab(2 * i + k)
                term = term if w == 1.0 else term * w
                total = term if total is None else total + term
        out.append(masked(total, x_mask(level + 1, i)))
    return out


def restrict_kernel(q_ref, s1f_ref, s1b_ref, s2_ref, v_ref, far):
    for s in range(8):
        s1b_ref[pl.ds(s * 64, 64), :] = q_ref[s]
        s1f_ref[pl.ds(s * 64, 64), :] = q_ref[s + 24]
    ix, iy, iz = lax.axis_index("gx"), lax.axis_index("gy"), lax.axis_index("gz")
    low = lanes_mask(0, EZ[1])
    slab = lambda i: q_ref[i]
    kept = {}
    for l in range(1, 5):
        planes = restrict_x(l - 1, slab)
        n, rows = EX[l], PY[l]
        wide = jnp.concatenate(planes, axis=1)
        wide = dot_left_exact(restrict_y(l - 1, iy), wide)
        tall = jnp.concatenate([wide[:, s * 128 : (s + 1) * 128] for s in range(n)], axis=0)
        tall = dot_right_exact(tall, restrict_z(l - 1, iz))
        planes = kept[l] = [tall[s * rows : (s + 1) * rows] for s in range(n)]
        slab = lambda i, planes=planes, low=LOW[l]: planes[i - low]
    for s in range(EX[2]):
        far[s] = kept[2][s]
    for s in range(11):
        for ref, at in ((s1b_ref, s), (s1f_ref, s + EX[1] - 11)):
            ref[pl.ds(512 + s * 40, 24), :] = jnp.where(low, kept[1][at][:24], kept[2][s])
            ref[pl.ds(512 + s * 40 + 24, 16), :] = kept[1][at][24:]
    for s in range(11, EX[2]):
        for ref in (s1b_ref, s1f_ref):
            ref[pl.ds(952 + (s - 11) * 24, 24), :] = kept[2][s]
    start = jnp.where(ix < 2, 8, 0)
    mask = lanes_mask(OZ[2], EZ[2])
    for k, members in enumerate(FAR):
        total = jnp.zeros((24, 128), F32)
        for n, s in enumerate(members):
            total = total + pltpu.roll(jnp.where(mask, far[start + s], 0.0), (n * EZ[2] - OZ[2]) % 128, 1)
        s2_ref[k] = total
    for c, (level, members) in enumerate(V_COLUMNS):
        mask = lanes_mask(OZ[level], EZ[level])
        total = jnp.zeros((16, 128), F32)
        for n, s in enumerate(members):
            value = jnp.where(mask, kept[level][s], 0.0)
            total = total + pltpu.roll(value, (n * EZ[level] - OZ[level]) % 128, 1)
        for d in range(8):
            v_ref[d, :, pl.ds(c * 128, 128)] = total


def conv_x(out_count, taps_ref, level, load, store):
    if len(taps_ref.shape) == 3:
        taps = [taps_ref[level, 0, t] for t in range(17)]
    else:
        taps = [taps_ref[pl.ds((level - 3) * 24 + t, 1), :] for t in range(17)]
    for i in range(out_count):
        total = load(i) * taps[0]
        for t in range(1, 17):
            total = total + load(i + t) * taps[t]
        store(i, total)


def x_kernel(taps_ref, q_ref, sf_ref, sb_ref, l_ref, r_ref, f_ref, y0_ref, o_ref, fw_ref, bw_ref, tb_ref, q1, q2):
    ix = lax.axis_index("gx")
    taps0 = [taps_ref[0, 0, t] for t in range(17)]

    def level0(j, _):
        rows = pl.ds(pl.multiple_of(j * 8, 8), 8)
        for first in (0, 16):
            acc = {}
            for p in range(first, first + 32):
                if p < 8:
                    v = l_ref[pl.ds(pl.multiple_of(p * 64 + j * 8, 8), 8), :]
                elif p < 40:
                    v = q_ref[p - 8, rows, :]
                else:
                    v = r_ref[pl.ds(pl.multiple_of((p - 40) * 64 + j * 8, 8), 8), :]
                for t in range(17):
                    i = p - t
                    if first <= i < first + 16:
                        term = v * taps0[t]
                        acc[i] = acc[i] + term if i in acc else term
            for i, value in acc.items():
                y0_ref[i, rows, :] = value
        return 0

    lax.fori_loop(0, 8, level0, 0)
    for i in range(32):
        bw_ref[pl.ds(i * 8, 8), :] = y0_ref[i, pl.ds(0, 8), :]
        fw_ref[pl.ds(i * 8, 8), :] = y0_ref[i, pl.ds(56, 8), :]

    def received(ref, at, rows):
        if not 0 <= at < (11 if rows == 40 else 13):
            return None
        return ref[pl.ds(512 + at * 40 if at < 11 else 952 + (at - 11) * 24, rows), :]

    def added(values):
        values = [v for v in values if v is not None]
        total = values[0]
        for v in values[1:]:
            total = total + v
        return total

    def own(at, rows):
        if rows == 24 or at < 11:
            return received(sb_ref, at, rows)
        return received(sf_ref, at - 8, rows)

    for r in range(35):
        cell = r - 9
        q1[r] = added([own(cell + 1, 40), received(l_ref, cell + 9, 40), received(r_ref, cell - 15, 40)])
    for r in range(29):
        cell = r - 10
        q2[r] = added([own(cell + 2, 24), received(l_ref, cell + 10, 24), received(r_ref, cell - 6, 24)])
    start = jnp.where(ix < 2, 24, 0)
    mask = lanes_mask(OZ[2], EZ[2])
    for k, members in enumerate(FAR):
        for n, s in enumerate(members):
            q2[start + s] += jnp.where(mask, pltpu.roll(f_ref[pl.ds(48 + k * 24, 24), :], (OZ[2] - n * EZ[2]) % 128, 1), 0.0)
    low = lanes_mask(0, EZ[1])
    two = {}

    def keep2(i, total):
        two[i] = masked(total, x_mask(2, LOW[2] + i))

    def keep1(s, total):
        total = masked(total, x_mask(1, LOW[1] + s))
        f, b = total[24:40], total[:16]
        o_ref[s, pl.ds(24, 16), :] = f
        o_ref[s, pl.ds(0, 24), :] = jnp.where(low, total[:24], two[s]) if s < EX[2] else total[:24]
        if s < EX[2]:
            f = jnp.where(low, f, two[s][8:])
            b = jnp.where(low, b, two[s][:16])
        fw_ref[pl.ds(256 + s * 16, 16), :] = f
        bw_ref[pl.ds(256 + s * 16, 16), :] = b

    for level in (3, 4):
        for t in range(17):
            tb_ref[pl.ds((level - 3) * 24 + t, 1), :] = jnp.full((1, 128), taps_ref[level, 0, t], F32)
    conv_x(EX[2], taps_ref, 2, lambda r: q2[r], keep2)
    conv_x(EX[1], taps_ref, 1, lambda r: q1[r], keep1)


def coarse_y_kernel(taps_ref, v_ref, s2_ref, near_ref, far_ref):
    iy = lax.axis_index("gy")
    block = stacked(jnp.concatenate([v_ref[k] for k in range(8)], axis=0), 0, 1, 0)
    for level, first, last in ((3, 0, 256), (4, 256, 384)):
        i, j = iota((16, 384), 0), iota((16, 384), 1) & 127
        to = out_cells(level, BY, EY, i, iy, 8)
        d, r = j >> 4, j & 15
        at = jnp.where(r < EY[level], (d - iy) * BY[level] + r + LOW[level], BAD)
        out = dot(thirds(toeplitz(taps_ref, level, 1, at - to + 8), 128), block[:, first:last])
        for c in range(first, last, 128):
            for ref in (near_ref, far_ref):
                ref[pl.ds(c // 8, 16), :] = out[:, c - first : c - first + 128]
    for k in range(2):
        far_ref[pl.ds(48 + k * 24, 24), :] = s2_ref[k]


def coarse_kernel(taps_ref, own_ref, low_ref, high_ref, far_ref, z3_ref, z4_ref, t4_ref, g3, g4):
    ix = lax.axis_index("gx")
    for g in (g3, g4):
        g[...] = jnp.zeros_like(g)
    for ref, step in ((own_ref, 0), (low_ref, 3), (high_ref, 1), (far_ref, 2)):
        source = (ix + step) & 3
        for c, (level, members) in enumerate(V_COLUMNS):
            g = g3 if level == 3 else g4
            column = ref[pl.ds(c * 16, 16), :]
            for n, s in enumerate(members):
                g[source * BX[level] + (LOW[level] + s + 10)] += pltpu.roll(column, (OZ[level] - n * EZ[level]) % 128, 1)
    for level, g, z_ref in ((3, g3, z3_ref), (4, g4, z4_ref)):
        start = ix * BX[level] + 10 + LOW[level] - 8

        def keep(i, total, level=level, z_ref=z_ref):
            z_ref[pl.ds(i * 16, 16), :] = masked(total, x_mask(level, LOW[level] + i))

        conv_x(EX[level], taps_ref, level, lambda r, g=g, start=start: g[start + r], keep)
    t4_ref[...] = level4_rows(z4_ref)


BAD = 1000


def out_cells(level, blocks, ext, index, position, count):
    return jnp.where(in_grid(level, ext, blocks, count, index, position), index + LOW[level], -BAD)


def thirds(value, third):
    hi, lo = split(value)
    return jnp.where(iota(value.shape, 1) < 2 * third, hi.astype(F32), lo.astype(F32)).astype(BF16)


def toeplitz(taps_ref, level, axis, diff):
    total = jnp.zeros(diff.shape, F32)
    for t in range(17):
        total = jnp.where(diff == t, taps_ref[level, axis, t], total)
    return total


def store_z(ref, halo_ref, own, halo):
    ref[...] = jnp.concatenate(split(own), axis=1)
    hi, lo = split(halo)
    halo_ref[...] = jnp.concatenate([hi, hi, lo], axis=0)


def prep_kernel(taps_ref, *out):
    iy = lax.axis_index("gy")
    iz = lax.axis_index("gz")
    outs = out[:3]
    z_outs = [out[3 + 2 * k : 5 + 2 * k] for k in range(5)]

    for level, width, ref in ((0, 80, outs[0]), (1, 80, outs[1]), (2, 64, outs[2])):
        shape = (PY[level], 3 * width)
        i, j = iota(shape, 0), repeated(iota(shape, 1), width)
        to = out_cells(level, BY, EY, i, iy, 8)
        if level == 0:
            at = j - 8
        else:
            halo, reach = 16, 11 if level == 1 else 13
            own = j - halo
            upper = own - PY[level]
            lowest = LOW[level] - 8
            at = jnp.where(
                own < 0,
                jnp.where(j < reach, j + lowest, BAD),
                jnp.where(
                    upper < 0,
                    jnp.where(own < EY[level], own + LOW[level], BAD),
                    jnp.where(upper < reach, upper + LOW[level] + BY[level], BAD),
                ),
            )
        ref[...] = thirds(toeplitz(taps_ref, level, 1, at - to + 8), width)
    j = iota((128, 128), 0)
    c = iota((128, 128), 1)
    own = toeplitz(taps_ref, 0, 2, j - c + 8)
    j, c = iota((16, 128), 0), iota((16, 128), 1)
    store_z(*z_outs[0], own, toeplitz(taps_ref, 0, 2, jnp.where(j < 8, j - 8, j - 8 + 128) - c + 8))
    for level in range(4):
        out[13 + level][...] = prolong_y(level, iy)
    prolong = None
    for level in range(1, 5):
        shape = (128, 128)
        one = cubic_matrix(level - 1, EZ, BZ, 8, iz, iota(shape, 1), iota(shape, 0)).astype(BF16)
        whole = one.astype(F32) if prolong is None else dot(one, prolong[0]) + dot(one, prolong[1])
        prolong = split(whole)
        c = iota((128, 128), 1)
        to = out_cells(level, BZ, EZ, c, iz, 8)
        j = iota((128, 128), 0) - OZ[level]
        at = jnp.where((j >= 0) & (j < EZ[level]), j + LOW[level], BAD)
        own = dot3(split(toeplitz(taps_ref, level, 2, at - to + 8)), prolong)
        rows = 64 if level == 4 else 32
        c = iota((rows, 128), 1)
        to = out_cells(level, BZ, EZ, c, iz, 8)
        j = iota((rows, 128), 0)
        r = j & 15
        if level == 4:
            d = j >> 4
            shift = jnp.where(d == 0, -2, jnp.where(d == 1, -1, jnp.where(d == 2, 1, 2))) * BZ[4]
            at = jnp.where(r < EZ[4], shift + r + LOW[4], BAD)
        else:
            reach = 11 if level == 1 else 13
            at = jnp.where(j < 16, r + LOW[level] - 8, r + LOW[level] + BZ[level])
            at = jnp.where(r < reach, at, BAD)
        store_z(*z_outs[level], own, dot3(split(toeplitz(taps_ref, level, 2, at - to + 8)), prolong))


def level4_rows(z4_ref):
    block = pltpu.roll(z4_ref[...], (-OZ[4]) % 128, 1)
    return jnp.concatenate([block, jnp.zeros((16, 128), F32)], axis=0).T[:16]


def y_kernel(y0_ref, o_ref, lo_ref, hi_ref, z3_ref, z4_ref, *refs):
    my = [ref[...] for ref in refs[:3]]
    z0_ref, z1_ref, z2_ref, fw_ref, bw_ref = refs[3:]
    for base in range(0, 32, 4):
        parts = []
        for i in range(base, base + 4):
            parts.append(jnp.concatenate(
                [lo_ref[pl.ds(i * 8, 8), :], y0_ref[i], hi_ref[pl.ds(i * 8, 8), :]], axis=0))
        out = dot(my[0], stacked(jnp.concatenate(parts, axis=1), 0, 1, 0))
        for n in range(4):
            z0_ref[pl.ds((base + n) * 64, 64), :] = out[:, n * 128 : (n + 1) * 128]
    for level, z_ref in ((1, z1_ref), (2, z2_ref)):
        n, rows = EX[level], PY[level]
        parts = [jnp.concatenate([lo_ref[pl.ds(256 + s * 16, 16), :], o_ref[s, pl.ds(0, rows), :], hi_ref[pl.ds(256 + s * 16, 16), :]], axis=0)
                 for s in range(n)]
        out = dot(my[level], stacked(jnp.concatenate(parts, axis=1), 0, 1, 0))
        for s in range(n):
            z_ref[pl.ds(s * rows, rows), :] = out[:, s * 128 : (s + 1) * 128]
    for k in range(16):
        t = z0_ref[pl.ds(k * 128, 128), :].T
        bw_ref[pl.ds(0, 8), pl.ds(k * 128, 128)] = t[:8]
        fw_ref[pl.ds(0, 8), pl.ds(k * 128, 128)] = t[120:]
    for k in range(6):
        size = 128 if k < 5 else 120
        block = z1_ref[pl.ds(k * 128, size), :]
        if size < 128:
            block = jnp.concatenate([block, jnp.zeros((128 - size, 128), F32)], axis=0)
        t = block.T
        bw_ref[pl.ds(8, 16), pl.ds(k * 128, 128)] = t[0:16]
        fw_ref[pl.ds(8, 16), pl.ds(k * 128, 128)] = t[56:72]
    for level, z_ref, at, f, count in ((2, z2_ref, 768, 24, 312), (3, z3_ref, 1152, 8, 144)):
        for k in range((count + 127) // 128):
            size = min(128, count - k * 128)
            block = pltpu.roll(z_ref[pl.ds(k * 128, size), :], (-OZ[level]) % 128, 1)
            if size < 128:
                block = jnp.concatenate([block, jnp.zeros((128 - size, 128), F32)], axis=0)
            t = block.T
            bw_ref[pl.ds(8, 16), pl.ds(at + k * 128, 128)] = t[0:16]
            fw_ref[pl.ds(8, 16), pl.ds(at + k * 128, 128)] = t[f : f + 16]
    t = level4_rows(z4_ref)
    for ref in (bw_ref, fw_ref):
        ref[pl.ds(8, 16), pl.ds(1408, 128)] = t


Z_AT = {0: 0, 1: 0, 2: 768, 3: 1152, 4: 1408}
Z_ROWS = {0: 2048, 1: 760, 2: 312, 3: 144, 4: 112}


def own_kernel(*refs):
    for level in range(5):
        z_ref, m_ref, t_ref = refs[level], refs[5 + level], refs[10 + level]
        m = m_ref[...]
        m = jnp.concatenate([m, jnp.concatenate([m[:, :128], jnp.zeros((128, 128), BF16)], axis=1)], axis=0)
        step = 512 if level == 0 else Z_ROWS[level]
        for k in range(0, Z_ROWS[level], step):
            both = dot(jnp.concatenate(split(z_ref[pl.ds(k, step), :]), axis=1), m)
            t_ref[pl.ds(k, step), :] = both[:, :128] + both[:, 128:]


def z_kernel(*refs):
    t_refs, (lo_ref, hi_ref, l4_ref, h4_ref), m_refs, py = refs[:5], refs[5:9], refs[9:14], refs[14:18]
    out_ref, acc = refs[18:]
    first = (((0,), (0,)), ((), ()))

    def halo_part(level, halo):
        return dot(stacked(halo, 0, 1, 0), m_refs[level][...], first)

    total = None
    for level in (4, 3, 2, 1):
        n = Z_ROWS[level]
        columns = pl.ds(Z_AT[level], (n + 127) // 128 * 128)
        halo = [lo_ref[pl.ds(8, 16), columns], hi_ref[pl.ds(8, 16), columns]]
        if level == 4:
            halo = [l4_ref[...], *halo, h4_ref[...]]
        term = t_refs[level][...] + halo_part(level, jnp.concatenate(halo, axis=0))[:n]
        planes = [term[s * PY[level] : (s + 1) * PY[level]] for s in range(EX[level])]
        if total is not None:
            planes = [a + b for a, b in zip(planes, total)]
        fine = level - 1
        wide = dot_left_exact(py[fine][...], jnp.concatenate(planes, axis=1))
        coarse = [wide[:, s * 128 : (s + 1) * 128] for s in range(EX[level])]
        total = []
        for cell in range(LOW[fine], LOW[fine] + EX[fine]):
            value = None
            for k, w in TAPS_AT:
                if (cell - k) % 2 == 0:
                    s = (cell - k) // 2 - LOW[level]
                    if 0 <= s < EX[level]:
                        part = coarse[s] if w == 1.0 else coarse[s] * w
                        value = part if value is None else value + part
            value = masked(value, x_mask(fine, cell)) if fine else value
            total.append(value)
            if fine == 0:
                acc[cell] = value
    halo = jnp.concatenate([lo_ref[pl.ds(0, 8), :], hi_ref[pl.ds(0, 8), :]], axis=0)
    for k in range(4):
        term = halo_part(0, halo[:, k * 512 : (k + 1) * 512])
        for i in range(8):
            s = k * 8 + i
            out_ref[s] = acc[s] + (t_refs[0][pl.ds(s * 64, 64), :] + term[i * 64 : (i + 1) * 64])


VMEM_LIMIT = 24 * 2**20
VM = pl.BlockSpec(memory_space=pltpu.VMEM)
SM = pl.BlockSpec(memory_space=pltpu.SMEM)


def call(body, shapes, in_specs, scratch=(), flops=4 * 10**8):
    return pl.pallas_call(
        body,
        out_shape=[jax.ShapeDtypeStruct(s, d) for s, d in shapes],
        in_specs=in_specs,
        out_specs=[VM] * len(shapes),
        scratch_shapes=list(scratch),
        compiler_params=pltpu.CompilerParams(vmem_limit_bytes=VMEM_LIMIT),
        cost_estimate=pl.CostEstimate(flops=flops, bytes_accessed=2**21, transcendentals=0),
    )


def steps(axis, by):
    count = lax.axis_size(axis)
    return [(i, i + by) for i in range(count) if 0 <= i + by < count]


def per_device(charges, kernel_taps):
    taps = kernel_taps

    def shift(v, axis, by):
        return lax.ppermute(v, axis, steps(axis, by))

    s1f, s1b, s2, v = call(
        restrict_kernel,
        [((1000, 128), F32), ((1000, 128), F32), ((2, 24, 128), F32),
         ((8, 16, 384), F32)],
        [VM], [pltpu.VMEM((13, 24, 128), F32)],
    )(charges)
    l1 = shift(s1f, "gx", 1)
    r1 = shift(s1b, "gx", -1)
    vs = lax.all_to_all(v, "gy", 0, 0)
    near, far = call(coarse_y_kernel, [((48, 128), F32), ((96, 128), F32)], [SM] + [VM] * 2)(taps, vs, s2)
    low = lax.ppermute(near, "gx", [(i, (i + 1) % 4) for i in range(4)])
    high = lax.ppermute(near, "gx", [(i, (i + 3) % 4) for i in range(4)])
    far = lax.ppermute(far, "gx", [(i, (i + 2) % 4) for i in range(4)])
    mats_shapes = [(64, 240), (40, 240), (24, 192)]
    for halo in (16, 32, 32, 32, 64):
        mats_shapes += [(128, 256), (3 * halo, 128)]
    mats_shapes += [(PY[l], 2 * up16(PY[l + 1])) for l in range(4)]
    mats = call(prep_kernel, [(w, BF16) for w in mats_shapes], [SM])(taps)
    my, own, halo, py = mats[:3], mats[3:13:2], mats[4:13:2], mats[13:]
    y0, o, fw, bw, tb = call(
        x_kernel,
        [((32, 64, 128), F32), ((19, 40, 128), F32), ((560, 128), F32), ((560, 128), F32), ((48, 128), F32)],
        [SM] + [VM] * 6,
        [pltpu.VMEM((35, 40, 128), F32), pltpu.VMEM((29, 24, 128), F32)],
    )(taps, charges, s1f, s1b, l1, r1, far)
    lo = shift(fw, "gy", 1)
    hi = shift(bw, "gy", -1)
    z3, z4, t4 = call(
        coarse_kernel, [((144, 128), F32), ((112, 128), F32), ((16, 128), F32)], [VM] * 5,
        [pltpu.VMEM((37, 16, 128), F32), pltpu.VMEM((29, 16, 128), F32)],
    )(tb, near, low, high, far)
    l4 = shift(t4, "gz", 2)
    h4 = shift(t4, "gz", -2)
    z0, z1, z2, fw, bw = call(
        y_kernel, [((Z_ROWS[l], 128), F32) for l in range(3)] + [((24, 2048), F32), ((24, 2048), F32)], [VM] * 9
    )(y0, o, lo, hi, z3, z4, *my[:3])
    z = (z0, z1, z2, z3, z4)
    lo = shift(fw, "gz", 1)
    hi = shift(bw, "gz", -1)
    terms = call(own_kernel, [((Z_ROWS[l], 128), F32) for l in range(5)], [VM] * 10)(*z, *own)
    (out,) = call(
        z_kernel, [((32, 64, 128), F32)], [VM] * 18, [pltpu.VMEM((32, 64, 128), F32)]
    )(*terms, lo, hi, l4, h4, *halo, *py)
    return out


def solution(mesh):
    return jax.shard_map(
        per_device,
        mesh=mesh,
        in_specs=(P("gx", "gy", "gz"), P()),
        out_specs=P("gx", "gy", "gz"),
        check_vma=False,
    )
```

time: 80.7 us -> 63.9 us (0.79)
  the two profiles are of different devices: /device:TPU:216 before, /device:TPU:224 now
where the time goes in v2:
time: 63.9 us; the launch traced here: 63.5 us
  starting transfers between devices  32.8 us (51%)
  blocking collectives  11.2 us (18%)
  Pallas kernels  10.9 us (17%)
  waiting for transfers between devices  7.23 us (11%)
  local copies, waits for them, and re-layouts  1.23 us (2%)
    ppermute x8, starting transfers between devices, shift(): return lax.ppermute(v, axis, steps(axis, by))  25.1 us
    all_to_all x1, blocking collectives, per_device(): vs = lax.all_to_all(v, 'gy', 0, 0)  11.2 us
    ppermute x8, waiting for transfers between devices, shift(): return lax.ppermute(v, axis, steps(axis, by))  4.49 us
    ppermute x1, starting transfers between devices, per_device(): far = lax.ppermute(far, 'gx', [(i, (i + 2) % 4) for i in range(4)])  4.16 us
    pallas_call x1, Pallas kernels, per_device(): call(x_kernel, [((32, 64, 128), F32), ((19, 40, 128), F32), ((560, 128),...  2.66 us
    pallas_call x1, Pallas kernels, per_device(): call(z_kernel, [((32, 64, 128), F32)], [VM] * 18, [pltpu.VMEM((32, 64, 12...  2.1 us
    ppermute x1, starting transfers between devices, per_device(): low = lax.ppermute(near, 'gx', [(i, (i + 1) % 4) for i in range(4)])  2.09 us
    ppermute x1, waiting for transfers between devices, per_device(): far = lax.ppermute(far, 'gx', [(i, (i + 2) % 4) for i in range(4)])  2.07 us
  transfers between devices with their start and end apart: 11, of which 3 were waited for; matrix products, arithmetic and copies ran while one was open for 0% of the time, Pallas kernels for 6%

profile of v2, /device:TPU:224, one launch (start us, length us, event | category | flops | bytes accessed | tf_op | source)
XLA Modules:
  0.0 63.5 jit_solution(7953739394559831031)
XLA Ops:
  0.0 1.2 %copy-done = f32[32,64,128]{2,1,0:T(8,128)S(1)} copy-done((f32[32,64,128]{2,1,0:T(8,128)S(1)}, f32[32,64,128]{2,1,0:T(8,128)}, u32[]{:S(2)}) %copy-start) | copy-done | bytes 1048600
  1.2 1.5 %shard_map.28 = (f32[1000,128]{1,0:T(8,128)S(1)}, f32[1000,128]{1,0:T(8,128)S(1)}, f32[2,24,128]{2,1,0:T(8,128)S(1)}, f32[8,16,384]{2,1,0:T(8,128)S(1)}) custom-call(f32[32,64,128]{2,1,0:T(8,128)S(1)} %copy-done), custom_call_target="tpu_custom_call" | custom-call | flops 400000000 | bytes 2097152 | tf_op jit(solution)/shard_map/pallas_call | solution.py:527
  2.7 3.6 %collective-permute-start = (f32[1000,128]{1,0:T(8,128)S(1)}, f32[1000,128]{1,0:T(8,128)S(1)}, u32[]{:S(2)}, u32[]{:S(2)}) collective-permute-start(f32[1000,128]{1,0:T(8,128)S(1)} %get-tuple-element.46.sf_ref), channel_id=1, source_target_pairs={{0,64},{64,128},{128,192},{1,65},{65,129},{129,193},{2,66},{66,130... | collective-permute-start | bytes 1536008 | tf_op jit(solution)/shard_map/ppermute | solution.py:525
  6.3 1.3 %collective-permute-start.1 = (f32[1000,128]{1,0:T(8,128)S(1)}, f32[1000,128]{1,0:T(8,128)S(1)}, u32[]{:S(2)}, u32[]{:S(2)}) collective-permute-start(f32[1000,128]{1,0:T(8,128)S(1)} %get-tuple-element.47.sb_ref), channel_id=1, source_target_pairs={{64,0},{128,64},{192,128},{65,1},{129,65},{193,129},{66,2},{130,66... | collective-permute-start | bytes 1536008 | tf_op jit(solution)/shard_map/ppermute | solution.py:525
  7.6 11.2 %all_to_all.5.v_ref = f32[8,16,384]{2,1,0:T(8,128)S(1)} all-to-all(f32[8,16,384]{2,1,0:T(8,128)S(1)} %get-tuple-element.48), channel_id=1, replica_groups=mesh['gx'=4,'gy'=8,'gz'=8] {'gy'}, dimensions={0} | all-to-all | bytes 393216 | tf_op jit(solution)/shard_map/all_to_all | solution.py:535
  18.8 0.9 %shard_map.29 = (f32[48,128]{1,0:T(8,128)S(1)}, f32[96,128]{1,0:T(8,128)S(1)}) custom-call(f32[5,3,17]{2,1,0:T(4,128)S(1)} %copy-done.2, f32[8,16,384]{2,1,0:T(8,128)S(1)} %all_to_all.5.v_ref, f32[2,24,128]{2,1,0:T(8,128)S(1)} %get-tuple-element.49.s2_ref), custom_call_target="tpu_custom_call" | custom-call | flops 400000000 | bytes 2097152 | tf_op jit(solution)/shard_map/pallas_call | solution.py:536
  19.7 4.2 %collective-permute-start.2 = (f32[96,128]{1,0:T(8,128)S(1)}, f32[96,128]{1,0:T(8,128)S(1)}, u32[]{:S(2)}, u32[]{:S(2)}) collective-permute-start(f32[96,128]{1,0:T(8,128)S(1)} %get-tuple-element.50), channel_id=1, source_target_pairs={{0,128},{64,192},{128,0},{192,64},{1,129},{65,193},{129,1},{193,65... | collective-permute-start | bytes 147464 | tf_op jit(solution)/shard_map/ppermute | solution.py:539
  23.9 2.1 %collective-permute-done.2.f_ref.far_ref = f32[96,128]{1,0:T(8,128)S(1)} collective-permute-done((f32[96,128]{1,0:T(8,128)S(1)}, f32[96,128]{1,0:T(8,128)S(1)}, u32[]{:S(2)}, u32[]{:S(2)}) %collective-permute-start.2) | collective-permute-done | bytes 49184 | tf_op jit(solution)/shard_map/ppermute | solution.py:539
  26.0 2.7 %shard_map.30 = (f32[32,64,128]{2,1,0:T(8,128)S(1)}, f32[19,40,128]{2,1,0:T(8,128)S(1)}, f32[560,128]{1,0:T(8,128)S(1)}, f32[560,128]{1,0:T(8,128)S(1)}, f32[48,128]{1,0:T(8,128)S(1)}) custom-call(f32[5,3,17]{2,1,0:T(4,128)S(1)} %copy-done.2, f32[32,64,128]{2,1,0:T(8,128)S(1)} %copy-done.1, f32[1000,128]{1,0:T(8,128)S(1)} %get-tuple-element.46.sf_ref, ...), custom_call_target="tpu_custom_call" | custom-call | flops 400000000 | bytes 2097152 | tf_op jit(solution)/shard_map/pallas_call | solution.py:546
  28.6 2.7 %collective-permute-start.3 = (f32[560,128]{1,0:T(8,128)S(1)}, f32[560,128]{1,0:T(8,128)S(1)}, u32[]{:S(2)}, u32[]{:S(2)}) collective-permute-start(f32[560,128]{1,0:T(8,128)S(1)} %get-tuple-element.53), channel_id=1, source_target_pairs={{0,8},{8,16},{16,24},{24,32},{32,40},{40,48},{48,56},{1,9},{9,17},... | collective-permute-start | bytes 860168 | tf_op jit(solution)/shard_map/ppermute | solution.py:525
  31.4 5.2 %collective-permute-start.4 = (f32[560,128]{1,0:T(8,128)S(1)}, f32[560,128]{1,0:T(8,128)S(1)}, u32[]{:S(2)}, u32[]{:S(2)}) collective-permute-start(f32[560,128]{1,0:T(8,128)S(1)} %get-tuple-element.54), channel_id=1, source_target_pairs={{8,0},{16,8},{24,16},{32,24},{40,32},{48,40},{56,48},{9,1},{17,9},... | collective-permute-start | bytes 860168 | tf_op jit(solution)/shard_map/ppermute | solution.py:525
  36.6 2.1 %collective-permute-start.5 = (f32[48,128]{1,0:T(8,128)S(1)}, f32[48,128]{1,0:T(8,128)S(1)}, u32[]{:S(2)}, u32[]{:S(2)}) collective-permute-start(f32[48,128]{1,0:T(8,128)S(1)} %get-tuple-element.56.own_ref), channel_id=1, source_target_pairs={{0,64},{64,128},{128,192},{192,0},{1,65},{65,129},{129,193},{193,1... | collective-permute-start | bytes 73736 | tf_op jit(solution)/shard_map/ppermute | solution.py:537
  38.7 1.4 %collective-permute-start.6 = (f32[48,128]{1,0:T(8,128)S(1)}, f32[48,128]{1,0:T(8,128)S(1)}, u32[]{:S(2)}, u32[]{:S(2)}) collective-permute-start(f32[48,128]{1,0:T(8,128)S(1)} %get-tuple-element.56.own_ref), channel_id=1, source_target_pairs={{0,192},{64,0},{128,64},{192,128},{1,193},{65,1},{129,65},{193,129... | collective-permute-start | bytes 73736 | tf_op jit(solution)/shard_map/ppermute | solution.py:538
  40.1 1.8 %shard_map.32 = (bf16[64,240]{1,0:T(8,128)(2,1)S(1)}, bf16[40,240]{1,0:T(8,128)(2,1)S(1)}, bf16[24,192]{1,0:T(8,128)(2,1)S(1)}, bf16[128,256]{1,0:T(8,128)(2,1)S...) custom-call(f32[5,3,17]{2,1,0:T(4,128)S(1)} %copy-done.2), custom_call_target="tpu_custom_call" | custom-call | flops 400000000 | bytes 2097152 | tf_op jit(solution)/shard_map/pallas_call | solution.py:544
  41.9 0.7 %collective-permute-done.6.high_ref = f32[48,128]{1,0:T(8,128)S(1)} collective-permute-done((f32[48,128]{1,0:T(8,128)S(1)}, f32[48,128]{1,0:T(8,128)S(1)}, u32[]{:S(2)}, u32[]{:S(2)}) %collective-permute-start.6) | collective-permute-done | bytes 24608 | tf_op jit(solution)/shard_map/ppermute | solution.py:538
  42.5 0.4 shard_map.31
  42.9 1.0 %shard_map.33 = (f32[2048,128]{1,0:T(8,128)S(1)}, f32[760,128]{1,0:T(8,128)S(1)}, f32[312,128]{1,0:T(8,128)S(1)}, f32[24,2048]{1,0:T(8,128)S(1)}, f32[24,2048]{1,0:T(8,128)S(1)}) custom-call(f32[32,64,128]{2,1,0:T(8,128)S(1)} %get-tuple-element.51.y0_ref, f32[19,40,128]{2,1,0:T(8,128)S(1)} %get-tuple-element.52.o_ref, ...), custom_call_target="tpu_custom_call" | custom-call | flops 400000000 | bytes 2097152 | tf_op jit(solution)/shard_map/pallas_call | solution.py:560
  43.9 1.9 %collective-permute-start.7 = (f32[24,2048]{1,0:T(8,128)S(1)}, f32[24,2048]{1,0:T(8,128)S(1)}, u32[]{:S(2)}, u32[]{:S(2)}) collective-permute-start(f32[24,2048]{1,0:T(8,128)S(1)} %get-tuple-element.75), channel_id=1, source_target_pairs={{0,1},{1,2},{2,3},{3,4},{4,5},{5,6},{6,7},{8,9},{9,10},{10,11},{11... | collective-permute-start | bytes 589832 | tf_op jit(solution)/shard_map/ppermute | solution.py:525
  45.8 4.5 %collective-permute-start.8 = (f32[24,2048]{1,0:T(8,128)S(1)}, f32[24,2048]{1,0:T(8,128)S(1)}, u32[]{:S(2)}, u32[]{:S(2)}) collective-permute-start(f32[24,2048]{1,0:T(8,128)S(1)} %get-tuple-element.76), channel_id=1, source_target_pairs={{1,0},{2,1},{3,2},{4,3},{5,4},{6,5},{7,6},{9,8},{10,9},{11,10},{12... | collective-permute-start | bytes 589832 | tf_op jit(solution)/shard_map/ppermute | solution.py:525
  50.4 4.6 %collective-permute-start.10 = (f32[16,128]{1,0:T(8,128)S(1)}, f32[16,128]{1,0:T(8,128)S(1)}, u32[]{:S(2)}, u32[]{:S(2)}) collective-permute-start(f32[16,128]{1,0:T(8,128)S(1)} %get-tuple-element.77), channel_id=1, source_target_pairs={{2,0},{3,1},{4,2},{5,3},{6,4},{7,5},{10,8},{11,9},{12,10},{13,11},... | collective-permute-start | bytes 24584 | tf_op jit(solution)/shard_map/ppermute | solution.py:525
  55.0 1.3 %collective-permute-start.9 = (f32[16,128]{1,0:T(8,128)S(1)}, f32[16,128]{1,0:T(8,128)S(1)}, u32[]{:S(2)}, u32[]{:S(2)}) collective-permute-start(f32[16,128]{1,0:T(8,128)S(1)} %get-tuple-element.77), channel_id=1, source_target_pairs={{0,2},{1,3},{2,4},{3,5},{4,6},{5,7},{8,10},{9,11},{10,12},{11,13},... | collective-permute-start | bytes 24584 | tf_op jit(solution)/shard_map/ppermute | solution.py:525
  56.3 0.7 %shard_map.34 = (f32[2048,128]{1,0:T(8,128)S(1)}, f32[760,128]{1,0:T(8,128)S(1)}, f32[312,128]{1,0:T(8,128)S(1)}, f32[144,128]{1,0:T(8,128)S(1)}, f32[112,128]{1,0:T(8,128)S(1)}) custom-call(f32[2048,128]{1,0:T(8,128)S(1)} %get-tuple-element.62.refs_0_, f32[760,128]{1,0:T(8,128)S(1)} %get-tuple-element.63.refs_1_, f32[312,128]{1,0:T(8,128)S(1)} %get-tuple-element.64.refs_2_, ...), custom_call_target="tpu_custom_call" | custom-call | flops 400000000 | bytes 2097152 | tf_op jit(solution)/shard_map/pallas_call | solution.py:566
  56.9 4.5 %collective-permute-done.9.refs_7_ = f32[16,128]{1,0:T(8,128)S(1)} collective-permute-done((f32[16,128]{1,0:T(8,128)S(1)}, f32[16,128]{1,0:T(8,128)S(1)}, u32[]{:S(2)}, u32[]{:S(2)}) %collective-permute-start.9) | collective-permute-done | bytes 8224 | tf_op jit(solution)/shard_map/ppermute | solution.py:525
  61.4 2.1 %shard_map.35 = f32[32,64,128]{2,1,0:T(8,128)} custom-call(f32[2048,128]{1,0:T(8,128)S(1)} %get-tuple-element.70.refs_0_, f32[760,128]{1,0:T(8,128)S(1)} %get-tuple-element.71.refs_1_, f32[312,128]{1,0:T(8,128)S(1)} %get-tuple-element.72.refs_2_, f32[144,128]{1,0:T(8,128)S(1)} %get-tuple-element.73.refs_3_, f32[112,128]{1,0:T(8,128)S(1)} %get-tuple-element.74.refs_4_, ...), custom_call_target="tpu_custom_call" | custom-call | flops 400000000 | bytes 2097152 | tf_op jit(solution)/shard_map/pallas_call | solution.py:567
  (13 shorter events, 0.0 us)
Async XLA Ops:
  0.0 1.2 %copy-start = (f32[32,64,128]{2,1,0:T(8,128)S(1)}, f32[32,64,128]{2,1,0:T(8,128)}, u32[]{:S(2)}) copy-start(f32[32,64,128]{2,1,0:T(8,128)} %q_ref.3) | copy-start | bytes 3145732
  1.2 17.6 %copy-start.2 = (f32[5,3,17]{2,1,0:T(4,128)S(1)}, f32[5,3,17]{2,1,0:T(4,128)}, u32[]{:S(2)}) copy-start(f32[5,3,17]{2,1,0:T(4,128)} %taps_ref.5) | copy-start | bytes 3064
  2.7 23.3 %copy-start.1 = (f32[32,64,128]{2,1,0:T(8,128)S(1)}, f32[32,64,128]{2,1,0:T(8,128)}, u32[]{:S(2)}) copy-start(f32[32,64,128]{2,1,0:T(8,128)} %q_ref.3) | copy-start | bytes 3145732
  2.7 23.2 %collective-permute-start = (f32[1000,128]{1,0:T(8,128)S(1)}, f32[1000,128]{1,0:T(8,128)S(1)}, u32[]{:S(2)}, u32[]{:S(2)}) collective-permute-start(f32[1000,128]{1,0:T(8,128)S(1)} %get-tuple-element.46.sf_ref), channel_id=1, source_target_pairs={{0,64},{64,128},{128,192},{1,65},{65,129},{129,193},{2,66},{66,130... | collective-permute-start | bytes 1536008 | tf_op jit(solution)/shard_map/ppermute | solution.py:525
  6.3 19.7 %collective-permute-start.1 = (f32[1000,128]{1,0:T(8,128)S(1)}, f32[1000,128]{1,0:T(8,128)S(1)}, u32[]{:S(2)}, u32[]{:S(2)}) collective-permute-start(f32[1000,128]{1,0:T(8,128)S(1)} %get-tuple-element.47.sb_ref), channel_id=1, source_target_pairs={{64,0},{128,64},{192,128},{65,1},{129,65},{193,129},{66,2},{130,66... | collective-permute-start | bytes 1536008 | tf_op jit(solution)/shard_map/ppermute | solution.py:525
  19.7 6.2 %collective-permute-start.2 = (f32[96,128]{1,0:T(8,128)S(1)}, f32[96,128]{1,0:T(8,128)S(1)}, u32[]{:S(2)}, u32[]{:S(2)}) collective-permute-start(f32[96,128]{1,0:T(8,128)S(1)} %get-tuple-element.50), channel_id=1, source_target_pairs={{0,128},{64,192},{128,0},{192,64},{1,129},{65,193},{129,1},{193,65... | collective-permute-start | bytes 147464 | tf_op jit(solution)/shard_map/ppermute | solution.py:539
  28.6 14.3 %collective-permute-start.3 = (f32[560,128]{1,0:T(8,128)S(1)}, f32[560,128]{1,0:T(8,128)S(1)}, u32[]{:S(2)}, u32[]{:S(2)}) collective-permute-start(f32[560,128]{1,0:T(8,128)S(1)} %get-tuple-element.53), channel_id=1, source_target_pairs={{0,8},{8,16},{16,24},{24,32},{32,40},{40,48},{48,56},{1,9},{9,17},... | collective-permute-start | bytes 860168 | tf_op jit(solution)/shard_map/ppermute | solution.py:525
  31.4 11.5 %collective-permute-start.4 = (f32[560,128]{1,0:T(8,128)S(1)}, f32[560,128]{1,0:T(8,128)S(1)}, u32[]{:S(2)}, u32[]{:S(2)}) collective-permute-start(f32[560,128]{1,0:T(8,128)S(1)} %get-tuple-element.54), channel_id=1, source_target_pairs={{8,0},{16,8},{24,16},{32,24},{40,32},{48,40},{56,48},{9,1},{17,9},... | collective-permute-start | bytes 860168 | tf_op jit(solution)/shard_map/ppermute | solution.py:525
  36.6 5.2 %collective-permute-start.5 = (f32[48,128]{1,0:T(8,128)S(1)}, f32[48,128]{1,0:T(8,128)S(1)}, u32[]{:S(2)}, u32[]{:S(2)}) collective-permute-start(f32[48,128]{1,0:T(8,128)S(1)} %get-tuple-element.56.own_ref), channel_id=1, source_target_pairs={{0,64},{64,128},{128,192},{192,0},{1,65},{65,129},{129,193},{193,1... | collective-permute-start | bytes 73736 | tf_op jit(solution)/shard_map/ppermute | solution.py:537
  38.7 3.8 %collective-permute-start.6 = (f32[48,128]{1,0:T(8,128)S(1)}, f32[48,128]{1,0:T(8,128)S(1)}, u32[]{:S(2)}, u32[]{:S(2)}) collective-permute-start(f32[48,128]{1,0:T(8,128)S(1)} %get-tuple-element.56.own_ref), channel_id=1, source_target_pairs={{0,192},{64,0},{128,64},{192,128},{1,193},{65,1},{129,65},{193,129... | collective-permute-start | bytes 73736 | tf_op jit(solution)/shard_map/ppermute | solution.py:538
  43.9 17.5 %collective-permute-start.7 = (f32[24,2048]{1,0:T(8,128)S(1)}, f32[24,2048]{1,0:T(8,128)S(1)}, u32[]{:S(2)}, u32[]{:S(2)}) collective-permute-start(f32[24,2048]{1,0:T(8,128)S(1)} %get-tuple-element.75), channel_id=1, source_target_pairs={{0,1},{1,2},{2,3},{3,4},{4,5},{5,6},{6,7},{8,9},{9,10},{10,11},{11... | collective-permute-start | bytes 589832 | tf_op jit(solution)/shard_map/ppermute | solution.py:525
  45.8 15.6 %collective-permute-start.8 = (f32[24,2048]{1,0:T(8,128)S(1)}, f32[24,2048]{1,0:T(8,128)S(1)}, u32[]{:S(2)}, u32[]{:S(2)}) collective-permute-start(f32[24,2048]{1,0:T(8,128)S(1)} %get-tuple-element.76), channel_id=1, source_target_pairs={{1,0},{2,1},{3,2},{4,3},{5,4},{6,5},{7,6},{9,8},{10,9},{11,10},{12... | collective-permute-start | bytes 589832 | tf_op jit(solution)/shard_map/ppermute | solution.py:525
  50.4 6.5 %collective-permute-start.10 = (f32[16,128]{1,0:T(8,128)S(1)}, f32[16,128]{1,0:T(8,128)S(1)}, u32[]{:S(2)}, u32[]{:S(2)}) collective-permute-start(f32[16,128]{1,0:T(8,128)S(1)} %get-tuple-element.77), channel_id=1, source_target_pairs={{2,0},{3,1},{4,2},{5,3},{6,4},{7,5},{10,8},{11,9},{12,10},{13,11},... | collective-permute-start | bytes 24584 | tf_op jit(solution)/shard_map/ppermute | solution.py:525
  55.0 6.4 %collective-permute-start.9 = (f32[16,128]{1,0:T(8,128)S(1)}, f32[16,128]{1,0:T(8,128)S(1)}, u32[]{:S(2)}, u32[]{:S(2)}) collective-permute-start(f32[16,128]{1,0:T(8,128)S(1)} %get-tuple-element.77), channel_id=1, source_target_pairs={{0,2},{1,3},{2,4},{3,5},{4,6},{5,7},{8,10},{9,11},{10,12},{11,13},... | collective-permute-start | bytes 24584 | tf_op jit(solution)/shard_map/ppermute | solution.py:525

commit v3 on v2

--- a/solution.py
+++ b/solution.py
@@ -18,6 +18,21 @@
 EZ = (128, 67, 37, 21, 13)
 PY = (64, 40, 24, 16, 16)
 OZ = (0, 0, 67, 104, 44)
+
+
+def is_even(axis):
+    return (lax.axis_index(axis) & 1) == 0
+
+
+def store_pair(even, a_ref, b_ref, where, up, down):
+    a_ref[where] = jnp.where(even, up, down)
+    b_ref[where] = jnp.where(even, down, up)
+
+
+def picked(even, a_ref, b_ref):
+    return lambda where: jnp.where(even, a_ref[where], b_ref[where])
+
+
 FAR = (range(0, 3), range(3, 5))
 V_COLUMNS = ((3, range(0, 5)), (3, range(5, 9)), (4, range(0, 7)))
 
@@ -130,10 +145,10 @@
     return out
 
 
-def restrict_kernel(q_ref, s1f_ref, s1b_ref, s2_ref, v_ref, far):
+def restrict_kernel(q_ref, sa_ref, sb_ref, s2_ref, v_ref, far):
+    even = is_even("gx")
     for s in range(8):
-        s1b_ref[pl.ds(s * 64, 64), :] = q_ref[s]
-        s1f_ref[pl.ds(s * 64, 64), :] = q_ref[s + 24]
+        store_pair(even, sa_ref, sb_ref, pl.ds(s * 64, 64), q_ref[s + 24], q_ref[s])
     ix, iy, iz = lax.axis_index("gx"), lax.axis_index("gy"), lax.axis_index("gz")
     low = lanes_mask(0, EZ[1])
     slab = lambda i: q_ref[i]
@@ -150,11 +165,11 @@
     for s in range(EX[2]):
         far[s] = kept[2][s]
     for s in range(11):
-        for ref, at in ((s1b_ref, s), (s1f_ref, s + EX[1] - 11)):
-            ref[pl.ds(512 + s * 40, 24), :] = jnp.where(low, kept[1][at][:24], kept[2][s])
-            ref[pl.ds(512 + s * 40 + 24, 16), :] = kept[1][at][24:]
+        up, down = kept[1][s + EX[1] - 11], kept[1][s]
+        store_pair(even, sa_ref, sb_ref, pl.ds(512 + s * 40, 24), jnp.where(low, up[:24], kept[2][s]), jnp.where(low, down[:24], kept[2][s]))
+        store_pair(even, sa_ref, sb_ref, pl.ds(512 + s * 40 + 24, 16), up[24:], down[24:])
     for s in range(11, EX[2]):
-        for ref in (s1b_ref, s1f_ref):
+        for ref in (sa_ref, sb_ref):
             ref[pl.ds(952 + (s - 11) * 24, 24), :] = kept[2][s]
     start = jnp.where(ix < 2, 8, 0)
     mask = lanes_mask(OZ[2], EZ[2])
@@ -185,8 +200,11 @@
         store(i, total)
 
 
-def x_kernel(taps_ref, q_ref, sf_ref, sb_ref, l_ref, r_ref, f_ref, y0_ref, o_ref, fw_ref, bw_ref, tb_ref, q1, q2):
+def x_kernel(taps_ref, q_ref, sa_ref, sb_ref, ra_ref, rb_ref, f_ref, y0_ref, o_ref, fa_ref, fb_ref, tb_ref, q1, q2):
     ix = lax.axis_index("gx")
+    even, even_y = is_even("gx"), is_even("gy")
+    below, above = picked(even, rb_ref, ra_ref), picked(even, ra_ref, rb_ref)
+    sent_up, sent_down = picked(even, sa_ref, sb_ref), picked(even, sb_ref, sa_ref)
     taps0 = [taps_ref[0, 0, t] for t in range(17)]
 
     def level0(j, _):
@@ -195,11 +213,11 @@
             acc = {}
             for p in range(first, first + 32):
                 if p < 8:
-                    v = l_ref[pl.ds(pl.multiple_of(p * 64 + j * 8, 8), 8), :]
+                    v = below(pl.ds(pl.multiple_of(p * 64 + j * 8, 8), 8))
                 elif p < 40:
                     v = q_ref[p - 8, rows, :]
                 else:
-                    v = r_ref[pl.ds(pl.multiple_of((p - 40) * 64 + j * 8, 8), 8), :]
+                    v = above(pl.ds(pl.multiple_of((p - 40) * 64 + j * 8, 8), 8))
                 for t in range(17):
                     i = p - t
                     if first <= i < first + 16:
@@ -211,13 +229,12 @@
 
     lax.fori_loop(0, 8, level0, 0)
     for i in range(32):
-        bw_ref[pl.ds(i * 8, 8), :] = y0_ref[i, pl.ds(0, 8), :]
-        fw_ref[pl.ds(i * 8, 8), :] = y0_ref[i, pl.ds(56, 8), :]
+        store_pair(even_y, fa_ref, fb_ref, pl.ds(i * 8, 8), y0_ref[i, pl.ds(56, 8), :], y0_ref[i, pl.ds(0, 8), :])
 
     def received(ref, at, rows):
         if not 0 <= at < (11 if rows == 40 else 13):
             return None
-        return ref[pl.ds(512 + at * 40 if at < 11 else 952 + (at - 11) * 24, rows), :]
+        return ref(pl.ds(512 + at * 40 if at < 11 else 952 + (at - 11) * 24, rows))
 
     def added(values):
         values = [v for v in values if v is not None]
@@ -228,20 +245,20 @@
 
     def own(at, rows):
         if rows == 24 or at < 11:
-            return received(sb_ref, at, rows)
-        return received(sf_ref, at - 8, rows)
+            return received(sent_down, at, rows)
+        return received(sent_up, at - 8, rows)
 
     for r in range(35):
         cell = r - 9
-        q1[r] = added([own(cell + 1, 40), received(l_ref, cell + 9, 40), received(r_ref, cell - 15, 40)])
+        q1[r] = added([own(cell + 1, 40), received(below, cell + 9, 40), received(above, cell - 15, 40)])
     for r in range(29):
         cell = r - 10
-        q2[r] = added([own(cell + 2, 24), received(l_ref, cell + 10, 24), received(r_ref, cell - 6, 24)])
+        q2[r] = added([own(cell + 2, 24), received(below, cell + 10, 24), received(above, cell - 6, 24)])
     start = jnp.where(ix < 2, 24, 0)
     mask = lanes_mask(OZ[2], EZ[2])
     for k, members in enumerate(FAR):
         for n, s in enumerate(members):
-            q2[start + s] += jnp.where(mask, pltpu.roll(f_ref[pl.ds(48 + k * 24, 24), :], (OZ[2] - n * EZ[2]) % 128, 1), 0.0)
+            q2[start + s] += jnp.where(mask, pltpu.roll(f_ref[k], (OZ[2] - n * EZ[2]) % 128, 1), 0.0)
     low = lanes_mask(0, EZ[1])
     two = {}
 
@@ -256,8 +273,7 @@
         if s < EX[2]:
             f = jnp.where(low, f, two[s][8:])
             b = jnp.where(low, b, two[s][:16])
-        fw_ref[pl.ds(256 + s * 16, 16), :] = f
-        bw_ref[pl.ds(256 + s * 16, 16), :] = b
+        store_pair(even_y, fa_ref, fb_ref, pl.ds(256 + s * 16, 16), f, b)
 
     for level in (3, 4):
         for t in range(17):
@@ -266,7 +282,7 @@
     conv_x(EX[1], taps_ref, 1, lambda r: q1[r], keep1)
 
 
-def coarse_y_kernel(taps_ref, v_ref, s2_ref, near_ref, far_ref):
+def coarse_y_kernel(taps_ref, v_ref, u_ref):
     iy = lax.axis_index("gy")
     block = stacked(jnp.concatenate([v_ref[k] for k in range(8)], axis=0), 0, 1, 0)
     for level, first, last in ((3, 0, 256), (4, 256, 384)):
@@ -276,10 +292,7 @@
         at = jnp.where(r < EY[level], (d - iy) * BY[level] + r + LOW[level], BAD)
         out = dot(thirds(toeplitz(taps_ref, level, 1, at - to + 8), 128), block[:, first:last])
         for c in range(first, last, 128):
-            for ref in (near_ref, far_ref):
-                ref[pl.ds(c // 8, 16), :] = out[:, c - first : c - first + 128]
-    for k in range(2):
-        far_ref[pl.ds(48 + k * 24, 24), :] = s2_ref[k]
+            u_ref[pl.ds(c // 8, 16), :] = out[:, c - first : c - first + 128]
 
 
 def coarse_kernel(taps_ref, own_ref, low_ref, high_ref, far_ref, z3_ref, z4_ref, t4_ref, g3, g4):
@@ -394,36 +407,45 @@
     return jnp.concatenate([block, jnp.zeros((16, 128), F32)], axis=0).T[:16]
 
 
-def y_kernel(y0_ref, o_ref, lo_ref, hi_ref, z3_ref, z4_ref, *refs):
+def store_rows(even, a_ref, b_ref, at, up, down):
+    store_pair(even, a_ref, b_ref, (slice(None), pl.ds(2048 + at, 128)), up[:8], down[:8])
+    store_pair(even, a_ref, b_ref, (slice(None), pl.ds(3584 + at, 128)), up[8:], down[8:])
+
+
+def load_rows(pick, at, count):
+    return jnp.concatenate([pick((slice(None), pl.ds(2048 + at, count))), pick((slice(None), pl.ds(3584 + at, count)))], axis=0)
+
+
+def y_kernel(y0_ref, o_ref, ra_ref, rb_ref, z3_ref, z4_ref, *refs):
+    even, even_z = is_even("gy"), is_even("gz")
+    below, above = picked(even, rb_ref, ra_ref), picked(even, ra_ref, rb_ref)
     my = [ref[...] for ref in refs[:3]]
-    z0_ref, z1_ref, z2_ref, fw_ref, bw_ref = refs[3:]
+    z0_ref, z1_ref, z2_ref, fa_ref, fb_ref = refs[3:]
     for base in range(0, 32, 4):
         parts = []
         for i in range(base, base + 4):
             parts.append(jnp.concatenate(
-                [lo_ref[pl.ds(i * 8, 8), :], y0_ref[i], hi_ref[pl.ds(i * 8, 8), :]], axis=0))
+                [below(pl.ds(i * 8, 8)), y0_ref[i], above(pl.ds(i * 8, 8))], axis=0))
         out = dot(my[0], stacked(jnp.concatenate(parts, axis=1), 0, 1, 0))
         for n in range(4):
             z0_ref[pl.ds((base + n) * 64, 64), :] = out[:, n * 128 : (n + 1) * 128]
     for level, z_ref in ((1, z1_ref), (2, z2_ref)):
         n, rows = EX[level], PY[level]
-        parts = [jnp.concatenate([lo_ref[pl.ds(256 + s * 16, 16), :], o_ref[s, pl.ds(0, rows), :], hi_ref[pl.ds(256 + s * 16, 16), :]], axis=0)
+        parts = [jnp.concatenate([below(pl.ds(256 + s * 16, 16)), o_ref[s, pl.ds(0, rows), :], above(pl.ds(256 + s * 16, 16))], axis=0)
                  for s in range(n)]
         out = dot(my[level], stacked(jnp.concatenate(parts, axis=1), 0, 1, 0))
         for s in range(n):
             z_ref[pl.ds(s * rows, rows), :] = out[:, s * 128 : (s + 1) * 128]
     for k in range(16):
         t = z0_ref[pl.ds(k * 128, 128), :].T
-        bw_ref[pl.ds(0, 8), pl.ds(k * 128, 128)] = t[:8]
-        fw_ref[pl.ds(0, 8), pl.ds(k * 128, 128)] = t[120:]
+        store_pair(even_z, fa_ref, fb_ref, (slice(None), pl.ds(k * 128, 128)), t[120:], t[:8])
     for k in range(6):
         size = 128 if k < 5 else 120
         block = z1_ref[pl.ds(k * 128, size), :]
         if size < 128:
             block = jnp.concatenate([block, jnp.zeros((128 - size, 128), F32)], axis=0)
         t = block.T
-        bw_ref[pl.ds(8, 16), pl.ds(k * 128, 128)] = t[0:16]
-        fw_ref[pl.ds(8, 16), pl.ds(k * 128, 128)] = t[56:72]
+        store_rows(even_z, fa_ref, fb_ref, k * 128, t[56:72], t[0:16])
     for level, z_ref, at, f, count in ((2, z2_ref, 768, 24, 312), (3, z3_ref, 1152, 8, 144)):
         for k in range((count + 127) // 128):
             size = min(128, count - k * 128)
@@ -431,11 +453,9 @@
             if size < 128:
                 block = jnp.concatenate([block, jnp.zeros((128 - size, 128), F32)], axis=0)
             t = block.T
-            bw_ref[pl.ds(8, 16), pl.ds(at + k * 128, 128)] = t[0:16]
-            fw_ref[pl.ds(8, 16), pl.ds(at + k * 128, 128)] = t[f : f + 16]
+            store_rows(even_z, fa_ref, fb_ref, at + k * 128, t[f : f + 16], t[0:16])
     t = level4_rows(z4_ref)
-    for ref in (bw_ref, fw_ref):
-        ref[pl.ds(8, 16), pl.ds(1408, 128)] = t
+    store_rows(even_z, fa_ref, fb_ref, 1408, t, t)
 
 
 Z_AT = {0: 0, 1: 0, 2: 768, 3: 1152, 4: 1408}
@@ -454,7 +474,10 @@
 
 
 def z_kernel(*refs):
-    t_refs, (lo_ref, hi_ref, l4_ref, h4_ref), m_refs, py = refs[:5], refs[5:9], refs[9:14], refs[14:18]
+    t_refs, (ra_ref, rb_ref, a4_ref, b4_ref), m_refs, py = refs[:5], refs[5:9], refs[9:14], refs[14:18]
+    even, even2 = is_even("gz"), (lax.axis_index("gz") & 2) == 0
+    below, above = picked(even, rb_ref, ra_ref), picked(even, ra_ref, rb_ref)
+    below2, above2 = picked(even2, b4_ref, a4_ref), picked(even2, a4_ref, b4_ref)
     out_ref, acc = refs[18:]
     first = (((0,), (0,)), ((), ()))
 
@@ -464,10 +487,9 @@
     total = None
     for level in (4, 3, 2, 1):
         n = Z_ROWS[level]
-        columns = pl.ds(Z_AT[level], (n + 127) // 128 * 128)
-        halo = [lo_ref[pl.ds(8, 16), columns], hi_ref[pl.ds(8, 16), columns]]
+        halo = [load_rows(ref, Z_AT[level], (n + 127) // 128 * 128) for ref in (below, above)]
         if level == 4:
-            halo = [l4_ref[...], *halo, h4_ref[...]]
+            halo = [below2(...), *halo, above2(...)]
         term = t_refs[level][...] + halo_part(level, jnp.concatenate(halo, axis=0))[:n]
         planes = [term[s * PY[level] : (s + 1) * PY[level]] for s in range(EX[level])]
         if total is not None:
@@ -488,7 +510,7 @@
             total.append(value)
             if fine == 0:
                 acc[cell] = value
-    halo = jnp.concatenate([lo_ref[pl.ds(0, 8), :], hi_ref[pl.ds(0, 8), :]], axis=0)
+    halo = jnp.concatenate([pick((slice(None), pl.ds(0, 2048))) for pick in (below, above)], axis=0)
     for k in range(4):
         term = halo_part(0, halo[:, k * 512 : (k + 1) * 512])
         for i in range(8):
@@ -513,60 +535,58 @@
     )
 
 
-def steps(axis, by):
-    count = lax.axis_size(axis)
-    return [(i, i + by) for i in range(count) if 0 <= i + by < count]
-
-
 def per_device(charges, kernel_taps):
     taps = kernel_taps
 
-    def shift(v, axis, by):
-        return lax.ppermute(v, axis, steps(axis, by))
-
-    s1f, s1b, s2, v = call(
+    def swap(v, axis, by=1, second=False):
+        count = lax.axis_size(axis)
+        partner = lambda i: i ^ by if not second else ((i + by) ^ by) - by
+        return lax.ppermute(v, axis, [(i, partner(i)) for i in range(count) if 0 <= partner(i) < count])
+
+    sa, sb, s2, v = call(
         restrict_kernel,
         [((1000, 128), F32), ((1000, 128), F32), ((2, 24, 128), F32),
          ((8, 16, 384), F32)],
         [VM], [pltpu.VMEM((13, 24, 128), F32)],
     )(charges)
-    l1 = shift(s1f, "gx", 1)
-    r1 = shift(s1b, "gx", -1)
+    ra = swap(sa, "gx")
+    rb = swap(sb, "gx", second=True)
+    f2 = lax.ppermute(s2, "gx", [(i, i ^ 2) for i in range(4)])
     vs = lax.all_to_all(v, "gy", 0, 0)
-    near, far = call(coarse_y_kernel, [((48, 128), F32), ((96, 128), F32)], [SM] + [VM] * 2)(taps, vs, s2)
-    low = lax.ppermute(near, "gx", [(i, (i + 1) % 4) for i in range(4)])
-    high = lax.ppermute(near, "gx", [(i, (i + 3) % 4) for i in range(4)])
-    far = lax.ppermute(far, "gx", [(i, (i + 2) % 4) for i in range(4)])
+    (u,) = call(coarse_y_kernel, [((48, 128), F32)], [SM, VM])(taps, vs)
+    others = []
+    for by in (1, 3, 2):
+        others.append(lax.ppermute(u, "gx", [(i, (i + by) % 4) for i in range(4)]))
     mats_shapes = [(64, 240), (40, 240), (24, 192)]
     for halo in (16, 32, 32, 32, 64):
         mats_shapes += [(128, 256), (3 * halo, 128)]
     mats_shapes += [(PY[l], 2 * up16(PY[l + 1])) for l in range(4)]
     mats = call(prep_kernel, [(w, BF16) for w in mats_shapes], [SM])(taps)
     my, own, halo, py = mats[:3], mats[3:13:2], mats[4:13:2], mats[13:]
-    y0, o, fw, bw, tb = call(
+    y0, o, sa, sb, tb = call(
         x_kernel,
         [((32, 64, 128), F32), ((19, 40, 128), F32), ((560, 128), F32), ((560, 128), F32), ((48, 128), F32)],
         [SM] + [VM] * 6,
         [pltpu.VMEM((35, 40, 128), F32), pltpu.VMEM((29, 24, 128), F32)],
-    )(taps, charges, s1f, s1b, l1, r1, far)
-    lo = shift(fw, "gy", 1)
-    hi = shift(bw, "gy", -1)
+    )(taps, charges, sa, sb, ra, rb, f2)
+    ra = swap(sa, "gy")
+    rb = swap(sb, "gy", second=True)
     z3, z4, t4 = call(
         coarse_kernel, [((144, 128), F32), ((112, 128), F32), ((16, 128), F32)], [VM] * 5,
         [pltpu.VMEM((37, 16, 128), F32), pltpu.VMEM((29, 16, 128), F32)],
-    )(tb, near, low, high, far)
-    l4 = shift(t4, "gz", 2)
-    h4 = shift(t4, "gz", -2)
-    z0, z1, z2, fw, bw = call(
-        y_kernel, [((Z_ROWS[l], 128), F32) for l in range(3)] + [((24, 2048), F32), ((24, 2048), F32)], [VM] * 9
-    )(y0, o, lo, hi, z3, z4, *my[:3])
+    )(tb, u, *others)
+    a4 = swap(t4, "gz", 2)
+    b4 = swap(t4, "gz", 2, second=True)
+    z0, z1, z2, sa, sb = call(
+        y_kernel, [((Z_ROWS[l], 128), F32) for l in range(3)] + [((8, 5120), F32), ((8, 5120), F32)], [VM] * 9
+    )(y0, o, ra, rb, z3, z4, *my[:3])
     z = (z0, z1, z2, z3, z4)
-    lo = shift(fw, "gz", 1)
-    hi = shift(bw, "gz", -1)
+    ra = swap(sa, "gz")
+    rb = swap(sb, "gz", second=True)
     terms = call(own_kernel, [((Z_ROWS[l], 128), F32) for l in range(5)], [VM] * 10)(*z, *own)
     (out,) = call(
         z_kernel, [((32, 64, 128), F32)], [VM] * 18, [pltpu.VMEM((32, 64, 128), F32)]
-    )(*terms, lo, hi, l4, h4, *halo, *py)
+    )(*terms, ra, rb, a4, b4, *halo, *py)
     return out
 
 

time: 63.9 us -> 59.3 us (0.928)
  the two profiles are of different devices: /device:TPU:224 before, /device:TPU:160 now
where the time goes in v3:
time: 59.3 us; the launch traced here: 58.8 us
  starting transfers between devices  30.1 us (51%)
  Pallas kernels  12.8 us (22%)
  waiting for transfers between devices  11 us (19%)
  local copies, waits for them, and re-layouts  4.9 us (8%)
    ppermute x8, starting transfers between devices, swap(): lax.ppermute(v, axis, [(i, partner(i)) for i in range(count) if 0 <= part...  15.3 us
    all_to_all x1, starting transfers between devices, per_device(): vs = lax.all_to_all(v, 'gy', 0, 0)  5.94 us
    ppermute x8, waiting for transfers between devices, swap(): lax.ppermute(v, axis, [(i, partner(i)) for i in range(count) if 0 <= part...  5.08 us
    unnamed x14, local copies, waits for them, and re-layouts  4.9 us
    ppermute x3, starting transfers between devices, per_device(): others.append(lax.ppermute(u, 'gx', [(i, (i + by) % 4) for i in range(4)]))  4.88 us
    ppermute x1, waiting for transfers between devices, per_device(): f2 = lax.ppermute(s2, 'gx', [(i, i ^ 2) for i in range(4)])  4.03 us
    ppermute x1, starting transfers between devices, per_device(): f2 = lax.ppermute(s2, 'gx', [(i, i ^ 2) for i in range(4)])  3.95 us
    pallas_call x1, Pallas kernels, per_device(): call(x_kernel, [((32, 64, 128), F32), ((19, 40, 128), F32), ((560, 128),...  3.53 us
  transfers between devices with their start and end apart: 13, of which 4 were waited for; matrix products, arithmetic and copies ran while one was open for 0% of the time, Pallas kernels for 13%

profile of v3, /device:TPU:160, one launch (start us, length us, event | category | flops | bytes accessed | tf_op | source)
XLA Modules:
  0.0 58.8 jit_solution(474836051474383245)
XLA Ops:
  0.0 1.2 %copy-done = f32[32,64,128]{2,1,0:T(8,128)S(1)} copy-done((f32[32,64,128]{2,1,0:T(8,128)S(1)}, f32[32,64,128]{2,1,0:T(8,128)}, u32[]{:S(2)}) %copy-start) | copy-done | bytes 1048600
  1.2 2.2 %shard_map.28 = (f32[1000,128]{1,0:T(8,128)S(1)}, f32[1000,128]{1,0:T(8,128)S(1)}, f32[2,24,128]{2,1,0:T(8,128)S(1)}, f32[8,16,384]{2,1,0:T(8,128)}) custom-call(f32[32,64,128]{2,1,0:T(8,128)S(1)} %copy-done), custom_call_target="tpu_custom_call" | custom-call | flops 400000000 | bytes 2097152 | tf_op jit(solution)/shard_map/pallas_call | solution.py:546
  3.4 1.5 %collective-permute-start = (f32[1000,128]{1,0:T(8,128)S(1)}, f32[1000,128]{1,0:T(8,128)S(1)}, u32[]{:S(2)}, u32[]{:S(2)}) collective-permute-start(f32[1000,128]{1,0:T(8,128)S(1)} %get-tuple-element.44.sa_ref), channel_id=1, source_target_pairs={{0,64},{64,0},{128,192},{192,128},{1,65},{65,1},{129,193},{193,129... | collective-permute-start | bytes 1536008 | tf_op jit(solution)/shard_map/ppermute | solution.py:544
  5.6 5.9 %all-to-all-start = ((f32[8,16,384]{2,1,0:T(8,128)}), f32[8,16,384]{2,1,0:T(8,128)}, u32[]{:S(2)}, u32[]{:S(2)}) async-start(f32[8,16,384]{2,1,0:T(8,128)} %get-tuple-element.52), calls=%async_computation | async-start | bytes 393216 | tf_op jit(solution)/shard_map/all_to_all | solution.py:555
  11.5 4.0 %collective-permute-start.2 = (f32[2,24,128]{2,1,0:T(8,128)S(1)}, f32[2,24,128]{2,1,0:T(8,128)S(1)}, u32[]{:S(2)}, u32[]{:S(2)}) collective-permute-start(f32[2,24,128]{2,1,0:T(8,128)S(1)} %get-tuple-element.46), channel_id=1, source_target_pairs={{0,128},{64,192},{128,0},{192,64},{1,129},{65,193},{129,1},{193,65... | collective-permute-start | bytes 73736 | tf_op jit(solution)/shard_map/ppermute | solution.py:554
  15.5 4.0 %collective-permute-done.2.f_ref = f32[2,24,128]{2,1,0:T(8,128)S(1)} collective-permute-done((f32[2,24,128]{2,1,0:T(8,128)S(1)}, f32[2,24,128]{2,1,0:T(8,128)S(1)}, u32[]{:S(2)}, u32[]{:S(2)}) %collective-permute-start.2) | collective-permute-done | bytes 24608 | tf_op jit(solution)/shard_map/ppermute | solution.py:554
  20.3 0.8 %copy-done.4 = f32[1000,128]{1,0:T(8,128)} copy-done((f32[1000,128]{1,0:T(8,128)}, f32[1000,128]{1,0:T(8,128)S(1)}, u32[]{:S(2)}) %copy-start.4) | copy-done | bytes 512024
  21.1 1.0 %copy-done.3 = f32[1000,128]{1,0:T(8,128)S(1)} copy-done((f32[1000,128]{1,0:T(8,128)S(1)}, f32[1000,128]{1,0:T(8,128)}, u32[]{:S(2)}) %copy-start.3) | copy-done | bytes 512024
  22.1 1.0 %copy-done.5 = f32[1000,128]{1,0:T(8,128)S(1)} copy-done((f32[1000,128]{1,0:T(8,128)S(1)}, f32[1000,128]{1,0:T(8,128)}, u32[]{:S(2)}) %copy-start.5) | copy-done | bytes 512024
  23.2 3.5 %shard_map.29 = (f32[32,64,128]{2,1,0:T(8,128)S(1)}, f32[19,40,128]{2,1,0:T(8,128)S(1)}, f32[560,128]{1,0:T(8,128)}, f32[560,128]{1,0:T(8,128)}, f32[48,128]{1,0:T(8,128)S(1)}) custom-call(f32[5,3,17]{2,1,0:T(4,128)S(1)} %copy-done.6, f32[32,64,128]{2,1,0:T(8,128)S(1)} %copy-done.1, f32[1000,128]{1,0:T(8,128)S(1)} %get-tuple-element.44.sa_ref, ...), custom_call_target="tpu_custom_call" | custom-call | flops 400000000 | bytes 2097152 | tf_op jit(solution)/shard_map/pallas_call | solution.py:566
  26.7 1.6 %collective-permute-start.3 = (f32[560,128]{1,0:T(8,128)}, f32[560,128]{1,0:T(8,128)S(1)}, u32[]{:S(2)}, u32[]{:S(2)}) collective-permute-start(f32[560,128]{1,0:T(8,128)} %get-tuple-element.49), channel_id=1, source_target_pairs={{0,8},{8,0},{16,24},{24,16},{32,40},{40,32},{48,56},{56,48},{1,9},... | collective-permute-start | bytes 860168 | tf_op jit(solution)/shard_map/ppermute | solution.py:544
  28.3 4.5 %collective-permute-start.4 = (f32[560,128]{1,0:T(8,128)}, f32[560,128]{1,0:T(8,128)S(1)}, u32[]{:S(2)}, u32[]{:S(2)}) collective-permute-start(f32[560,128]{1,0:T(8,128)} %get-tuple-element.50), channel_id=1, source_target_pairs={{8,16},{16,8},{24,32},{32,24},{40,48},{48,40},{9,17},{17,9},{25,33... | collective-permute-start | bytes 860168 | tf_op jit(solution)/shard_map/ppermute | solution.py:544
  32.8 1.2 %shard_map.30.own_ref = f32[48,128]{1,0:T(8,128)S(1)} custom-call(f32[5,3,17]{2,1,0:T(4,128)S(1)} %copy-done.6, f32[8,16,384]{2,1,0:T(8,128)} %all-to-all-done.v_ref), custom_call_target="tpu_custom_call" | custom-call | flops 400000000 | bytes 2097152 | tf_op jit(solution)/shard_map/pallas_call | solution.py:556
  34.0 1.1 %collective-permute-start.5 = (f32[48,128]{1,0:T(8,128)S(1)}, f32[48,128]{1,0:T(8,128)S(1)}, u32[]{:S(2)}, u32[]{:S(2)}) collective-permute-start(f32[48,128]{1,0:T(8,128)S(1)} %shard_map.30.own_ref), channel_id=1, source_target_pairs={{0,64},{64,128},{128,192},{192,0},{1,65},{65,129},{129,193},{193,1... | collective-permute-start | bytes 73736 | tf_op jit(solution)/shard_map/ppermute | solution.py:559
  35.1 2.2 %collective-permute-start.6 = (f32[48,128]{1,0:T(8,128)S(1)}, f32[48,128]{1,0:T(8,128)S(1)}, u32[]{:S(2)}, u32[]{:S(2)}) collective-permute-start(f32[48,128]{1,0:T(8,128)S(1)} %shard_map.30.own_ref), channel_id=1, source_target_pairs={{0,192},{64,0},{128,64},{192,128},{1,193},{65,1},{129,65},{193,129... | collective-permute-start | bytes 73736 | tf_op jit(solution)/shard_map/ppermute | solution.py:559
  37.2 1.6 %collective-permute-start.7 = (f32[48,128]{1,0:T(8,128)S(1)}, f32[48,128]{1,0:T(8,128)S(1)}, u32[]{:S(2)}, u32[]{:S(2)}) collective-permute-start(f32[48,128]{1,0:T(8,128)S(1)} %shard_map.30.own_ref), channel_id=1, source_target_pairs={{0,128},{64,192},{128,0},{192,64},{1,129},{65,193},{129,1},{193,65... | collective-permute-start | bytes 73736 | tf_op jit(solution)/shard_map/ppermute | solution.py:559
  38.9 1.8 %shard_map.32 = (bf16[64,240]{1,0:T(8,128)(2,1)S(1)}, bf16[40,240]{1,0:T(8,128)(2,1)S(1)}, bf16[24,192]{1,0:T(8,128)(2,1)S(1)}, bf16[128,256]{1,0:T(8,128)(2,1)S...) custom-call(f32[5,3,17]{2,1,0:T(4,128)S(1)} %copy-done.6), custom_call_target="tpu_custom_call" | custom-call | flops 400000000 | bytes 2097152 | tf_op jit(solution)/shard_map/pallas_call | solution.py:564
  40.7 1.9 %collective-permute-done.7.far_ref = f32[48,128]{1,0:T(8,128)S(1)} collective-permute-done((f32[48,128]{1,0:T(8,128)S(1)}, f32[48,128]{1,0:T(8,128)S(1)}, u32[]{:S(2)}, u32[]{:S(2)}) %collective-permute-start.7) | collective-permute-done | bytes 24608 | tf_op jit(solution)/shard_map/ppermute | solution.py:559
  42.9 1.0 %shard_map.33 = (f32[2048,128]{1,0:T(8,128)S(1)}, f32[760,128]{1,0:T(8,128)S(1)}, f32[312,128]{1,0:T(8,128)S(1)}, f32[8,5120]{1,0:T(8,128)S(1)}, f32[8,5120]{1,0:T(8,128)S(1)}) custom-call(f32[32,64,128]{2,1,0:T(8,128)S(1)} %get-tuple-element.47.y0_ref, f32[19,40,128]{2,1,0:T(8,128)S(1)} %get-tuple-element.48.o_ref, ...), custom_call_target="tpu_custom_call" | custom-call | flops 400000000 | bytes 2097152 | tf_op jit(solution)/shard_map/pallas_call | solution.py:580
  44.1 1.9 %collective-permute-start.9 = (f32[8,5120]{1,0:T(8,128)S(1)}, f32[8,5120]{1,0:T(8,128)S(1)}, u32[]{:S(2)}, u32[]{:S(2)}) collective-permute-start(f32[8,5120]{1,0:T(8,128)S(1)} %get-tuple-element.72), channel_id=1, source_target_pairs={{1,2},{2,1},{3,4},{4,3},{5,6},{6,5},{9,10},{10,9},{11,12},{12,11},... | collective-permute-start | bytes 491528 | tf_op jit(solution)/shard_map/ppermute | solution.py:544
  46.0 3.1 %collective-permute-start.10 = (f32[16,128]{1,0:T(8,128)S(1)}, f32[16,128]{1,0:T(8,128)S(1)}, u32[]{:S(2)}, u32[]{:S(2)}) collective-permute-start(f32[16,128]{1,0:T(8,128)S(1)} %get-tuple-element.73), channel_id=1, source_target_pairs={{0,2},{1,3},{2,0},{3,1},{4,6},{5,7},{6,4},{7,5},{8,10},{9,11},{10,... | collective-permute-start | bytes 24584 | tf_op jit(solution)/shard_map/ppermute | solution.py:544
  49.1 1.9 %collective-permute-start.11 = (f32[16,128]{1,0:T(8,128)S(1)}, f32[16,128]{1,0:T(8,128)S(1)}, u32[]{:S(2)}, u32[]{:S(2)}) collective-permute-start(f32[16,128]{1,0:T(8,128)S(1)} %get-tuple-element.73), channel_id=1, source_target_pairs={{2,4},{3,5},{4,2},{5,3},{10,12},{11,13},{12,10},{13,11},{18,20},{1... | collective-permute-start | bytes 24584 | tf_op jit(solution)/shard_map/ppermute | solution.py:544
  52.4 4.3 %collective-permute-done.11.refs_8_ = f32[16,128]{1,0:T(8,128)S(1)} collective-permute-done((f32[16,128]{1,0:T(8,128)S(1)}, f32[16,128]{1,0:T(8,128)S(1)}, u32[]{:S(2)}, u32[]{:S(2)}) %collective-permute-start.11) | collective-permute-done | bytes 8224 | tf_op jit(solution)/shard_map/ppermute | solution.py:544
  56.7 2.1 %shard_map.35 = f32[32,64,128]{2,1,0:T(8,128)} custom-call(f32[2048,128]{1,0:T(8,128)S(1)} %get-tuple-element.66.refs_0_, f32[760,128]{1,0:T(8,128)S(1)} %get-tuple-element.67.refs_1_, f32[312,128]{1,0:T(8,128)S(1)} %get-tuple-element.68.refs_2_, f32[144,128]{1,0:T(8,128)S(1)} %get-tuple-element.69.refs_3_, f32[112,128]{1,0:T(8,128)S(1)} %get-tuple-element.70.refs_4_, ...), custom_call_target="tpu_custom_call" | custom-call | flops 400000000 | bytes 2097152 | tf_op jit(solution)/shard_map/pallas_call | solution.py:587
  (24 shorter events, 3.4 us)
Async XLA Ops:
  0.0 1.2 %copy-start = (f32[32,64,128]{2,1,0:T(8,128)S(1)}, f32[32,64,128]{2,1,0:T(8,128)}, u32[]{:S(2)}) copy-start(f32[32,64,128]{2,1,0:T(8,128)} %q_ref.3) | copy-start | bytes 3145732
  1.2 19.9 %copy-start.1 = (f32[32,64,128]{2,1,0:T(8,128)S(1)}, f32[32,64,128]{2,1,0:T(8,128)}, u32[]{:S(2)}) copy-start(f32[32,64,128]{2,1,0:T(8,128)} %q_ref.3) | copy-start | bytes 3145732
  3.4 16.1 %collective-permute-start = (f32[1000,128]{1,0:T(8,128)S(1)}, f32[1000,128]{1,0:T(8,128)S(1)}, u32[]{:S(2)}, u32[]{:S(2)}) collective-permute-start(f32[1000,128]{1,0:T(8,128)S(1)} %get-tuple-element.44.sa_ref), channel_id=1, source_target_pairs={{0,64},{64,0},{128,192},{192,128},{1,65},{65,1},{129,193},{193,129... | collective-permute-start | bytes 1536008 | tf_op jit(solution)/shard_map/ppermute | solution.py:544
  4.9 15.4 %collective-permute-start.1 = (f32[1000,128]{1,0:T(8,128)S(1)}, f32[1000,128]{1,0:T(8,128)S(1)}, u32[]{:S(2)}, u32[]{:S(2)}) collective-permute-start(f32[1000,128]{1,0:T(8,128)S(1)} %get-tuple-element.45.sb_ref), channel_id=1, source_target_pairs={{64,128},{128,64},{65,129},{129,65},{66,130},{130,66},{67,131},{13... | collective-permute-start | bytes 1536008 | tf_op jit(solution)/shard_map/ppermute | solution.py:544
  5.6 15.5 %copy-start.6 = (f32[5,3,17]{2,1,0:T(4,128)S(1)}, f32[5,3,17]{2,1,0:T(4,128)}, u32[]{:S(2)}) copy-start(f32[5,3,17]{2,1,0:T(4,128)} %taps_ref.5) | copy-start | bytes 3064
  5.6 27.2 %all-to-all-start = ((f32[8,16,384]{2,1,0:T(8,128)}), f32[8,16,384]{2,1,0:T(8,128)}, u32[]{:S(2)}, u32[]{:S(2)}) async-start(f32[8,16,384]{2,1,0:T(8,128)} %get-tuple-element.52), calls=%async_computation | async-start | bytes 393216 | tf_op jit(solution)/shard_map/all_to_all | solution.py:555
  11.5 8.0 %collective-permute-start.2 = (f32[2,24,128]{2,1,0:T(8,128)S(1)}, f32[2,24,128]{2,1,0:T(8,128)S(1)}, u32[]{:S(2)}, u32[]{:S(2)}) collective-permute-start(f32[2,24,128]{2,1,0:T(8,128)S(1)} %get-tuple-element.46), channel_id=1, source_target_pairs={{0,128},{64,192},{128,0},{192,64},{1,129},{65,193},{129,1},{193,65... | collective-permute-start | bytes 73736 | tf_op jit(solution)/shard_map/ppermute | solution.py:554
  19.5 0.8 %copy-start.2 = (f32[1000,128]{1,0:T(8,128)}, f32[1000,128]{1,0:T(8,128)S(1)}, u32[]{:S(2)}) copy-start(f32[1000,128]{1,0:T(8,128)S(1)} %collective-permute-done.ra_ref) | copy-start | bytes 1536004
  20.3 0.8 %copy-start.4 = (f32[1000,128]{1,0:T(8,128)}, f32[1000,128]{1,0:T(8,128)S(1)}, u32[]{:S(2)}) copy-start(f32[1000,128]{1,0:T(8,128)S(1)} %collective-permute-done.1.rb_ref) | copy-start | bytes 1536004
  21.1 1.0 %copy-start.3 = (f32[1000,128]{1,0:T(8,128)S(1)}, f32[1000,128]{1,0:T(8,128)}, u32[]{:S(2)}) copy-start(f32[1000,128]{1,0:T(8,128)} %copy-done.2) | copy-start | bytes 1536004
  22.1 1.0 %copy-start.5 = (f32[1000,128]{1,0:T(8,128)S(1)}, f32[1000,128]{1,0:T(8,128)}, u32[]{:S(2)}) copy-start(f32[1000,128]{1,0:T(8,128)} %copy-done.4) | copy-start | bytes 1536004
  26.7 16.2 %collective-permute-start.3 = (f32[560,128]{1,0:T(8,128)}, f32[560,128]{1,0:T(8,128)S(1)}, u32[]{:S(2)}, u32[]{:S(2)}) collective-permute-start(f32[560,128]{1,0:T(8,128)} %get-tuple-element.49), channel_id=1, source_target_pairs={{0,8},{8,0},{16,24},{24,16},{32,40},{40,32},{48,56},{56,48},{1,9},... | collective-permute-start | bytes 860168 | tf_op jit(solution)/shard_map/ppermute | solution.py:544
  28.3 14.6 %collective-permute-start.4 = (f32[560,128]{1,0:T(8,128)}, f32[560,128]{1,0:T(8,128)S(1)}, u32[]{:S(2)}, u32[]{:S(2)}) collective-permute-start(f32[560,128]{1,0:T(8,128)} %get-tuple-element.50), channel_id=1, source_target_pairs={{8,16},{16,8},{24,32},{32,24},{40,48},{48,40},{9,17},{17,9},{25,33... | collective-permute-start | bytes 860168 | tf_op jit(solution)/shard_map/ppermute | solution.py:544
  34.0 6.7 %collective-permute-start.5 = (f32[48,128]{1,0:T(8,128)S(1)}, f32[48,128]{1,0:T(8,128)S(1)}, u32[]{:S(2)}, u32[]{:S(2)}) collective-permute-start(f32[48,128]{1,0:T(8,128)S(1)} %shard_map.30.own_ref), channel_id=1, source_target_pairs={{0,64},{64,128},{128,192},{192,0},{1,65},{65,129},{129,193},{193,1... | collective-permute-start | bytes 73736 | tf_op jit(solution)/shard_map/ppermute | solution.py:559
  35.1 5.6 %collective-permute-start.6 = (f32[48,128]{1,0:T(8,128)S(1)}, f32[48,128]{1,0:T(8,128)S(1)}, u32[]{:S(2)}, u32[]{:S(2)}) collective-permute-start(f32[48,128]{1,0:T(8,128)S(1)} %shard_map.30.own_ref), channel_id=1, source_target_pairs={{0,192},{64,0},{128,64},{192,128},{1,193},{65,1},{129,65},{193,129... | collective-permute-start | bytes 73736 | tf_op jit(solution)/shard_map/ppermute | solution.py:559
  37.2 5.3 %collective-permute-start.7 = (f32[48,128]{1,0:T(8,128)S(1)}, f32[48,128]{1,0:T(8,128)S(1)}, u32[]{:S(2)}, u32[]{:S(2)}) collective-permute-start(f32[48,128]{1,0:T(8,128)S(1)} %shard_map.30.own_ref), channel_id=1, source_target_pairs={{0,128},{64,192},{128,0},{192,64},{1,129},{65,193},{129,1},{193,65... | collective-permute-start | bytes 73736 | tf_op jit(solution)/shard_map/ppermute | solution.py:559
  44.0 12.8 %collective-permute-start.8 = (f32[8,5120]{1,0:T(8,128)S(1)}, f32[8,5120]{1,0:T(8,128)S(1)}, u32[]{:S(2)}, u32[]{:S(2)}) collective-permute-start(f32[8,5120]{1,0:T(8,128)S(1)} %get-tuple-element.71), channel_id=1, source_target_pairs={{0,1},{1,0},{2,3},{3,2},{4,5},{5,4},{6,7},{7,6},{8,9},{9,8},{10,11... | collective-permute-start | bytes 491528 | tf_op jit(solution)/shard_map/ppermute | solution.py:544
  44.1 12.7 %collective-permute-start.9 = (f32[8,5120]{1,0:T(8,128)S(1)}, f32[8,5120]{1,0:T(8,128)S(1)}, u32[]{:S(2)}, u32[]{:S(2)}) collective-permute-start(f32[8,5120]{1,0:T(8,128)S(1)} %get-tuple-element.72), channel_id=1, source_target_pairs={{1,2},{2,1},{3,4},{4,3},{5,6},{6,5},{9,10},{10,9},{11,12},{12,11},... | collective-permute-start | bytes 491528 | tf_op jit(solution)/shard_map/ppermute | solution.py:544
  46.0 6.4 %collective-permute-start.10 = (f32[16,128]{1,0:T(8,128)S(1)}, f32[16,128]{1,0:T(8,128)S(1)}, u32[]{:S(2)}, u32[]{:S(2)}) collective-permute-start(f32[16,128]{1,0:T(8,128)S(1)} %get-tuple-element.73), channel_id=1, source_target_pairs={{0,2},{1,3},{2,0},{3,1},{4,6},{5,7},{6,4},{7,5},{8,10},{9,11},{10,... | collective-permute-start | bytes 24584 | tf_op jit(solution)/shard_map/ppermute | solution.py:544
  49.1 7.6 %collective-permute-start.11 = (f32[16,128]{1,0:T(8,128)S(1)}, f32[16,128]{1,0:T(8,128)S(1)}, u32[]{:S(2)}, u32[]{:S(2)}) collective-permute-start(f32[16,128]{1,0:T(8,128)S(1)} %get-tuple-element.73), channel_id=1, source_target_pairs={{2,4},{3,5},{4,2},{5,3},{10,12},{11,13},{12,10},{13,11},{18,20},{1... | collective-permute-start | bytes 24584 | tf_op jit(solution)/shard_map/ppermute | solution.py:544

commit v4 on v3

--- a/solution.py
+++ b/solution.py
@@ -167,10 +167,12 @@
     for s in range(11):
         up, down = kept[1][s + EX[1] - 11], kept[1][s]
         store_pair(even, sa_ref, sb_ref, pl.ds(512 + s * 40, 24), jnp.where(low, up[:24], kept[2][s]), jnp.where(low, down[:24], kept[2][s]))
-        store_pair(even, sa_ref, sb_ref, pl.ds(512 + s * 40 + 24, 16), up[24:], down[24:])
-    for s in range(11, EX[2]):
-        for ref in (sa_ref, sb_ref):
-            ref[pl.ds(952 + (s - 11) * 24, 24), :] = kept[2][s]
+        up, down = up[24:], down[24:]
+        if s < 6:
+            k, at = divmod(s, 3)
+            extra = jnp.concatenate([kept[2][11 + k][at * 8 : at * 8 + 8], jnp.zeros((8, 128), F32)], axis=0)
+            up, down = jnp.where(low, up, extra), jnp.where(low, down, extra)
+        store_pair(even, sa_ref, sb_ref, pl.ds(512 + s * 40 + 24, 16), up, down)
     start = jnp.where(ix < 2, 8, 0)
     mask = lanes_mask(OZ[2], EZ[2])
     for k, members in enumerate(FAR):
@@ -234,7 +236,9 @@
     def received(ref, at, rows):
         if not 0 <= at < (11 if rows == 40 else 13):
             return None
-        return ref(pl.ds(512 + at * 40 if at < 11 else 952 + (at - 11) * 24, rows))
+        if at < 11:
+            return ref(pl.ds(512 + at * 40, rows))
+        return jnp.concatenate([ref(pl.ds(512 + ((at - 11) * 3 + k) * 40 + 24, 8)) for k in range(3)], axis=0)
 
     def added(values):
         values = [v for v in values if v is not None]
@@ -282,7 +286,7 @@
     conv_x(EX[1], taps_ref, 1, lambda r: q1[r], keep1)
 
 
-def coarse_y_kernel(taps_ref, v_ref, u_ref):
+def coarse_y_kernel(taps_ref, v_ref, u_ref, *outs):
     iy = lax.axis_index("gy")
     block = stacked(jnp.concatenate([v_ref[k] for k in range(8)], axis=0), 0, 1, 0)
     for level, first, last in ((3, 0, 256), (4, 256, 384)):
@@ -293,60 +297,6 @@
         out = dot(thirds(toeplitz(taps_ref, level, 1, at - to + 8), 128), block[:, first:last])
         for c in range(first, last, 128):
             u_ref[pl.ds(c // 8, 16), :] = out[:, c - first : c - first + 128]
-
-
-def coarse_kernel(taps_ref, own_ref, low_ref, high_ref, far_ref, z3_ref, z4_ref, t4_ref, g3, g4):
-    ix = lax.axis_index("gx")
-    for g in (g3, g4):
-        g[...] = jnp.zeros_like(g)
-    for ref, step in ((own_ref, 0), (low_ref, 3), (high_ref, 1), (far_ref, 2)):
-        source = (ix + step) & 3
-        for c, (level, members) in enumerate(V_COLUMNS):
-            g = g3 if level == 3 else g4
-            column = ref[pl.ds(c * 16, 16), :]
-            for n, s in enumerate(members):
-                g[source * BX[level] + (LOW[level] + s + 10)] += pltpu.roll(column, (OZ[level] - n * EZ[level]) % 128, 1)
-    for level, g, z_ref in ((3, g3, z3_ref), (4, g4, z4_ref)):
-        start = ix * BX[level] + 10 + LOW[level] - 8
-
-        def keep(i, total, level=level, z_ref=z_ref):
-            z_ref[pl.ds(i * 16, 16), :] = masked(total, x_mask(level, LOW[level] + i))
-
-        conv_x(EX[level], taps_ref, level, lambda r, g=g, start=start: g[start + r], keep)
-    t4_ref[...] = level4_rows(z4_ref)
-
-
-BAD = 1000
-
-
-def out_cells(level, blocks, ext, index, position, count):
-    return jnp.where(in_grid(level, ext, blocks, count, index, position), index + LOW[level], -BAD)
-
-
-def thirds(value, third):
-    hi, lo = split(value)
-    return jnp.where(iota(value.shape, 1) < 2 * third, hi.astype(F32), lo.astype(F32)).astype(BF16)
-
-
-def toeplitz(taps_ref, level, axis, diff):
-    total = jnp.zeros(diff.shape, F32)
-    for t in range(17):
-        total = jnp.where(diff == t, taps_ref[level, axis, t], total)
-    return total
-
-
-def store_z(ref, halo_ref, own, halo):
-    ref[...] = jnp.concatenate(split(own), axis=1)
-    hi, lo = split(halo)
-    halo_ref[...] = jnp.concatenate([hi, hi, lo], axis=0)
-
-
-def prep_kernel(taps_ref, *out):
-    iy = lax.axis_index("gy")
-    iz = lax.axis_index("gz")
-    outs = out[:3]
-    z_outs = [out[3 + 2 * k : 5 + 2 * k] for k in range(5)]
-
     for level, width, ref in ((0, 80, outs[0]), (1, 80, outs[1]), (2, 64, outs[2])):
         shape = (PY[level], 3 * width)
         i, j = iota(shape, 0), repeated(iota(shape, 1), width)
@@ -368,13 +318,65 @@
                 ),
             )
         ref[...] = thirds(toeplitz(taps_ref, level, 1, at - to + 8), width)
+
+
+def coarse_kernel(taps_ref, own_ref, r1_ref, r2_ref, r3_ref, z3_ref, z4_ref, t4_ref, g3, g4):
+    ix = lax.axis_index("gx")
+    for g in (g3, g4):
+        g[...] = jnp.zeros_like(g)
+    for ref, step in ((own_ref, 0), (r1_ref, 1), (r2_ref, 2), (r3_ref, 3)):
+        source = ix ^ step
+        for c, (level, members) in enumerate(V_COLUMNS):
+            g = g3 if level == 3 else g4
+            column = ref[pl.ds(c * 16, 16), :]
+            for n, s in enumerate(members):
+                g[source * BX[level] + (LOW[level] + s + 10)] += pltpu.roll(column, (OZ[level] - n * EZ[level]) % 128, 1)
+    for level, g, z_ref in ((3, g3, z3_ref), (4, g4, z4_ref)):
+        start = ix * BX[level] + 10 + LOW[level] - 8
+
+        def keep(i, total, level=level, z_ref=z_ref):
+            z_ref[pl.ds(i * 16, 16), :] = masked(total, x_mask(level, LOW[level] + i))
+
+        conv_x(EX[level], taps_ref, level, lambda r, g=g, start=start: g[start + r], keep)
+    t4_ref[...] = level4_rows(z4_ref)
+
+
+BAD = 1000
+
+
+def out_cells(level, blocks, ext, index, position, count):
+    return jnp.where(in_grid(level, ext, blocks, count, index, position), index + LOW[level], -BAD)
+
+
+def thirds(value, third):
+    hi, lo = split(value)
+    return jnp.where(iota(value.shape, 1) < 2 * third, hi.astype(F32), lo.astype(F32)).astype(BF16)
+
+
+def toeplitz(taps_ref, level, axis, diff):
+    total = jnp.zeros(diff.shape, F32)
+    for t in range(17):
+        total = jnp.where(diff == t, taps_ref[level, axis, t], total)
+    return total
+
+
+def store_z(ref, halo_ref, own, halo):
+    ref[...] = jnp.concatenate(split(own), axis=1)
+    hi, lo = split(halo)
+    halo_ref[...] = jnp.concatenate([hi, hi, lo], axis=0)
+
+
+def prep_z_kernel(taps_ref, *out):
+    iy = lax.axis_index("gy")
+    iz = lax.axis_index("gz")
+    z_outs = [out[2 * k : 2 * k + 2] for k in range(5)]
     j = iota((128, 128), 0)
     c = iota((128, 128), 1)
     own = toeplitz(taps_ref, 0, 2, j - c + 8)
     j, c = iota((16, 128), 0), iota((16, 128), 1)
     store_z(*z_outs[0], own, toeplitz(taps_ref, 0, 2, jnp.where(j < 8, j - 8, j - 8 + 128) - c + 8))
     for level in range(4):
-        out[13 + level][...] = prolong_y(level, iy)
+        out[10 + level][...] = prolong_y(level, iy)
     prolong = None
     for level in range(1, 5):
         shape = (128, 128)
@@ -409,11 +411,22 @@
 
 def store_rows(even, a_ref, b_ref, at, up, down):
     store_pair(even, a_ref, b_ref, (slice(None), pl.ds(2048 + at, 128)), up[:8], down[:8])
-    store_pair(even, a_ref, b_ref, (slice(None), pl.ds(3584 + at, 128)), up[8:], down[8:])
-
-
-def load_rows(pick, at, count):
-    return jnp.concatenate([pick((slice(None), pl.ds(2048 + at, count))), pick((slice(None), pl.ds(3584 + at, count)))], axis=0)
+    if at == 1408:
+        store_pair(even, a_ref, b_ref, (slice(None), pl.ds(4352, 128)), up[8:], down[8:])
+
+
+def store_rest(even, a_ref, b_ref, at, first, second):
+    row = iota((8, 128), 0)
+    up, down = [jnp.where(row < 3, f[8:], pltpu.roll(s[8:], 3, 0)) for f, s in zip(first, second)]
+    store_pair(even, a_ref, b_ref, (slice(None), pl.ds(3584 + at, 128)), up, down)
+
+
+def load_rows(pick, level, at, count):
+    start = {1: 3584, 2: 3584, 3: 3968, 4: 4352}[level]
+    rest = pick((slice(None), pl.ds(start, count)))
+    if level in (2, 3):
+        rest = pltpu.roll(rest, 5, 0)
+    return jnp.concatenate([pick((slice(None), pl.ds(2048 + at, count))), rest], axis=0)
 
 
 def y_kernel(y0_ref, o_ref, ra_ref, rb_ref, z3_ref, z4_ref, *refs):
@@ -439,6 +452,7 @@
     for k in range(16):
         t = z0_ref[pl.ds(k * 128, 128), :].T
         store_pair(even_z, fa_ref, fb_ref, (slice(None), pl.ds(k * 128, 128)), t[120:], t[:8])
+    firsts, seconds = [], []
     for k in range(6):
         size = 128 if k < 5 else 120
         block = z1_ref[pl.ds(k * 128, size), :]
@@ -446,6 +460,7 @@
             block = jnp.concatenate([block, jnp.zeros((128 - size, 128), F32)], axis=0)
         t = block.T
         store_rows(even_z, fa_ref, fb_ref, k * 128, t[56:72], t[0:16])
+        firsts.append((t[56:72], t[0:16]))
     for level, z_ref, at, f, count in ((2, z2_ref, 768, 24, 312), (3, z3_ref, 1152, 8, 144)):
         for k in range((count + 127) // 128):
             size = min(128, count - k * 128)
@@ -454,6 +469,10 @@
                 block = jnp.concatenate([block, jnp.zeros((128 - size, 128), F32)], axis=0)
             t = block.T
             store_rows(even_z, fa_ref, fb_ref, at + k * 128, t[f : f + 16], t[0:16])
+            seconds.append((t[f : f + 16], t[0:16]))
+    seconds.append(seconds[-1])
+    for k in range(6):
+        store_rest(even_z, fa_ref, fb_ref, k * 128, firsts[k], seconds[k])
     t = level4_rows(z4_ref)
     store_rows(even_z, fa_ref, fb_ref, 1408, t, t)
 
@@ -487,7 +506,7 @@
     total = None
     for level in (4, 3, 2, 1):
         n = Z_ROWS[level]
-        halo = [load_rows(ref, Z_AT[level], (n + 127) // 128 * 128) for ref in (below, above)]
+        halo = [load_rows(ref, level, Z_AT[level], (n + 127) // 128 * 128) for ref in (below, above)]
         if level == 4:
             halo = [below2(...), *halo, above2(...)]
         term = t_refs[level][...] + halo_part(level, jnp.concatenate(halo, axis=0))[:n]
@@ -535,6 +554,10 @@
     )
 
 
+def prepared(body, shapes, taps):
+    return call(body, [(w, BF16) for w in shapes], [SM])(taps)
+
+
 def per_device(charges, kernel_taps):
     taps = kernel_taps
 
@@ -545,7 +568,7 @@
 
     sa, sb, s2, v = call(
         restrict_kernel,
-        [((1000, 128), F32), ((1000, 128), F32), ((2, 24, 128), F32),
+        [((952, 128), F32), ((952, 128), F32), ((2, 24, 128), F32),
          ((8, 16, 384), F32)],
         [VM], [pltpu.VMEM((13, 24, 128), F32)],
     )(charges)
@@ -553,16 +576,18 @@
     rb = swap(sb, "gx", second=True)
     f2 = lax.ppermute(s2, "gx", [(i, i ^ 2) for i in range(4)])
     vs = lax.all_to_all(v, "gy", 0, 0)
-    (u,) = call(coarse_y_kernel, [((48, 128), F32)], [SM, VM])(taps, vs)
+    u, *my = call(
+        coarse_y_kernel, [((48, 128), F32), ((64, 240), BF16), ((40, 240), BF16), ((24, 192), BF16)], [SM, VM]
+    )(taps, vs)
     others = []
-    for by in (1, 3, 2):
-        others.append(lax.ppermute(u, "gx", [(i, (i + by) % 4) for i in range(4)]))
-    mats_shapes = [(64, 240), (40, 240), (24, 192)]
+    for by in (1, 2, 3):
+        others.append(lax.ppermute(u, "gx", [(i, i ^ by) for i in range(4)]))
+    z_shapes = []
     for halo in (16, 32, 32, 32, 64):
-        mats_shapes += [(128, 256), (3 * halo, 128)]
-    mats_shapes += [(PY[l], 2 * up16(PY[l + 1])) for l in range(4)]
-    mats = call(prep_kernel, [(w, BF16) for w in mats_shapes], [SM])(taps)
-    my, own, halo, py = mats[:3], mats[3:13:2], mats[4:13:2], mats[13:]
+        z_shapes += [(128, 256), (3 * halo, 128)]
+    z_shapes += [(PY[l], 2 * up16(PY[l + 1])) for l in range(4)]
+    mats = prepared(prep_z_kernel, z_shapes, taps)
+    own, halo, py = mats[:10:2], mats[1:10:2], mats[10:]
     y0, o, sa, sb, tb = call(
         x_kernel,
         [((32, 64, 128), F32), ((19, 40, 128), F32), ((560, 128), F32), ((560, 128), F32), ((48, 128), F32)],
@@ -578,8 +603,8 @@
     a4 = swap(t4, "gz", 2)
     b4 = swap(t4, "gz", 2, second=True)
     z0, z1, z2, sa, sb = call(
-        y_kernel, [((Z_ROWS[l], 128), F32) for l in range(3)] + [((8, 5120), F32), ((8, 5120), F32)], [VM] * 9
-    )(y0, o, ra, rb, z3, z4, *my[:3])
+        y_kernel, [((Z_ROWS[l], 128), F32) for l in range(3)] + [((8, 4480), F32), ((8, 4480), F32)], [VM] * 9
+    )(y0, o, ra, rb, z3, z4, *my)
     z = (z0, z1, z2, z3, z4)
     ra = swap(sa, "gz")
     rb = swap(sb, "gz", second=True)

time: 59.3 us -> 60.1 us (1.013)
  waiting for transfers between devices: 11 us -> 11.9 us
    ppermute x3, waiting for transfers between devices: 1.9 us -> 3.28 us  [per_device(): others.append(lax.ppermute(u, 'gx', [(i, i ^ by) for i in range(4)]))]
where the time goes in v4:
time: 60.1 us; the launch traced here: 59.7 us
  starting transfers between devices  29.9 us (50%)
  Pallas kernels  12.9 us (21%)
  waiting for transfers between devices  11.9 us (20%)
  local copies, waits for them, and re-layouts  4.87 us (8%)
    ppermute x8, starting transfers between devices, swap(): lax.ppermute(v, axis, [(i, partner(i)) for i in range(count) if 0 <= part...  15.3 us
    all_to_all x1, starting transfers between devices, per_device(): vs = lax.all_to_all(v, 'gy', 0, 0)  5.94 us
    ppermute x8, waiting for transfers between devices, swap(): lax.ppermute(v, axis, [(i, partner(i)) for i in range(count) if 0 <= part...  5.07 us
    unnamed x14, local copies, waits for them, and re-layouts  4.87 us
    ppermute x3, starting transfers between devices, per_device(): others.append(lax.ppermute(u, 'gx', [(i, i ^ by) for i in range(4)]))  4.72 us
    ppermute x1, starting transfers between devices, per_device(): f2 = lax.ppermute(s2, 'gx', [(i, i ^ 2) for i in range(4)])  3.95 us
    pallas_call x1, Pallas kernels, per_device(): call(x_kernel, [((32, 64, 128), F32), ((19, 40, 128), F32), ((560, 128),...  3.53 us
    ppermute x1, waiting for transfers between devices, per_device(): f2 = lax.ppermute(s2, 'gx', [(i, i ^ 2) for i in range(4)])  3.5 us
  transfers between devices with their start and end apart: 13, of which 4 were waited for; matrix products, arithmetic and copies ran while one was open for 0% of the time, Pallas kernels for 13%

profile of v4, /device:TPU:160, one launch (start us, length us, event | category | flops | bytes accessed | tf_op | source)
XLA Modules:
  0.0 59.7 jit_solution(8558196955671069490)
XLA Ops:
  0.0 1.2 %copy-done = f32[32,64,128]{2,1,0:T(8,128)S(1)} copy-done((f32[32,64,128]{2,1,0:T(8,128)S(1)}, f32[32,64,128]{2,1,0:T(8,128)}, u32[]{:S(2)}) %copy-start) | copy-done | bytes 1048600
  1.2 2.2 %shard_map.28 = (f32[952,128]{1,0:T(8,128)S(1)}, f32[952,128]{1,0:T(8,128)S(1)}, f32[2,24,128]{2,1,0:T(8,128)S(1)}, f32[8,16,384]{2,1,0:T(8,128)}) custom-call(f32[32,64,128]{2,1,0:T(8,128)S(1)} %copy-done), custom_call_target="tpu_custom_call" | custom-call | flops 400000000 | bytes 2097152 | tf_op jit(solution)/shard_map/pallas_call | solution.py:569
  3.4 1.5 %collective-permute-start = (f32[952,128]{1,0:T(8,128)S(1)}, f32[952,128]{1,0:T(8,128)S(1)}, u32[]{:S(2)}, u32[]{:S(2)}) collective-permute-start(f32[952,128]{1,0:T(8,128)S(1)} %get-tuple-element.45.sa_ref), channel_id=1, source_target_pairs={{0,64},{64,0},{128,192},{192,128},{1,65},{65,1},{129,193},{193,129... | collective-permute-start | bytes 1462280 | tf_op jit(solution)/shard_map/ppermute | solution.py:567
  5.6 5.9 %all-to-all-start = ((f32[8,16,384]{2,1,0:T(8,128)}), f32[8,16,384]{2,1,0:T(8,128)}, u32[]{:S(2)}, u32[]{:S(2)}) async-start(f32[8,16,384]{2,1,0:T(8,128)} %get-tuple-element.53), calls=%async_computation | async-start | bytes 393216 | tf_op jit(solution)/shard_map/all_to_all | solution.py:578
  11.5 4.0 %collective-permute-start.2 = (f32[2,24,128]{2,1,0:T(8,128)S(1)}, f32[2,24,128]{2,1,0:T(8,128)S(1)}, u32[]{:S(2)}, u32[]{:S(2)}) collective-permute-start(f32[2,24,128]{2,1,0:T(8,128)S(1)} %get-tuple-element.47), channel_id=1, source_target_pairs={{0,128},{64,192},{128,0},{192,64},{1,129},{65,193},{129,1},{193,65... | collective-permute-start | bytes 73736 | tf_op jit(solution)/shard_map/ppermute | solution.py:577
  15.5 3.5 %collective-permute-done.2.f_ref = f32[2,24,128]{2,1,0:T(8,128)S(1)} collective-permute-done((f32[2,24,128]{2,1,0:T(8,128)S(1)}, f32[2,24,128]{2,1,0:T(8,128)S(1)}, u32[]{:S(2)}, u32[]{:S(2)}) %collective-permute-start.2) | collective-permute-done | bytes 24608 | tf_op jit(solution)/shard_map/ppermute | solution.py:577
  20.6 1.0 %copy-done.3 = f32[952,128]{1,0:T(8,128)S(1)} copy-done((f32[952,128]{1,0:T(8,128)S(1)}, f32[952,128]{1,0:T(8,128)}, u32[]{:S(2)}) %copy-start.3) | copy-done | bytes 487448
  21.6 1.0 %copy-done.5 = f32[952,128]{1,0:T(8,128)S(1)} copy-done((f32[952,128]{1,0:T(8,128)S(1)}, f32[952,128]{1,0:T(8,128)}, u32[]{:S(2)}) %copy-start.5) | copy-done | bytes 487448
  22.6 3.5 %shard_map.29 = (f32[32,64,128]{2,1,0:T(8,128)S(1)}, f32[19,40,128]{2,1,0:T(8,128)S(1)}, f32[560,128]{1,0:T(8,128)}, f32[560,128]{1,0:T(8,128)}, f32[48,128]{1,0:T(8,128)S(1)}) custom-call(f32[5,3,17]{2,1,0:T(4,128)S(1)} %copy-done.6, f32[32,64,128]{2,1,0:T(8,128)S(1)} %copy-done.1, f32[952,128]{1,0:T(8,128)S(1)} %get-tuple-element.45.sa_ref, ...), custom_call_target="tpu_custom_call" | custom-call | flops 400000000 | bytes 2097152 | tf_op jit(solution)/shard_map/pallas_call | solution.py:591
  26.2 1.6 %collective-permute-start.3 = (f32[560,128]{1,0:T(8,128)}, f32[560,128]{1,0:T(8,128)S(1)}, u32[]{:S(2)}, u32[]{:S(2)}) collective-permute-start(f32[560,128]{1,0:T(8,128)} %get-tuple-element.50), channel_id=1, source_target_pairs={{0,8},{8,0},{16,24},{24,16},{32,40},{40,32},{48,56},{56,48},{1,9},... | collective-permute-start | bytes 860168 | tf_op jit(solution)/shard_map/ppermute | solution.py:567
  27.7 4.5 %collective-permute-start.4 = (f32[560,128]{1,0:T(8,128)}, f32[560,128]{1,0:T(8,128)S(1)}, u32[]{:S(2)}, u32[]{:S(2)}) collective-permute-start(f32[560,128]{1,0:T(8,128)} %get-tuple-element.51), channel_id=1, source_target_pairs={{8,16},{16,8},{24,32},{32,24},{40,48},{48,40},{9,17},{17,9},{25,33... | collective-permute-start | bytes 860168 | tf_op jit(solution)/shard_map/ppermute | solution.py:567
  32.3 1.4 %shard_map.30 = (f32[48,128]{1,0:T(8,128)S(1)}, bf16[64,240]{1,0:T(8,128)(2,1)S(1)}, bf16[40,240]{1,0:T(8,128)(2,1)S(1)}, bf16[24,192]{1,0:T(8,128)(2,1)S(1)}) custom-call(f32[5,3,17]{2,1,0:T(4,128)S(1)} %copy-done.6, f32[8,16,384]{2,1,0:T(8,128)} %all-to-all-done.v_ref), custom_call_target="tpu_custom_call" | custom-call | flops 400000000 | bytes 2097152 | tf_op jit(solution)/shard_map/pallas_call | solution.py:579
  33.7 1.2 %collective-permute-start.5 = (f32[48,128]{1,0:T(8,128)S(1)}, f32[48,128]{1,0:T(8,128)S(1)}, u32[]{:S(2)}, u32[]{:S(2)}) collective-permute-start(f32[48,128]{1,0:T(8,128)S(1)} %get-tuple-element.54.own_ref), channel_id=1, source_target_pairs={{0,64},{64,0},{128,192},{192,128},{1,65},{65,1},{129,193},{193,129... | collective-permute-start | bytes 73736 | tf_op jit(solution)/shard_map/ppermute | solution.py:584
  34.9 1.7 %collective-permute-start.6 = (f32[48,128]{1,0:T(8,128)S(1)}, f32[48,128]{1,0:T(8,128)S(1)}, u32[]{:S(2)}, u32[]{:S(2)}) collective-permute-start(f32[48,128]{1,0:T(8,128)S(1)} %get-tuple-element.54.own_ref), channel_id=1, source_target_pairs={{0,128},{64,192},{128,0},{192,64},{1,129},{65,193},{129,1},{193,65... | collective-permute-start | bytes 73736 | tf_op jit(solution)/shard_map/ppermute | solution.py:584
  36.6 1.8 %collective-permute-start.7 = (f32[48,128]{1,0:T(8,128)S(1)}, f32[48,128]{1,0:T(8,128)S(1)}, u32[]{:S(2)}, u32[]{:S(2)}) collective-permute-start(f32[48,128]{1,0:T(8,128)S(1)} %get-tuple-element.54.own_ref), channel_id=1, source_target_pairs={{0,192},{64,128},{128,64},{192,0},{1,193},{65,129},{129,65},{193,1... | collective-permute-start | bytes 73736 | tf_op jit(solution)/shard_map/ppermute | solution.py:584
  38.4 1.8 %collective-permute-done.6.r2_ref = f32[48,128]{1,0:T(8,128)S(1)} collective-permute-done((f32[48,128]{1,0:T(8,128)S(1)}, f32[48,128]{1,0:T(8,128)S(1)}, u32[]{:S(2)}, u32[]{:S(2)}) %collective-permute-start.6) | collective-permute-done | bytes 24608 | tf_op jit(solution)/shard_map/ppermute | solution.py:584
  40.2 1.5 %collective-permute-done.7.r3_ref = f32[48,128]{1,0:T(8,128)S(1)} collective-permute-done((f32[48,128]{1,0:T(8,128)S(1)}, f32[48,128]{1,0:T(8,128)S(1)}, u32[]{:S(2)}, u32[]{:S(2)}) %collective-permute-start.7) | collective-permute-done | bytes 24608 | tf_op jit(solution)/shard_map/ppermute | solution.py:584
  42.1 1.0 %shard_map.32 = (f32[2048,128]{1,0:T(8,128)S(1)}, f32[760,128]{1,0:T(8,128)S(1)}, f32[312,128]{1,0:T(8,128)S(1)}, f32[8,4480]{1,0:T(8,128)S(1)}, f32[8,4480]{1,0:T(8,128)S(1)}) custom-call(f32[32,64,128]{2,1,0:T(8,128)S(1)} %get-tuple-element.48.y0_ref, f32[19,40,128]{2,1,0:T(8,128)S(1)} %get-tuple-element.49.o_ref, ...), custom_call_target="tpu_custom_call" | custom-call | flops 400000000 | bytes 2097152 | tf_op jit(solution)/shard_map/pallas_call | solution.py:605
  43.2 1.9 %collective-permute-start.9 = (f32[8,4480]{1,0:T(8,128)S(1)}, f32[8,4480]{1,0:T(8,128)S(1)}, u32[]{:S(2)}, u32[]{:S(2)}) collective-permute-start(f32[8,4480]{1,0:T(8,128)S(1)} %get-tuple-element.74), channel_id=1, source_target_pairs={{1,2},{2,1},{3,4},{4,3},{5,6},{6,5},{9,10},{10,9},{11,12},{12,11},... | collective-permute-start | bytes 430088 | tf_op jit(solution)/shard_map/ppermute | solution.py:567
  45.2 1.7 %shard_map.33 = (bf16[128,256]{1,0:T(8,128)(2,1)S(1)}, bf16[48,128]{1,0:T(8,128)(2,1)S(1)}, bf16[128,256]{1,0:T(8,128)(2,1)S(1)}, bf16[96,128]{1,0:T(8,128)(2,1)...) custom-call(f32[5,3,17]{2,1,0:T(4,128)S(1)} %copy-done.6), custom_call_target="tpu_custom_call" | custom-call | flops 400000000 | bytes 2097152 | tf_op jit(solution)/shard_map/pallas_call | solution.py:558
  46.8 3.1 %collective-permute-start.10 = (f32[16,128]{1,0:T(8,128)S(1)}, f32[16,128]{1,0:T(8,128)S(1)}, u32[]{:S(2)}, u32[]{:S(2)}) collective-permute-start(f32[16,128]{1,0:T(8,128)S(1)} %get-tuple-element.75), channel_id=1, source_target_pairs={{0,2},{1,3},{2,0},{3,1},{4,6},{5,7},{6,4},{7,5},{8,10},{9,11},{10,... | collective-permute-start | bytes 24584 | tf_op jit(solution)/shard_map/ppermute | solution.py:567
  49.9 1.9 %collective-permute-start.11 = (f32[16,128]{1,0:T(8,128)S(1)}, f32[16,128]{1,0:T(8,128)S(1)}, u32[]{:S(2)}, u32[]{:S(2)}) collective-permute-start(f32[16,128]{1,0:T(8,128)S(1)} %get-tuple-element.75), channel_id=1, source_target_pairs={{2,4},{3,5},{4,2},{5,3},{10,12},{11,13},{12,10},{13,11},{18,20},{1... | collective-permute-start | bytes 24584 | tf_op jit(solution)/shard_map/ppermute | solution.py:567
  52.5 5.1 %collective-permute-done.11.refs_8_ = f32[16,128]{1,0:T(8,128)S(1)} collective-permute-done((f32[16,128]{1,0:T(8,128)S(1)}, f32[16,128]{1,0:T(8,128)S(1)}, u32[]{:S(2)}, u32[]{:S(2)}) %collective-permute-start.11) | collective-permute-done | bytes 8224 | tf_op jit(solution)/shard_map/ppermute | solution.py:567
  57.6 2.1 %shard_map.35 = f32[32,64,128]{2,1,0:T(8,128)} custom-call(f32[2048,128]{1,0:T(8,128)S(1)} %get-tuple-element.68.refs_0_, f32[760,128]{1,0:T(8,128)S(1)} %get-tuple-element.69.refs_1_, f32[312,128]{1,0:T(8,128)S(1)} %get-tuple-element.70.refs_2_, f32[144,128]{1,0:T(8,128)S(1)} %get-tuple-element.71.refs_3_, f32[112,128]{1,0:T(8,128)S(1)} %get-tuple-element.72.refs_4_, ...), custom_call_target="tpu_custom_call" | custom-call | flops 400000000 | bytes 2097152 | tf_op jit(solution)/shard_map/pallas_call | solution.py:612
  (24 shorter events, 3.4 us)
Async XLA Ops:
  0.0 1.2 %copy-start = (f32[32,64,128]{2,1,0:T(8,128)S(1)}, f32[32,64,128]{2,1,0:T(8,128)}, u32[]{:S(2)}) copy-start(f32[32,64,128]{2,1,0:T(8,128)} %q_ref.3) | copy-start | bytes 3145732
  1.2 19.3 %copy-start.1 = (f32[32,64,128]{2,1,0:T(8,128)S(1)}, f32[32,64,128]{2,1,0:T(8,128)}, u32[]{:S(2)}) copy-start(f32[32,64,128]{2,1,0:T(8,128)} %q_ref.3) | copy-start | bytes 3145732
  3.4 15.6 %collective-permute-start = (f32[952,128]{1,0:T(8,128)S(1)}, f32[952,128]{1,0:T(8,128)S(1)}, u32[]{:S(2)}, u32[]{:S(2)}) collective-permute-start(f32[952,128]{1,0:T(8,128)S(1)} %get-tuple-element.45.sa_ref), channel_id=1, source_target_pairs={{0,64},{64,0},{128,192},{192,128},{1,65},{65,1},{129,193},{193,129... | collective-permute-start | bytes 1462280 | tf_op jit(solution)/shard_map/ppermute | solution.py:567
  4.9 14.9 %collective-permute-start.1 = (f32[952,128]{1,0:T(8,128)S(1)}, f32[952,128]{1,0:T(8,128)S(1)}, u32[]{:S(2)}, u32[]{:S(2)}) collective-permute-start(f32[952,128]{1,0:T(8,128)S(1)} %get-tuple-element.46.sb_ref), channel_id=1, source_target_pairs={{64,128},{128,64},{65,129},{129,65},{66,130},{130,66},{67,131},{13... | collective-permute-start | bytes 1462280 | tf_op jit(solution)/shard_map/ppermute | solution.py:567
  5.6 15.0 %copy-start.6 = (f32[5,3,17]{2,1,0:T(4,128)S(1)}, f32[5,3,17]{2,1,0:T(4,128)}, u32[]{:S(2)}) copy-start(f32[5,3,17]{2,1,0:T(4,128)} %taps_ref.5) | copy-start | bytes 3064
  5.6 26.7 %all-to-all-start = ((f32[8,16,384]{2,1,0:T(8,128)}), f32[8,16,384]{2,1,0:T(8,128)}, u32[]{:S(2)}, u32[]{:S(2)}) async-start(f32[8,16,384]{2,1,0:T(8,128)} %get-tuple-element.53), calls=%async_computation | async-start | bytes 393216 | tf_op jit(solution)/shard_map/all_to_all | solution.py:578
  11.5 7.5 %collective-permute-start.2 = (f32[2,24,128]{2,1,0:T(8,128)S(1)}, f32[2,24,128]{2,1,0:T(8,128)S(1)}, u32[]{:S(2)}, u32[]{:S(2)}) collective-permute-start(f32[2,24,128]{2,1,0:T(8,128)S(1)} %get-tuple-element.47), channel_id=1, source_target_pairs={{0,128},{64,192},{128,0},{192,64},{1,129},{65,193},{129,1},{193,65... | collective-permute-start | bytes 73736 | tf_op jit(solution)/shard_map/ppermute | solution.py:577
  19.0 0.8 %copy-start.2 = (f32[952,128]{1,0:T(8,128)}, f32[952,128]{1,0:T(8,128)S(1)}, u32[]{:S(2)}) copy-start(f32[952,128]{1,0:T(8,128)S(1)} %collective-permute-done.ra_ref) | copy-start | bytes 1462276
  19.8 0.8 %copy-start.4 = (f32[952,128]{1,0:T(8,128)}, f32[952,128]{1,0:T(8,128)S(1)}, u32[]{:S(2)}) copy-start(f32[952,128]{1,0:T(8,128)S(1)} %collective-permute-done.1.rb_ref) | copy-start | bytes 1462276
  20.6 1.0 %copy-start.3 = (f32[952,128]{1,0:T(8,128)S(1)}, f32[952,128]{1,0:T(8,128)}, u32[]{:S(2)}) copy-start(f32[952,128]{1,0:T(8,128)} %copy-done.2) | copy-start | bytes 1462276
  21.6 1.0 %copy-start.5 = (f32[952,128]{1,0:T(8,128)S(1)}, f32[952,128]{1,0:T(8,128)}, u32[]{:S(2)}) copy-start(f32[952,128]{1,0:T(8,128)} %copy-done.4) | copy-start | bytes 1462276
  26.2 15.9 %collective-permute-start.3 = (f32[560,128]{1,0:T(8,128)}, f32[560,128]{1,0:T(8,128)S(1)}, u32[]{:S(2)}, u32[]{:S(2)}) collective-permute-start(f32[560,128]{1,0:T(8,128)} %get-tuple-element.50), channel_id=1, source_target_pairs={{0,8},{8,0},{16,24},{24,16},{32,40},{40,32},{48,56},{56,48},{1,9},... | collective-permute-start | bytes 860168 | tf_op jit(solution)/shard_map/ppermute | solution.py:567
  27.7 14.3 %collective-permute-start.4 = (f32[560,128]{1,0:T(8,128)}, f32[560,128]{1,0:T(8,128)S(1)}, u32[]{:S(2)}, u32[]{:S(2)}) collective-permute-start(f32[560,128]{1,0:T(8,128)} %get-tuple-element.51), channel_id=1, source_target_pairs={{8,16},{16,8},{24,32},{32,24},{40,48},{48,40},{9,17},{17,9},{25,33... | collective-permute-start | bytes 860168 | tf_op jit(solution)/shard_map/ppermute | solution.py:567
  33.7 4.7 %collective-permute-start.5 = (f32[48,128]{1,0:T(8,128)S(1)}, f32[48,128]{1,0:T(8,128)S(1)}, u32[]{:S(2)}, u32[]{:S(2)}) collective-permute-start(f32[48,128]{1,0:T(8,128)S(1)} %get-tuple-element.54.own_ref), channel_id=1, source_target_pairs={{0,64},{64,0},{128,192},{192,128},{1,65},{65,1},{129,193},{193,129... | collective-permute-start | bytes 73736 | tf_op jit(solution)/shard_map/ppermute | solution.py:584
  34.9 5.3 %collective-permute-start.6 = (f32[48,128]{1,0:T(8,128)S(1)}, f32[48,128]{1,0:T(8,128)S(1)}, u32[]{:S(2)}, u32[]{:S(2)}) collective-permute-start(f32[48,128]{1,0:T(8,128)S(1)} %get-tuple-element.54.own_ref), channel_id=1, source_target_pairs={{0,128},{64,192},{128,0},{192,64},{1,129},{65,193},{129,1},{193,65... | collective-permute-start | bytes 73736 | tf_op jit(solution)/shard_map/ppermute | solution.py:584
  36.6 5.0 %collective-permute-start.7 = (f32[48,128]{1,0:T(8,128)S(1)}, f32[48,128]{1,0:T(8,128)S(1)}, u32[]{:S(2)}, u32[]{:S(2)}) collective-permute-start(f32[48,128]{1,0:T(8,128)S(1)} %get-tuple-element.54.own_ref), channel_id=1, source_target_pairs={{0,192},{64,128},{128,64},{192,0},{1,193},{65,129},{129,65},{193,1... | collective-permute-start | bytes 73736 | tf_op jit(solution)/shard_map/ppermute | solution.py:584
  43.1 14.5 %collective-permute-start.8 = (f32[8,4480]{1,0:T(8,128)S(1)}, f32[8,4480]{1,0:T(8,128)S(1)}, u32[]{:S(2)}, u32[]{:S(2)}) collective-permute-start(f32[8,4480]{1,0:T(8,128)S(1)} %get-tuple-element.73), channel_id=1, source_target_pairs={{0,1},{1,0},{2,3},{3,2},{4,5},{5,4},{6,7},{7,6},{8,9},{9,8},{10,11... | collective-permute-start | bytes 430088 | tf_op jit(solution)/shard_map/ppermute | solution.py:567
  43.2 14.4 %collective-permute-start.9 = (f32[8,4480]{1,0:T(8,128)S(1)}, f32[8,4480]{1,0:T(8,128)S(1)}, u32[]{:S(2)}, u32[]{:S(2)}) collective-permute-start(f32[8,4480]{1,0:T(8,128)S(1)} %get-tuple-element.74), channel_id=1, source_target_pairs={{1,2},{2,1},{3,4},{4,3},{5,6},{6,5},{9,10},{10,9},{11,12},{12,11},... | collective-permute-start | bytes 430088 | tf_op jit(solution)/shard_map/ppermute | solution.py:567
  46.8 5.7 %collective-permute-start.10 = (f32[16,128]{1,0:T(8,128)S(1)}, f32[16,128]{1,0:T(8,128)S(1)}, u32[]{:S(2)}, u32[]{:S(2)}) collective-permute-start(f32[16,128]{1,0:T(8,128)S(1)} %get-tuple-element.75), channel_id=1, source_target_pairs={{0,2},{1,3},{2,0},{3,1},{4,6},{5,7},{6,4},{7,5},{8,10},{9,11},{10,... | collective-permute-start | bytes 24584 | tf_op jit(solution)/shard_map/ppermute | solution.py:567
  49.9 7.6 %collective-permute-start.11 = (f32[16,128]{1,0:T(8,128)S(1)}, f32[16,128]{1,0:T(8,128)S(1)}, u32[]{:S(2)}, u32[]{:S(2)}) collective-permute-start(f32[16,128]{1,0:T(8,128)S(1)} %get-tuple-element.75), channel_id=1, source_target_pairs={{2,4},{3,5},{4,2},{5,3},{10,12},{11,13},{12,10},{13,11},{18,20},{1... | collective-permute-start | bytes 24584 | tf_op jit(solution)/shard_map/ppermute | solution.py:567

commit v5 on v3

--- a/solution.py
+++ b/solution.py
@@ -167,10 +167,12 @@
     for s in range(11):
         up, down = kept[1][s + EX[1] - 11], kept[1][s]
         store_pair(even, sa_ref, sb_ref, pl.ds(512 + s * 40, 24), jnp.where(low, up[:24], kept[2][s]), jnp.where(low, down[:24], kept[2][s]))
-        store_pair(even, sa_ref, sb_ref, pl.ds(512 + s * 40 + 24, 16), up[24:], down[24:])
-    for s in range(11, EX[2]):
-        for ref in (sa_ref, sb_ref):
-            ref[pl.ds(952 + (s - 11) * 24, 24), :] = kept[2][s]
+        up, down = up[24:], down[24:]
+        if s < 6:
+            k, at = divmod(s, 3)
+            extra = jnp.concatenate([kept[2][11 + k][at * 8 : at * 8 + 8], jnp.zeros((8, 128), F32)], axis=0)
+            up, down = jnp.where(low, up, extra), jnp.where(low, down, extra)
+        store_pair(even, sa_ref, sb_ref, pl.ds(512 + s * 40 + 24, 16), up, down)
     start = jnp.where(ix < 2, 8, 0)
     mask = lanes_mask(OZ[2], EZ[2])
     for k, members in enumerate(FAR):
@@ -234,7 +236,9 @@
     def received(ref, at, rows):
         if not 0 <= at < (11 if rows == 40 else 13):
             return None
-        return ref(pl.ds(512 + at * 40 if at < 11 else 952 + (at - 11) * 24, rows))
+        if at < 11:
+            return ref(pl.ds(512 + at * 40, rows))
+        return jnp.concatenate([ref(pl.ds(512 + ((at - 11) * 3 + k) * 40 + 24, 8)) for k in range(3)], axis=0)
 
     def added(values):
         values = [v for v in values if v is not None]
@@ -295,12 +299,12 @@
             u_ref[pl.ds(c // 8, 16), :] = out[:, c - first : c - first + 128]
 
 
-def coarse_kernel(taps_ref, own_ref, low_ref, high_ref, far_ref, z3_ref, z4_ref, t4_ref, g3, g4):
+def coarse_kernel(taps_ref, own_ref, r1_ref, r2_ref, r3_ref, z3_ref, z4_ref, t4_ref, g3, g4):
     ix = lax.axis_index("gx")
     for g in (g3, g4):
         g[...] = jnp.zeros_like(g)
-    for ref, step in ((own_ref, 0), (low_ref, 3), (high_ref, 1), (far_ref, 2)):
-        source = (ix + step) & 3
+    for ref, step in ((own_ref, 0), (r1_ref, 1), (r2_ref, 2), (r3_ref, 3)):
+        source = ix ^ step
         for c, (level, members) in enumerate(V_COLUMNS):
             g = g3 if level == 3 else g4
             column = ref[pl.ds(c * 16, 16), :]
@@ -341,12 +345,8 @@
     halo_ref[...] = jnp.concatenate([hi, hi, lo], axis=0)
 
 
-def prep_kernel(taps_ref, *out):
+def prep_y_kernel(taps_ref, *outs):
     iy = lax.axis_index("gy")
-    iz = lax.axis_index("gz")
-    outs = out[:3]
-    z_outs = [out[3 + 2 * k : 5 + 2 * k] for k in range(5)]
-
     for level, width, ref in ((0, 80, outs[0]), (1, 80, outs[1]), (2, 64, outs[2])):
         shape = (PY[level], 3 * width)
         i, j = iota(shape, 0), repeated(iota(shape, 1), width)
@@ -368,13 +368,19 @@
                 ),
             )
         ref[...] = thirds(toeplitz(taps_ref, level, 1, at - to + 8), width)
+
+
+def prep_z_kernel(taps_ref, *out):
+    iy = lax.axis_index("gy")
+    iz = lax.axis_index("gz")
+    z_outs = [out[2 * k : 2 * k + 2] for k in range(5)]
     j = iota((128, 128), 0)
     c = iota((128, 128), 1)
     own = toeplitz(taps_ref, 0, 2, j - c + 8)
     j, c = iota((16, 128), 0), iota((16, 128), 1)
     store_z(*z_outs[0], own, toeplitz(taps_ref, 0, 2, jnp.where(j < 8, j - 8, j - 8 + 128) - c + 8))
     for level in range(4):
-        out[13 + level][...] = prolong_y(level, iy)
+        out[10 + level][...] = prolong_y(level, iy)
     prolong = None
     for level in range(1, 5):
         shape = (128, 128)
@@ -535,6 +541,10 @@
     )
 
 
+def prepared(body, shapes, taps):
+    return call(body, [(w, BF16) for w in shapes], [SM])(taps)
+
+
 def per_device(charges, kernel_taps):
     taps = kernel_taps
 
@@ -545,7 +555,7 @@
 
     sa, sb, s2, v = call(
         restrict_kernel,
-        [((1000, 128), F32), ((1000, 128), F32), ((2, 24, 128), F32),
+        [((952, 128), F32), ((952, 128), F32), ((2, 24, 128), F32),
          ((8, 16, 384), F32)],
         [VM], [pltpu.VMEM((13, 24, 128), F32)],
     )(charges)
@@ -555,14 +565,15 @@
     vs = lax.all_to_all(v, "gy", 0, 0)
     (u,) = call(coarse_y_kernel, [((48, 128), F32)], [SM, VM])(taps, vs)
     others = []
-    for by in (1, 3, 2):
-        others.append(lax.ppermute(u, "gx", [(i, (i + by) % 4) for i in range(4)]))
-    mats_shapes = [(64, 240), (40, 240), (24, 192)]
+    for by in (1, 2, 3):
+        others.append(lax.ppermute(u, "gx", [(i, i ^ by) for i in range(4)]))
+    my = prepared(prep_y_kernel, [(64, 240), (40, 240), (24, 192)], taps)
+    z_shapes = []
     for halo in (16, 32, 32, 32, 64):
-        mats_shapes += [(128, 256), (3 * halo, 128)]
-    mats_shapes += [(PY[l], 2 * up16(PY[l + 1])) for l in range(4)]
-    mats = call(prep_kernel, [(w, BF16) for w in mats_shapes], [SM])(taps)
-    my, own, halo, py = mats[:3], mats[3:13:2], mats[4:13:2], mats[13:]
+        z_shapes += [(128, 256), (3 * halo, 128)]
+    z_shapes += [(PY[l], 2 * up16(PY[l + 1])) for l in range(4)]
+    mats = prepared(prep_z_kernel, z_shapes, taps)
+    own, halo, py = mats[:10:2], mats[1:10:2], mats[10:]
     y0, o, sa, sb, tb = call(
         x_kernel,
         [((32, 64, 128), F32), ((19, 40, 128), F32), ((560, 128), F32), ((560, 128), F32), ((48, 128), F32)],
@@ -579,7 +590,7 @@
     b4 = swap(t4, "gz", 2, second=True)
     z0, z1, z2, sa, sb = call(
         y_kernel, [((Z_ROWS[l], 128), F32) for l in range(3)] + [((8, 5120), F32), ((8, 5120), F32)], [VM] * 9
-    )(y0, o, ra, rb, z3, z4, *my[:3])
+    )(y0, o, ra, rb, z3, z4, *my)
     z = (z0, z1, z2, z3, z4)
     ra = swap(sa, "gz")
     rb = swap(sb, "gz", second=True)

time: 59.3 us -> 59.9 us (1.010)
  Pallas kernels: 12.8 us -> 13.6 us
    pallas_call x2 -> x3, Pallas kernels: 3.94 us -> 4.77 us  [the longest x2 2.61 us: prepared(): return call(body, [(w, BF16) for w in shapes], [SM])(taps)]
  transfers between devices with their start and end apart: 13 -> 13, of which waited for: 4 -> 4; matrix products, arithmetic and copies ran while one was open for 0% -> 0% of each run, Pallas kernels for 13% -> 14%
where the time goes in v5:
time: 59.9 us; the launch traced here: 59.4 us
  starting transfers between devices  29.9 us (50%)
  Pallas kernels  13.6 us (23%)
  waiting for transfers between devices  10.9 us (18%)
  local copies, waits for them, and re-layouts  4.87 us (8%)
    ppermute x8, starting transfers between devices, swap(): lax.ppermute(v, axis, [(i, partner(i)) for i in range(count) if 0 <= part...  15.3 us
    all_to_all x1, starting transfers between devices, per_device(): vs = lax.all_to_all(v, 'gy', 0, 0)  5.94 us
    ppermute x8, waiting for transfers between devices, swap(): lax.ppermute(v, axis, [(i, partner(i)) for i in range(count) if 0 <= part...  5.08 us
    unnamed x14, local copies, waits for them, and re-layouts  4.87 us
    ppermute x3, starting transfers between devices, per_device(): others.append(lax.ppermute(u, 'gx', [(i, i ^ by) for i in range(4)]))  4.72 us
    ppermute x1, starting transfers between devices, per_device(): f2 = lax.ppermute(s2, 'gx', [(i, i ^ 2) for i in range(4)])  3.95 us
    pallas_call x1, Pallas kernels, per_device(): call(x_kernel, [((32, 64, 128), F32), ((19, 40, 128), F32), ((560, 128),...  3.53 us
    ppermute x1, waiting for transfers between devices, per_device(): f2 = lax.ppermute(s2, 'gx', [(i, i ^ 2) for i in range(4)])  3.5 us
  transfers between devices with their start and end apart: 13, of which 4 were waited for; matrix products, arithmetic and copies ran while one was open for 0% of the time, Pallas kernels for 14%

profile of v5, /device:TPU:160, one launch (start us, length us, event | category | flops | bytes accessed | tf_op | source)
XLA Modules:
  0.0 59.4 jit_solution(7681271907372119346)
XLA Ops:
  0.0 1.2 %copy-done = f32[32,64,128]{2,1,0:T(8,128)S(1)} copy-done((f32[32,64,128]{2,1,0:T(8,128)S(1)}, f32[32,64,128]{2,1,0:T(8,128)}, u32[]{:S(2)}) %copy-start) | copy-done | bytes 1048600
  1.2 2.2 %shard_map.28 = (f32[952,128]{1,0:T(8,128)S(1)}, f32[952,128]{1,0:T(8,128)S(1)}, f32[2,24,128]{2,1,0:T(8,128)S(1)}, f32[8,16,384]{2,1,0:T(8,128)}) custom-call(f32[32,64,128]{2,1,0:T(8,128)S(1)} %copy-done), custom_call_target="tpu_custom_call" | custom-call | flops 400000000 | bytes 2097152 | tf_op jit(solution)/shard_map/pallas_call | solution.py:556
  3.4 1.5 %collective-permute-start = (f32[952,128]{1,0:T(8,128)S(1)}, f32[952,128]{1,0:T(8,128)S(1)}, u32[]{:S(2)}, u32[]{:S(2)}) collective-permute-start(f32[952,128]{1,0:T(8,128)S(1)} %get-tuple-element.44.sa_ref), channel_id=1, source_target_pairs={{0,64},{64,0},{128,192},{192,128},{1,65},{65,1},{129,193},{193,129... | collective-permute-start | bytes 1462280 | tf_op jit(solution)/shard_map/ppermute | solution.py:554
  5.6 5.9 %all-to-all-start = ((f32[8,16,384]{2,1,0:T(8,128)}), f32[8,16,384]{2,1,0:T(8,128)}, u32[]{:S(2)}, u32[]{:S(2)}) async-start(f32[8,16,384]{2,1,0:T(8,128)} %get-tuple-element.52), calls=%async_computation | async-start | bytes 393216 | tf_op jit(solution)/shard_map/all_to_all | solution.py:565
  11.5 4.0 %collective-permute-start.2 = (f32[2,24,128]{2,1,0:T(8,128)S(1)}, f32[2,24,128]{2,1,0:T(8,128)S(1)}, u32[]{:S(2)}, u32[]{:S(2)}) collective-permute-start(f32[2,24,128]{2,1,0:T(8,128)S(1)} %get-tuple-element.46), channel_id=1, source_target_pairs={{0,128},{64,192},{128,0},{192,64},{1,129},{65,193},{129,1},{193,65... | collective-permute-start | bytes 73736 | tf_op jit(solution)/shard_map/ppermute | solution.py:564
  15.5 3.5 %collective-permute-done.2.f_ref = f32[2,24,128]{2,1,0:T(8,128)S(1)} collective-permute-done((f32[2,24,128]{2,1,0:T(8,128)S(1)}, f32[2,24,128]{2,1,0:T(8,128)S(1)}, u32[]{:S(2)}, u32[]{:S(2)}) %collective-permute-start.2) | collective-permute-done | bytes 24608 | tf_op jit(solution)/shard_map/ppermute | solution.py:564
  20.6 1.0 %copy-done.3 = f32[952,128]{1,0:T(8,128)S(1)} copy-done((f32[952,128]{1,0:T(8,128)S(1)}, f32[952,128]{1,0:T(8,128)}, u32[]{:S(2)}) %copy-start.3) | copy-done | bytes 487448
  21.6 1.0 %copy-done.5 = f32[952,128]{1,0:T(8,128)S(1)} copy-done((f32[952,128]{1,0:T(8,128)S(1)}, f32[952,128]{1,0:T(8,128)}, u32[]{:S(2)}) %copy-start.5) | copy-done | bytes 487448
  22.6 3.5 %shard_map.29 = (f32[32,64,128]{2,1,0:T(8,128)S(1)}, f32[19,40,128]{2,1,0:T(8,128)S(1)}, f32[560,128]{1,0:T(8,128)}, f32[560,128]{1,0:T(8,128)}, f32[48,128]{1,0:T(8,128)S(1)}) custom-call(f32[5,3,17]{2,1,0:T(4,128)S(1)} %copy-done.6, f32[32,64,128]{2,1,0:T(8,128)S(1)} %copy-done.1, f32[952,128]{1,0:T(8,128)S(1)} %get-tuple-element.44.sa_ref, ...), custom_call_target="tpu_custom_call" | custom-call | flops 400000000 | bytes 2097152 | tf_op jit(solution)/shard_map/pallas_call | solution.py:577
  26.2 1.6 %collective-permute-start.3 = (f32[560,128]{1,0:T(8,128)}, f32[560,128]{1,0:T(8,128)S(1)}, u32[]{:S(2)}, u32[]{:S(2)}) collective-permute-start(f32[560,128]{1,0:T(8,128)} %get-tuple-element.49), channel_id=1, source_target_pairs={{0,8},{8,0},{16,24},{24,16},{32,40},{40,32},{48,56},{56,48},{1,9},... | collective-permute-start | bytes 860168 | tf_op jit(solution)/shard_map/ppermute | solution.py:554
  27.7 4.5 %collective-permute-start.4 = (f32[560,128]{1,0:T(8,128)}, f32[560,128]{1,0:T(8,128)S(1)}, u32[]{:S(2)}, u32[]{:S(2)}) collective-permute-start(f32[560,128]{1,0:T(8,128)} %get-tuple-element.50), channel_id=1, source_target_pairs={{8,16},{16,8},{24,32},{32,24},{40,48},{48,40},{9,17},{17,9},{25,33... | collective-permute-start | bytes 860168 | tf_op jit(solution)/shard_map/ppermute | solution.py:554
  32.3 1.2 %shard_map.30.own_ref = f32[48,128]{1,0:T(8,128)S(1)} custom-call(f32[5,3,17]{2,1,0:T(4,128)S(1)} %copy-done.6, f32[8,16,384]{2,1,0:T(8,128)} %all-to-all-done.v_ref), custom_call_target="tpu_custom_call" | custom-call | flops 400000000 | bytes 2097152 | tf_op jit(solution)/shard_map/pallas_call | solution.py:566
  33.4 1.2 %collective-permute-start.5 = (f32[48,128]{1,0:T(8,128)S(1)}, f32[48,128]{1,0:T(8,128)S(1)}, u32[]{:S(2)}, u32[]{:S(2)}) collective-permute-start(f32[48,128]{1,0:T(8,128)S(1)} %shard_map.30.own_ref), channel_id=1, source_target_pairs={{0,64},{64,0},{128,192},{192,128},{1,65},{65,1},{129,193},{193,129... | collective-permute-start | bytes 73736 | tf_op jit(solution)/shard_map/ppermute | solution.py:569
  34.7 1.7 %collective-permute-start.6 = (f32[48,128]{1,0:T(8,128)S(1)}, f32[48,128]{1,0:T(8,128)S(1)}, u32[]{:S(2)}, u32[]{:S(2)}) collective-permute-start(f32[48,128]{1,0:T(8,128)S(1)} %shard_map.30.own_ref), channel_id=1, source_target_pairs={{0,128},{64,192},{128,0},{192,64},{1,129},{65,193},{129,1},{193,65... | collective-permute-start | bytes 73736 | tf_op jit(solution)/shard_map/ppermute | solution.py:569
  36.4 1.8 %collective-permute-start.7 = (f32[48,128]{1,0:T(8,128)S(1)}, f32[48,128]{1,0:T(8,128)S(1)}, u32[]{:S(2)}, u32[]{:S(2)}) collective-permute-start(f32[48,128]{1,0:T(8,128)S(1)} %shard_map.30.own_ref), channel_id=1, source_target_pairs={{0,192},{64,128},{128,64},{192,0},{1,193},{65,129},{129,65},{193,1... | collective-permute-start | bytes 73736 | tf_op jit(solution)/shard_map/ppermute | solution.py:569
  38.2 0.9 %shard_map.32 = (bf16[64,240]{1,0:T(8,128)(2,1)S(1)}, bf16[40,240]{1,0:T(8,128)(2,1)S(1)}, bf16[24,192]{1,0:T(8,128)(2,1)S(1)}) custom-call(f32[5,3,17]{2,1,0:T(4,128)S(1)} %copy-done.6), custom_call_target="tpu_custom_call" | custom-call | flops 400000000 | bytes 2097152 | tf_op jit(solution)/shard_map/pallas_call | solution.py:545
  40.0 1.5 %collective-permute-done.7.r3_ref = f32[48,128]{1,0:T(8,128)S(1)} collective-permute-done((f32[48,128]{1,0:T(8,128)S(1)}, f32[48,128]{1,0:T(8,128)S(1)}, u32[]{:S(2)}, u32[]{:S(2)}) %collective-permute-start.7) | collective-permute-done | bytes 24608 | tf_op jit(solution)/shard_map/ppermute | solution.py:569
  41.9 1.0 %shard_map.33 = (f32[2048,128]{1,0:T(8,128)S(1)}, f32[760,128]{1,0:T(8,128)S(1)}, f32[312,128]{1,0:T(8,128)S(1)}, f32[8,5120]{1,0:T(8,128)S(1)}, f32[8,5120]{1,0:T(8,128)S(1)}) custom-call(f32[32,64,128]{2,1,0:T(8,128)S(1)} %get-tuple-element.47.y0_ref, f32[19,40,128]{2,1,0:T(8,128)S(1)} %get-tuple-element.48.o_ref, ...), custom_call_target="tpu_custom_call" | custom-call | flops 400000000 | bytes 2097152 | tf_op jit(solution)/shard_map/pallas_call | solution.py:591
  43.0 1.9 %collective-permute-start.9 = (f32[8,5120]{1,0:T(8,128)S(1)}, f32[8,5120]{1,0:T(8,128)S(1)}, u32[]{:S(2)}, u32[]{:S(2)}) collective-permute-start(f32[8,5120]{1,0:T(8,128)S(1)} %get-tuple-element.72), channel_id=1, source_target_pairs={{1,2},{2,1},{3,4},{4,3},{5,6},{6,5},{9,10},{10,9},{11,12},{12,11},... | collective-permute-start | bytes 491528 | tf_op jit(solution)/shard_map/ppermute | solution.py:554
  44.9 1.7 %shard_map.34 = (bf16[128,256]{1,0:T(8,128)(2,1)S(1)}, bf16[48,128]{1,0:T(8,128)(2,1)S(1)}, bf16[128,256]{1,0:T(8,128)(2,1)S(1)}, bf16[96,128]{1,0:T(8,128)(2,1)...) custom-call(f32[5,3,17]{2,1,0:T(4,128)S(1)} %copy-done.6), custom_call_target="tpu_custom_call" | custom-call | flops 400000000 | bytes 2097152 | tf_op jit(solution)/shard_map/pallas_call | solution.py:545
  46.6 3.1 %collective-permute-start.10 = (f32[16,128]{1,0:T(8,128)S(1)}, f32[16,128]{1,0:T(8,128)S(1)}, u32[]{:S(2)}, u32[]{:S(2)}) collective-permute-start(f32[16,128]{1,0:T(8,128)S(1)} %get-tuple-element.73), channel_id=1, source_target_pairs={{0,2},{1,3},{2,0},{3,1},{4,6},{5,7},{6,4},{7,5},{8,10},{9,11},{10,... | collective-permute-start | bytes 24584 | tf_op jit(solution)/shard_map/ppermute | solution.py:554
  49.7 1.9 %collective-permute-start.11 = (f32[16,128]{1,0:T(8,128)S(1)}, f32[16,128]{1,0:T(8,128)S(1)}, u32[]{:S(2)}, u32[]{:S(2)}) collective-permute-start(f32[16,128]{1,0:T(8,128)S(1)} %get-tuple-element.73), channel_id=1, source_target_pairs={{2,4},{3,5},{4,2},{5,3},{10,12},{11,13},{12,10},{13,11},{18,20},{1... | collective-permute-start | bytes 24584 | tf_op jit(solution)/shard_map/ppermute | solution.py:554
  52.3 5.1 %collective-permute-done.11.refs_8_ = f32[16,128]{1,0:T(8,128)S(1)} collective-permute-done((f32[16,128]{1,0:T(8,128)S(1)}, f32[16,128]{1,0:T(8,128)S(1)}, u32[]{:S(2)}, u32[]{:S(2)}) %collective-permute-start.11) | collective-permute-done | bytes 8224 | tf_op jit(solution)/shard_map/ppermute | solution.py:554
  57.3 2.1 %shard_map.36 = f32[32,64,128]{2,1,0:T(8,128)} custom-call(f32[2048,128]{1,0:T(8,128)S(1)} %get-tuple-element.66.refs_0_, f32[760,128]{1,0:T(8,128)S(1)} %get-tuple-element.67.refs_1_, f32[312,128]{1,0:T(8,128)S(1)} %get-tuple-element.68.refs_2_, f32[144,128]{1,0:T(8,128)S(1)} %get-tuple-element.69.refs_3_, f32[112,128]{1,0:T(8,128)S(1)} %get-tuple-element.70.refs_4_, ...), custom_call_target="tpu_custom_call" | custom-call | flops 400000000 | bytes 2097152 | tf_op jit(solution)/shard_map/pallas_call | solution.py:598
  (25 shorter events, 4.3 us)
Async XLA Ops:
  0.0 1.2 %copy-start = (f32[32,64,128]{2,1,0:T(8,128)S(1)}, f32[32,64,128]{2,1,0:T(8,128)}, u32[]{:S(2)}) copy-start(f32[32,64,128]{2,1,0:T(8,128)} %q_ref.3) | copy-start | bytes 3145732
  1.2 19.3 %copy-start.1 = (f32[32,64,128]{2,1,0:T(8,128)S(1)}, f32[32,64,128]{2,1,0:T(8,128)}, u32[]{:S(2)}) copy-start(f32[32,64,128]{2,1,0:T(8,128)} %q_ref.3) | copy-start | bytes 3145732
  3.4 15.6 %collective-permute-start = (f32[952,128]{1,0:T(8,128)S(1)}, f32[952,128]{1,0:T(8,128)S(1)}, u32[]{:S(2)}, u32[]{:S(2)}) collective-permute-start(f32[952,128]{1,0:T(8,128)S(1)} %get-tuple-element.44.sa_ref), channel_id=1, source_target_pairs={{0,64},{64,0},{128,192},{192,128},{1,65},{65,1},{129,193},{193,129... | collective-permute-start | bytes 1462280 | tf_op jit(solution)/shard_map/ppermute | solution.py:554
  4.9 14.9 %collective-permute-start.1 = (f32[952,128]{1,0:T(8,128)S(1)}, f32[952,128]{1,0:T(8,128)S(1)}, u32[]{:S(2)}, u32[]{:S(2)}) collective-permute-start(f32[952,128]{1,0:T(8,128)S(1)} %get-tuple-element.45.sb_ref), channel_id=1, source_target_pairs={{64,128},{128,64},{65,129},{129,65},{66,130},{130,66},{67,131},{13... | collective-permute-start | bytes 1462280 | tf_op jit(solution)/shard_map/ppermute | solution.py:554
  5.6 15.0 %copy-start.6 = (f32[5,3,17]{2,1,0:T(4,128)S(1)}, f32[5,3,17]{2,1,0:T(4,128)}, u32[]{:S(2)}) copy-start(f32[5,3,17]{2,1,0:T(4,128)} %taps_ref.7) | copy-start | bytes 3064
  5.6 26.7 %all-to-all-start = ((f32[8,16,384]{2,1,0:T(8,128)}), f32[8,16,384]{2,1,0:T(8,128)}, u32[]{:S(2)}, u32[]{:S(2)}) async-start(f32[8,16,384]{2,1,0:T(8,128)} %get-tuple-element.52), calls=%async_computation | async-start | bytes 393216 | tf_op jit(solution)/shard_map/all_to_all | solution.py:565
  11.5 7.5 %collective-permute-start.2 = (f32[2,24,128]{2,1,0:T(8,128)S(1)}, f32[2,24,128]{2,1,0:T(8,128)S(1)}, u32[]{:S(2)}, u32[]{:S(2)}) collective-permute-start(f32[2,24,128]{2,1,0:T(8,128)S(1)} %get-tuple-element.46), channel_id=1, source_target_pairs={{0,128},{64,192},{128,0},{192,64},{1,129},{65,193},{129,1},{193,65... | collective-permute-start | bytes 73736 | tf_op jit(solution)/shard_map/ppermute | solution.py:564
  19.0 0.8 %copy-start.2 = (f32[952,128]{1,0:T(8,128)}, f32[952,128]{1,0:T(8,128)S(1)}, u32[]{:S(2)}) copy-start(f32[952,128]{1,0:T(8,128)S(1)} %collective-permute-done.ra_ref) | copy-start | bytes 1462276
  19.8 0.8 %copy-start.4 = (f32[952,128]{1,0:T(8,128)}, f32[952,128]{1,0:T(8,128)S(1)}, u32[]{:S(2)}) copy-start(f32[952,128]{1,0:T(8,128)S(1)} %collective-permute-done.1.rb_ref) | copy-start | bytes 1462276
  20.6 1.0 %copy-start.3 = (f32[952,128]{1,0:T(8,128)S(1)}, f32[952,128]{1,0:T(8,128)}, u32[]{:S(2)}) copy-start(f32[952,128]{1,0:T(8,128)} %copy-done.2) | copy-start | bytes 1462276
  21.6 1.0 %copy-start.5 = (f32[952,128]{1,0:T(8,128)S(1)}, f32[952,128]{1,0:T(8,128)}, u32[]{:S(2)}) copy-start(f32[952,128]{1,0:T(8,128)} %copy-done.4) | copy-start | bytes 1462276
  26.2 15.7 %collective-permute-start.3 = (f32[560,128]{1,0:T(8,128)}, f32[560,128]{1,0:T(8,128)S(1)}, u32[]{:S(2)}, u32[]{:S(2)}) collective-permute-start(f32[560,128]{1,0:T(8,128)} %get-tuple-element.49), channel_id=1, source_target_pairs={{0,8},{8,0},{16,24},{24,16},{32,40},{40,32},{48,56},{56,48},{1,9},... | collective-permute-start | bytes 860168 | tf_op jit(solution)/shard_map/ppermute | solution.py:554
  27.7 14.1 %collective-permute-start.4 = (f32[560,128]{1,0:T(8,128)}, f32[560,128]{1,0:T(8,128)S(1)}, u32[]{:S(2)}, u32[]{:S(2)}) collective-permute-start(f32[560,128]{1,0:T(8,128)} %get-tuple-element.50), channel_id=1, source_target_pairs={{8,16},{16,8},{24,32},{32,24},{40,48},{48,40},{9,17},{17,9},{25,33... | collective-permute-start | bytes 860168 | tf_op jit(solution)/shard_map/ppermute | solution.py:554
  33.4 5.7 %collective-permute-start.5 = (f32[48,128]{1,0:T(8,128)S(1)}, f32[48,128]{1,0:T(8,128)S(1)}, u32[]{:S(2)}, u32[]{:S(2)}) collective-permute-start(f32[48,128]{1,0:T(8,128)S(1)} %shard_map.30.own_ref), channel_id=1, source_target_pairs={{0,64},{64,0},{128,192},{192,128},{1,65},{65,1},{129,193},{193,129... | collective-permute-start | bytes 73736 | tf_op jit(solution)/shard_map/ppermute | solution.py:569
  34.7 5.3 %collective-permute-start.6 = (f32[48,128]{1,0:T(8,128)S(1)}, f32[48,128]{1,0:T(8,128)S(1)}, u32[]{:S(2)}, u32[]{:S(2)}) collective-permute-start(f32[48,128]{1,0:T(8,128)S(1)} %shard_map.30.own_ref), channel_id=1, source_target_pairs={{0,128},{64,192},{128,0},{192,64},{1,129},{65,193},{129,1},{193,65... | collective-permute-start | bytes 73736 | tf_op jit(solution)/shard_map/ppermute | solution.py:569
  36.4 5.0 %collective-permute-start.7 = (f32[48,128]{1,0:T(8,128)S(1)}, f32[48,128]{1,0:T(8,128)S(1)}, u32[]{:S(2)}, u32[]{:S(2)}) collective-permute-start(f32[48,128]{1,0:T(8,128)S(1)} %shard_map.30.own_ref), channel_id=1, source_target_pairs={{0,192},{64,128},{128,64},{192,0},{1,193},{65,129},{129,65},{193,1... | collective-permute-start | bytes 73736 | tf_op jit(solution)/shard_map/ppermute | solution.py:569
  42.9 14.5 %collective-permute-start.8 = (f32[8,5120]{1,0:T(8,128)S(1)}, f32[8,5120]{1,0:T(8,128)S(1)}, u32[]{:S(2)}, u32[]{:S(2)}) collective-permute-start(f32[8,5120]{1,0:T(8,128)S(1)} %get-tuple-element.71), channel_id=1, source_target_pairs={{0,1},{1,0},{2,3},{3,2},{4,5},{5,4},{6,7},{7,6},{8,9},{9,8},{10,11... | collective-permute-start | bytes 491528 | tf_op jit(solution)/shard_map/ppermute | solution.py:554
  43.0 14.4 %collective-permute-start.9 = (f32[8,5120]{1,0:T(8,128)S(1)}, f32[8,5120]{1,0:T(8,128)S(1)}, u32[]{:S(2)}, u32[]{:S(2)}) collective-permute-start(f32[8,5120]{1,0:T(8,128)S(1)} %get-tuple-element.72), channel_id=1, source_target_pairs={{1,2},{2,1},{3,4},{4,3},{5,6},{6,5},{9,10},{10,9},{11,12},{12,11},... | collective-permute-start | bytes 491528 | tf_op jit(solution)/shard_map/ppermute | solution.py:554
  46.6 5.7 %collective-permute-start.10 = (f32[16,128]{1,0:T(8,128)S(1)}, f32[16,128]{1,0:T(8,128)S(1)}, u32[]{:S(2)}, u32[]{:S(2)}) collective-permute-start(f32[16,128]{1,0:T(8,128)S(1)} %get-tuple-element.73), channel_id=1, source_target_pairs={{0,2},{1,3},{2,0},{3,1},{4,6},{5,7},{6,4},{7,5},{8,10},{9,11},{10,... | collective-permute-start | bytes 24584 | tf_op jit(solution)/shard_map/ppermute | solution.py:554
  49.7 7.6 %collective-permute-start.11 = (f32[16,128]{1,0:T(8,128)S(1)}, f32[16,128]{1,0:T(8,128)S(1)}, u32[]{:S(2)}, u32[]{:S(2)}) collective-permute-start(f32[16,128]{1,0:T(8,128)S(1)} %get-tuple-element.73), channel_id=1, source_target_pairs={{2,4},{3,5},{4,2},{5,3},{10,12},{11,13},{12,10},{13,11},{18,20},{1... | collective-permute-start | bytes 24584 | tf_op jit(solution)/shard_map/ppermute | solution.py:554
